TPU v7x, 32 devices: a whole 2x2x4 slice. The times are simulated.
32 devices in a mesh: rep: 4 (over y, x), cp: 8 (over z, core).
Axes of the slice: x: 2, y: 2, z: 4, core: 2. Of those that a mesh axis runs over, the one named last changes fastest.
Arguments:
- tokens: bfloat16 [4, 2048, 768], P('rep', 'cp'), may hold values from -6 to 6
- query_weight: bfloat16 [768, 768], P('cp'), may hold values from -0.3125 to 0.3125
- query_bias: bfloat16 [768], P('cp'), may hold values from -3 to 3
- key_weight: bfloat16 [768, 768], P('cp'), may hold values from -0.3125 to 0.3125
- value_weight: bfloat16 [768, 768], P('cp'), may hold values from -0.21875 to 0.21875
- value_bias: bfloat16 [768], P('cp'), may hold values from -3 to 3
- output_weight: bfloat16 [768, 768], P('cp'), may hold values from -1.5 to 1.5
- output_bias: bfloat16 [768], P('cp'), may hold values from -1.796875 to 1.796875
- first_gain: bfloat16 [768], P('cp'), may hold values from 0.099609375 to 1.8984375
- first_shift: bfloat16 [768], P('cp'), may hold values from -1.796875 to 1.796875
- up_weight: bfloat16 [768, 3072], P('cp'), may hold values from -0.21875 to 0.21875
- up_bias: bfloat16 [3072], P('cp'), may hold values from -3 to 3
- down_weight: bfloat16 [3072, 768], P('cp'), may hold values from -0.109375 to 0.109375
- down_bias: bfloat16 [768], P('cp'), may hold values from -1.796875 to 1.796875
- second_gain: bfloat16 [768], P('cp'), may hold values from 0.099609375 to 1.8984375
- second_shift: bfloat16 [768], P('cp'), may hold values from -1.796875 to 1.796875
- cotangent: float32 [4, 2048, 768], P('rep', 'cp'), may hold values from -18 to 18
Outputs:
- layer_out: float32 [4, 2048, 768], P('rep', 'cp')
- grad_tokens: float32 [4, 2048, 768], P('rep', 'cp')
- grad_query_weight: float32 [768, 768], P('cp')
- grad_query_bias: float32 [768], P('cp')
- grad_key_weight: float32 [768, 768], P('cp')
- grad_value_weight: float32 [768, 768], P('cp')
- grad_value_bias: float32 [768], P('cp')
- grad_output_weight: float32 [768, 768], P('cp')
- grad_output_bias: float32 [768], P('cp')
- grad_first_gain: float32 [768], P('cp')
- grad_first_shift: float32 [768], P('cp')
- grad_up_weight: float32 [768, 3072], P('cp')
- grad_up_bias: float32 [3072], P('cp')
- grad_down_weight: float32 [3072, 768], P('cp')
- grad_down_bias: float32 [768], P('cp')
- grad_second_gain: float32 [768], P('cp')
- grad_second_shift: float32 [768], P('cp')
- rms_values: float32 [1], replicated
All inputs are finite; a program needn't handle non-finite values.
Results may differ from a plain program's by a relative error of at most 0.025.
Values may be sent and summed in bfloat16 or wider, within the bound.
A program may use at most 192 MiB of HBM per device.

v0:
```python
import functools
import math

import jax
import jax.numpy as jnp
from jax import lax
from jax.experimental import pallas as pl
from jax.experimental.pallas import tpu as pltpu
from jax.sharding import PartitionSpec as P

HD = 64
PAIR = 2 * HD
CHUNKS = 3
EPSILON = 1e-12
BF16 = jnp.bfloat16
F32 = jnp.float32
MESH = pl.DeviceIdType.MESH


def normalize(values, norm_gain, norm_shift):
    center = values - jnp.mean(values, axis=-1, keepdims=True)
    spread = jnp.mean(center * center, axis=-1, keepdims=True)
    return center * lax.rsqrt(spread + EPSILON) * norm_gain + norm_shift


def gelu_exact(values):
    return 0.5 * values * (1.0 + lax.erf(values * (1.0 / math.sqrt(2.0))))


def matmul(left, right):
    return jnp.dot(left, right, preferred_element_type=F32)


def over_rows(left, right):
    return lax.dot_general(left, right, (((0,), (0,)), ((), ())), preferred_element_type=F32)


def against(left, right):
    return lax.dot_general(left, right, (((1,), (1,)), ((), ())), preferred_element_type=F32)


def column_sum(values):
    return jnp.sum(values.astype(F32), axis=0)


def head_mask(shape, head):
    lane = lax.broadcasted_iota(jnp.int32, shape, 1)
    return (lane >= head * HD) & (lane < (head + 1) * HD)


def forward_kernel(query_ref, pair_ref, context_ref):
    keys = pair_ref[:, :PAIR]
    values = pair_ref[:, PAIR:]
    query = query_ref[...]
    total = None
    for head in range(2):
        mask = head_mask(query.shape, head)
        scores = against(jnp.where(mask, query, jnp.zeros_like(query)), keys)
        top = jnp.max(scores, axis=-1, keepdims=True)
        weight = jnp.exp(scores - top)
        inverse = 1.0 / jnp.sum(weight, axis=-1, keepdims=True)
        part = matmul((weight * inverse).astype(BF16), values)
        total = part if head == 0 else jnp.where(mask, part, total)
    context_ref[...] = total.astype(BF16)


def backward_kernel(query_ref, grad_ref, pair_ref, grad_query_ref, grad_pair_ref):
    keys = pair_ref[:, :PAIR]
    values = pair_ref[:, PAIR:]
    query = query_ref[...]
    grad = grad_ref[...]
    zeros = jnp.zeros_like(query)
    key_part = value_part = query_part = None
    for head in range(2):
        mask = head_mask(query.shape, head)
        own_query = jnp.where(mask, query, zeros)
        own_grad = jnp.where(mask, grad, zeros)
        scores = against(keys, own_query)
        top = jnp.max(scores, axis=0, keepdims=True)
        weight = jnp.exp(scores - top)
        inverse = 1.0 / jnp.sum(weight, axis=0, keepdims=True)
        probs = weight * inverse
        grad_probs = against(values, own_grad)
        delta = jnp.sum(probs * grad_probs, axis=0, keepdims=True)
        grad_scores = (probs * (grad_probs - delta)).astype(BF16)
        new_value = matmul(probs.astype(BF16), own_grad)
        new_key = matmul(grad_scores, own_query)
        new_query = over_rows(keys, grad_scores)
        if head == 0:
            key_part, value_part, query_part = new_key, new_value, new_query
        else:
            key_part = key_part + new_key
            value_part = value_part + new_value
            row = lax.broadcasted_iota(jnp.int32, new_query.shape, 0)
            query_part = jnp.where(row < HD, query_part, new_query)
    grad_query_ref[...] = (query_part.T * (1.0 / math.sqrt(HD))).astype(BF16)
    grad_pair_ref[:, :PAIR] = key_part.astype(BF16)
    grad_pair_ref[:, PAIR:] = value_part.astype(BF16)


def column_block(rows, width):
    return pl.BlockSpec((rows, width), lambda i: (0, i))


def attend(query, pairs):
    rows, width = query.shape
    keys = pairs.shape[0]
    return pl.pallas_call(
        forward_kernel,
        grid=(width // PAIR,),
        in_specs=[column_block(rows, PAIR), column_block(keys, 2 * PAIR)],
        out_specs=column_block(rows, PAIR),
        out_shape=jax.ShapeDtypeStruct((rows, width), BF16),
    )(query, pairs)


def attend_back(query, grad, pairs):
    rows, width = query.shape
    keys = pairs.shape[0]
    return pl.pallas_call(
        backward_kernel,
        grid=(width // PAIR,),
        in_specs=[
            column_block(rows, PAIR),
            column_block(rows, PAIR),
            column_block(keys, 2 * PAIR),
        ],
        out_specs=(column_block(rows, PAIR), column_block(keys, 2 * PAIR)),
        out_shape=(
            jax.ShapeDtypeStruct((rows, width), BF16),
            jax.ShapeDtypeStruct((keys, 2 * width), BF16),
        ),
    )(query, grad, pairs)


def mixed(left, right):
    parts = []
    for low in range(0, left.shape[1], PAIR):
        parts += [left[:, low : low + PAIR], right[:, low : low + PAIR]]
    return jnp.concatenate(parts, axis=1)


def unmixed(both):
    starts = range(0, both.shape[1], 2 * PAIR)
    return (
        jnp.concatenate([both[:, low : low + PAIR] for low in starts], axis=1),
        jnp.concatenate([both[:, low + PAIR : low + 2 * PAIR] for low in starts], axis=1),
    )


def gather_all(shard):
    return lax.all_gather(shard, "cp", axis=0, tiled=True)


def scatter_all(values):
    return lax.psum_scatter(values.astype(BF16), "cp", scatter_dimension=0, tiled=True)


def places():
    rep = lax.axis_index("rep")
    cp = lax.axis_index("cp")
    return rep, cp // 4, (cp // 2) % 2, cp % 2


def place_of(high, low, core):
    return 4 * high + 2 * low + core


def enter(reps):
    rep, high, low, core = places()
    barrier = pltpu.get_barrier_semaphore()
    peers = [
        (rep, place_of(high, low, 1 - core)),
        (rep, place_of(high, 1 - low, core)),
        (rep, place_of(1 - high, low, core)),
    ]
    peers += [((rep + k) % reps, place_of(high, low, core)) for k in range(1, reps)]
    for peer in peers:
        pl.semaphore_signal(barrier, inc=1, device_id=peer, device_id_type=MESH)
    pl.semaphore_wait(barrier, len(peers))


def remote(src, dst, sends, recvs, at, peer):
    return pltpu.make_async_remote_copy(
        src_ref=src,
        dst_ref=dst,
        send_sem=sends.at[at],
        recv_sem=recvs.at[at],
        device_id=peer,
        device_id_type=MESH,
    )


def gather_kernel(units, count, reps, *refs):
    ins = refs[:count]
    outs = refs[count : 2 * count]
    sends_z, recvs_z, sends_r, recvs_r, sends_c, recvs_c, local = refs[2 * count :]
    rep, high, low, core = places()
    me = (rep, place_of(high, low, core))
    sibling = (rep, place_of(high, low, 1 - core))
    far = (rep, place_of(1 - high, low, core))
    near = (rep, place_of(high, 1 - low, core))
    enter(reps)
    sent = []
    copies = []

    def send(src, dst, sends, recvs, at, peer):
        copy = remote(src, dst, sends, recvs, at, peer)
        copy.start()
        sent.append(copy)

    def arrived(block, sends, recvs, at):
        remote(block, block, sends, recvs, at, me).wait_recv()

    origins = (
        (high, low),
        (high, 1 - low),
        (1 - high, low),
        (1 - high, 1 - low),
    )

    def block_of(u, which, side, quarter):
        at, start, size = units[u]
        from_high, from_low = origins[which]
        return outs[at].at[from_high, from_low, side, quarter, :, pl.ds(start, size)]

    for u, (at, start, size) in enumerate(units):
        block = ins[at].at[rep, :, pl.ds(start, size)]
        send(block, block_of(u, 0, core, rep), sends_z, recvs_z, 3 * u + 1, far)
        send(block, block_of(u, 0, core, rep), sends_z, recvs_z, 3 * u, near)
    for u, (at, start, size) in enumerate(units):
        whole = ins[at].at[:, :, pl.ds(start, size)]
        send(whole, block_of(u, 0, core, slice(None)), sends_c, recvs_c, 4 * u, sibling)
    for at in range(count):
        copy = pltpu.make_async_copy(ins[at], outs[at].at[high, low, core], local.at[at])
        copy.start()
        copies.append(copy)

    def spread(u, which):
        block = block_of(u, which, core, rep)
        arrived(block, sends_z, recvs_z, 3 * u + which - 1)
        if which == 2:
            send(block, block, sends_z, recvs_z, 3 * u + 2, near)
        for j in range(1, reps):
            index = (3 * u + which - 1) * (reps - 1) + j - 1
            peer = ((rep + j) % reps, me[1])
            send(block, block, sends_r, recvs_r, index, peer)

    def pass_on(u, which):
        for j in range(1, reps):
            index = (3 * u + which - 1) * (reps - 1) + j - 1
            block = block_of(u, which, core, (rep + reps - j) % reps)
            arrived(block, sends_r, recvs_r, index)
        whole = block_of(u, which, core, slice(None))
        send(whole, whole, sends_c, recvs_c, 4 * u + which, sibling)

    total = len(units)
    for step in range(total + 2):
        if step < total:
            spread(step, 1)
            spread(step, 2)
        if 1 <= step < total + 1:
            spread(step - 1, 3)
        if 2 <= step:
            for which in range(1, 4):
                pass_on(step - 2, which)
    for u in range(total):
        for which in range(4):
            block = block_of(u, which, 1 - core, slice(None))
            arrived(block, sends_c, recvs_c, 4 * u + which)
    for copy in sent:
        copy.wait_send()
    for copy in copies:
        copy.wait()


def cut(width, pieces):
    size = width // pieces
    if size % 128:
        return [(0, width)]
    return [(size * i, size) for i in range(pieces)]


def gather_many(shards, pieces, identity):
    reps = lax.axis_size("rep")
    count = len(shards)
    units = [
        (at, low, size)
        for at, shard in enumerate(shards)
        for low, size in cut(shard.shape[2], pieces[at])
    ]
    total = len(units)
    hops = 3 * total * (reps - 1)
    dma = pltpu.SemaphoreType.DMA
    return pl.pallas_call(
        functools.partial(gather_kernel, units, count, reps),
        out_shape=[
            jax.ShapeDtypeStruct((2, 2, 2) + shard.shape, shard.dtype) for shard in shards
        ],
        in_specs=[pl.BlockSpec(memory_space=pl.ANY)] * count,
        out_specs=[pl.BlockSpec(memory_space=pl.ANY)] * count,
        scratch_shapes=[dma((3 * total,))] * 2
        + [dma((hops,))] * 2
        + [dma((4 * total,))] * 2
        + [dma((count,))],
        compiler_params=pltpu.CompilerParams(collective_id=identity, has_side_effects=True),
    )(*shards)


def summed(parts, kind):
    total = parts[0].astype(F32)
    for part in parts[1:]:
        total = total + part.astype(F32)
    return total.astype(kind)


def reduce_kernel(units, count, reps, *refs):
    ins = refs[:count]
    outs = refs[count : 2 * count]
    at = 2 * count
    size = len(units)
    first, second, third, fourth, own = [
        refs[at + i * size : at + (i + 1) * size] for i in range(5)
    ]
    sems = refs[at + 5 * size :]
    sends_c, recvs_c, sends_r, recvs_r, sends_z, recvs_z, sends_g, recvs_g = sems
    rep, high, low, core = places()
    me = (rep, place_of(high, low, core))
    sibling = (rep, place_of(high, low, 1 - core))
    far = (rep, place_of(1 - high, low, core))
    near = (rep, place_of(high, 1 - low, core))
    enter(reps)
    sent = []

    def send(src, dst, sends, recvs, at, peer):
        copy = remote(src, dst, sends, recvs, at, peer)
        copy.start()
        sent.append(copy)

    def arrived(block, sends, recvs, at):
        remote(block, block, sends, recvs, at, me).wait_recv()

    for u, (a, start, width) in enumerate(units):
        block = ins[a].at[:, :, 1 - core, :, :, pl.ds(start, width)]
        send(block, first[u], sends_c, recvs_c, u, sibling)

    def over_core(u):
        a, start, width = units[u]
        arrived(first[u], sends_c, recvs_c, u)

        def step(i, carry):
            h, w, q = i // (2 * reps), (i // reps) % 2, i % reps
            mine = ins[a][h, w, core, q, :, start : start + width]
            first[u][h, w, q] = summed([first[u][h, w, q], mine], first[u].dtype)
            return carry

        lax.fori_loop(0, 4 * reps, step, 0)
        for k in range(1, reps):
            target = (rep + k) % reps
            send(
                first[u].at[:, :, target],
                second[u].at[k - 1],
                sends_r,
                recvs_r,
                u * (reps - 1) + k - 1,
                (target, me[1]),
            )

    def over_rep(u):
        for k in range(1, reps):
            arrived(second[u].at[k - 1], sends_r, recvs_r, u * (reps - 1) + k - 1)

        def step(i, carry):
            h, w = i // 2, i % 2
            parts = [first[u][h, w, rep]] + [second[u][k, h, w] for k in range(reps - 1)]
            own[u][h, w] = summed(parts, own[u].dtype)
            return carry

        lax.fori_loop(0, 4, step, 0)
        send(own[u].at[:, 1 - low], third[u], sends_z, recvs_z, 2 * u, near)

    def over_near(u):
        arrived(third[u], sends_z, recvs_z, 2 * u)
        for h in range(2):
            own[u][h, low] = summed([own[u][h, low], third[u][h]], own[u].dtype)
        send(own[u].at[1 - high, low], fourth[u], sends_z, recvs_z, 2 * u + 1, far)

    def over_far(u):
        a, start, width = units[u]
        arrived(fourth[u], sends_z, recvs_z, 2 * u + 1)
        outs[a][rep, :, start : start + width] = summed(
            [own[u][high, low], fourth[u][...]], outs[a].dtype
        )
        block = outs[a].at[rep, :, pl.ds(start, width)]
        for k in range(1, reps):
            peer = ((rep + k) % reps, me[1])
            send(block, block, sends_g, recvs_g, u * (reps - 1) + k - 1, peer)

    stages = (over_core, over_rep, over_near, over_far)
    for step in range(size + len(stages) - 1):
        for lag, stage in enumerate(stages):
            if 0 <= step - lag < size:
                stage(step - lag)
    for u, (a, start, width) in enumerate(units):
        for k in range(1, reps):
            block = outs[a].at[(rep + reps - k) % reps, :, pl.ds(start, width)]
            arrived(block, sends_g, recvs_g, u * (reps - 1) + k - 1)
    for copy in sent:
        copy.wait_send()


def split_rows(part):
    reps = lax.axis_size("rep")
    rows, width = part.shape
    return part.reshape(2, 2, 2, reps, rows // (8 * reps), width)


def reduce_many(blocks, pieces, identity):
    reps = lax.axis_size("rep")
    count = len(blocks)
    units = [
        (at, low, size)
        for at, block in enumerate(blocks)
        for low, size in cut(block.shape[5], pieces[at])
    ]
    dma = pltpu.SemaphoreType.DMA
    vmem = pl.BlockSpec(memory_space=pltpu.VMEM)

    def buffers(*lead):
        return [
            pltpu.VMEM(lead + (blocks[at].shape[4], size), blocks[at].dtype)
            for at, _, size in units
        ]

    total = len(units)
    sums = pl.pallas_call(
        functools.partial(reduce_kernel, units, count, reps),
        out_shape=[
            jax.ShapeDtypeStruct((reps,) + block.shape[4:], block.dtype) for block in blocks
        ],
        in_specs=[vmem] * count,
        out_specs=[vmem] * count,
        scratch_shapes=buffers(2, 2, reps)
        + buffers(reps - 1, 2, 2)
        + buffers(2)
        + buffers()
        + buffers(2, 2)
        + [dma((total,))] * 2
        + [dma((total * (reps - 1),))] * 2
        + [dma((total * 2,))] * 2
        + [dma((total * (reps - 1),))] * 2,
        compiler_params=pltpu.CompilerParams(
            collective_id=identity, has_side_effects=True, vmem_limit_bytes=56 * 1024 * 1024
        ),
    )(*blocks)
    return [total.reshape(-1, total.shape[2]).astype(F32) for total in sums]


def blocked(shard):
    return shard.reshape(lax.axis_size("rep"), -1, shard.shape[1])


def divides(rows):
    reps = lax.axis_size("rep")
    return lax.axis_size("cp") == 8 and reps == 4 and rows % (8 * reps) == 0


def on_device(
    tokens,
    query_weight,
    query_bias,
    key_weight,
    value_weight,
    value_bias,
    output_weight,
    output_bias,
    first_gain,
    first_shift,
    up_weight,
    up_bias,
    down_weight,
    down_bias,
    second_gain,
    second_shift,
    cotangent,
):
    row_count = tokens.shape[1]
    width = tokens.shape[2]
    local_tokens = tokens[0]
    fast = divides(query_weight.shape[0])
    reps = lax.axis_size("rep")
    proj_shard = jnp.concatenate([query_weight, mixed(key_weight, value_weight)], axis=1)
    small = (
        query_bias,
        value_bias,
        output_bias,
        first_gain,
        first_shift,
        up_bias,
        down_bias,
        second_gain,
        second_shift,
    )
    if fast:
        rows = []
        for vector in small:
            lines = -(-vector.shape[0] // 128)
            rows.append(
                jnp.pad(vector.astype(F32), (0, 128 * lines - vector.shape[0])).reshape(lines, 128)
            )
        packed = jnp.concatenate(rows, axis=0)
        packed = jnp.pad(packed, ((0, -packed.shape[0] % (8 * reps)), (0, 0))).astype(BF16)
        w_proj, gathered = gather_many(
            (blocked(proj_shard), blocked(packed)), (3, 1), 1
        )
        w_proj = w_proj.reshape(-1, proj_shard.shape[1])
        gathered = gathered.reshape(-1, packed.shape[0], 128)
    else:
        w_proj = gather_all(proj_shard)
        gathered = lax.all_gather(jnp.concatenate(small)[None], "cp", axis=0, tiled=True)
    vectors = []
    at = 0
    for vector in small:
        size = vector.shape[0]
        if fast:
            lines = -(-size // 128)
            part = gathered[:, at : at + lines].reshape(-1, 128 * lines)[:, :size]
            at += lines
        else:
            part = gathered[:, at : at + size]
            at += size
        vectors.append(part.reshape(-1).astype(F32))
    b_query, b_value, b_output, gain_one, shift_one, b_up, b_down, gain_two, shift_two = vectors
    w_pair = w_proj[:, width:]
    pair_bias = mixed(jnp.zeros_like(b_value)[None], b_value[None])
    pair_rows = (matmul(local_tokens, w_pair) + pair_bias).astype(BF16)
    chunk = width // CHUNKS
    pairs = [
        lax.all_gather(
            pair_rows[:, 2 * chunk * i : 2 * chunk * (i + 1)], "cp", axis=0, tiled=True
        )
        for i in range(CHUNKS)
    ]
    query_rows = (matmul(local_tokens, w_proj[:, :width]) + b_query).astype(BF16)
    query_scaled = query_rows * jnp.asarray(1.0 / math.sqrt(HD), BF16)
    queries = [query_scaled[:, chunk * i : chunk * (i + 1)] for i in range(CHUNKS)]
    wide_shard = jnp.concatenate([output_weight, up_weight], axis=1)
    if fast:
        wide_shard, down_shard, _ = lax.optimization_barrier(
            (wide_shard, down_weight, pair_rows)
        )
        w_wide, w_down = gather_many((blocked(wide_shard), blocked(down_shard)), (2, 2), 2)
        w_wide = w_wide.reshape(-1, wide_shard.shape[1])
        w_down = w_down.reshape(-1, width)
        w_wide, queries = lax.optimization_barrier((w_wide, queries))
    else:
        w_wide = gather_all(wide_shard)
        w_down = gather_all(down_weight)
    w_output = w_wide[:, :width]
    w_up = w_wide[:, width:]

    context_low = jnp.concatenate(
        [attend(query, pair) for query, pair in zip(queries, pairs)], axis=1
    )
    attn_out = matmul(context_low, w_output) + b_output
    resid_first = local_tokens.astype(F32) + attn_out
    first_norm, pull_first = jax.vjp(normalize, resid_first, gain_one, shift_one)
    first_low = first_norm.astype(BF16)
    inner_act = matmul(first_low, w_up) + b_up
    hidden, pull_gelu = jax.vjp(gelu_exact, inner_act)
    hidden_low = hidden.astype(BF16)
    resid_second = first_norm + (matmul(hidden_low, w_down) + b_down)
    layer_out, pull_second = jax.vjp(normalize, resid_second, gain_two, shift_two)

    grad_resid2, grad_gain2, grad_shift2 = pull_second(cotangent[0])
    grad_outer = grad_resid2.astype(BF16)
    grad_down_bias = column_sum(grad_outer)
    part_down = over_rows(hidden_low, grad_outer).astype(BF16)
    grad_inner = pull_gelu(against(grad_outer, w_down))[0].astype(BF16)
    grad_up_bias = column_sum(grad_inner)
    part_up = over_rows(first_low, grad_inner).astype(BF16)
    grad_first = grad_resid2 + against(grad_inner, w_up)
    grad_resid1, grad_gain1, grad_shift1 = pull_first(grad_first)
    grad_attn = grad_resid1.astype(BF16)
    grad_output_bias = column_sum(grad_attn)
    part_output = over_rows(context_low, grad_attn).astype(BF16)
    grad_context = against(grad_attn, w_output).astype(BF16)

    grad_queries = []
    grad_pairs = []
    terms = []
    for i in range(CHUNKS):
        grad_query, grad_terms = attend_back(
            queries[i], grad_context[:, chunk * i : chunk * (i + 1)], pairs[i]
        )
        grad_queries.append(grad_query)
        terms.append(grad_terms)
        grad_pairs.append(
            lax.psum_scatter(grad_terms, "cp", scatter_dimension=0, tiled=True)
        )
    grad_query_low = jnp.concatenate(grad_queries, axis=1)
    part_query = over_rows(local_tokens, grad_query_low).astype(BF16)
    if fast:
        parts = (part_down, part_up, part_output, part_query)
        parts, _ = lax.optimization_barrier((parts, terms))
        full_down, full_up, full_output, full_query = reduce_many(
            [split_rows(part) for part in parts], (2, 2, 1, 1), 3
        )
    grad_pair_low = jnp.concatenate(grad_pairs, axis=1)
    grad_proj = jnp.concatenate([grad_query_low, grad_pair_low], axis=1)
    part_pair = over_rows(local_tokens, grad_pair_low).astype(BF16)
    grad_tokens = grad_resid1 + against(grad_proj, w_proj)
    proj_sums = column_sum(grad_proj)
    _, grad_value_bias = unmixed(proj_sums[None, width:])

    small_grads = (
        proj_sums[:width],
        grad_value_bias[0],
        grad_output_bias,
        grad_gain1,
        grad_shift1,
        grad_up_bias,
        grad_down_bias,
        grad_gain2,
        grad_shift2,
    )
    owners = lax.axis_size("cp")
    total_sq = jnp.broadcast_to(jnp.sum(grad_tokens * grad_tokens), (owners, 1))
    flat = jnp.concatenate(
        [vector.reshape(owners, -1) for vector in small_grads] + [total_sq], axis=1
    )
    if fast:
        flat = jnp.pad(flat, ((0, 0), (0, -flat.shape[1] % (8 * 128 * reps))))
        full_pair, sums = reduce_many(
            (split_rows(part_pair), flat.reshape(2, 2, 2, reps, -1, 128)), (3, 1), 4
        )
        sums = sums.reshape(-1)
    else:
        shards = [
            scatter_all(part)
            for part in (part_down, part_up, part_output, part_query, part_pair)
        ]
        full_down, full_up, full_output, full_query, full_pair = [
            part.astype(F32) for part in lax.psum(tuple(shards), "rep")
        ]
        sums = lax.psum(flat, ("rep", "cp"))
        sums = lax.dynamic_slice_in_dim(sums, lax.axis_index("cp"), 1, 0)[0]
    reduced = []
    at = 0
    for shard in small:
        reduced.append(sums[at : at + shard.shape[0]])
        at += shard.shape[0]
    entries = lax.axis_size("rep") * owners * row_count * width
    rms_values = jnp.sqrt(sums[at : at + 1] / entries)

    grad_key_weight, grad_value_weight = unmixed(full_pair)
    return (
        layer_out[None],
        grad_tokens[None],
        full_query,
        reduced[0],
        grad_key_weight,
        grad_value_weight,
        reduced[1],
        full_output,
        reduced[2],
        reduced[3],
        reduced[4],
        full_up,
        reduced[5],
        full_down,
        reduced[6],
        reduced[7],
        reduced[8],
        rms_values,
    )


def solution(mesh):
    rows = P("cp", None)
    vector = P("cp")
    whole = P("rep", "cp", None)
    params = (
        rows,
        vector,
        rows,
        rows,
        vector,
        rows,
        vector,
        vector,
        vector,
        rows,
        vector,
        rows,
        vector,
        vector,
        vector,
    )
    return jax.shard_map(
        on_device,
        mesh=mesh,
        in_specs=(whole,) + params + (whole,),
        out_specs=(whole, whole) + params + (P(),),
        check_vma=False,
    )
```

profile of v0, /device:TPU:0, one launch (start us, length us, event | category | flops | bytes accessed | tf_op | source)
XLA Modules:
  0.0 396.3 jit_solution(18105411836386386444)
XLA Ops:
  7.2 0.9 constant_dynamic-update-slice_fusion.12
  8.2 0.8 constant_dynamic-update-slice_fusion.11
  8.9 0.7 constant_dynamic-update-slice_fusion.10
  9.7 0.7 constant_dynamic-update-slice_fusion.9
  10.4 0.7 constant_dynamic-update-slice_fusion.8
  11.2 0.7 constant_dynamic-update-slice_fusion.7
  11.9 0.7 constant_dynamic-update-slice_fusion.6
  12.7 0.7 constant_dynamic-update-slice_fusion.5
  13.4 0.7 constant_dynamic-update-slice_fusion.4
  14.2 0.7 constant_dynamic-update-slice_fusion.3
  14.9 0.7 constant_dynamic-update-slice_fusion.2
  15.7 0.7 constant_dynamic-update-slice_fusion.1
  16.4 0.7 constant_dynamic-update-slice_fusion
  17.1 0.7 pad_bitcast_fusion.8
  19.9 0.7 concatenate.40
  21.2 30.4 %shard_map.304 = (bf16[2,2,2,4,24,2304]{5,4,3,2,1,0:T(8,128)(2,1)}, bf16[2,2,2,4,8,128]{5,4,3,2,1,0:T(8,128)(2,1)}) custom-call(bf16[4,24,2304]{2,1,0:T(8,128)(2,1)} %bitcast.124, bf16[4,8,128]{2,1,0:T(8,128)(2,1)} %pad_bitcast_fusion.1.refs_1_), custom_call_target="tpu_custom_call" | custom-call | tf_op jit(solution)/shard_map/pallas_call | solution.py:295
  51.7 1.0 fusion.51
  53.0 2.6 fusion.8
  55.6 0.9 fusion.48
  56.6 0.7 all-gather.6.cloned.1.call-update
  58.1 0.7 slice_convert_fusion
  58.9 0.9 pad_maximum_fusion
  59.9 66.5 %shard_map.305 = (bf16[2,2,2,4,24,3840]{5,4,3,2,1,0:T(8,128)(2,1)}, bf16[2,2,2,4,96,768]{5,4,3,2,1,0:T(8,128)(2,1)}) custom-call(bf16[4,24,3840]{2,1,0:T(8,128)(2,1)} %bitcast.121, bf16[4,96,768]{2,1,0:T(8,128)(2,1)} %bitcast.125), custom_call_target="tpu_custom_call" | custom-call | tf_op jit(solution)/shard_map/pallas_call | solution.py:295
  126.4 1.8 fusion.18
  128.1 0.7 fusion.50
  129.3 6.9 %shard_map.308 = bf16[256,256]{1,0:T(8,128)(2,1)} custom-call(bf16[256,256]{1,0:T(8,128)(2,1)} %get-tuple-element.51.query_ref, bf16[2048,512]{1,0:T(8,128)(2,1)} %all-gather.8.cloned.1.call-done.pair_ref), custom_call_target="tpu_custom_call" | custom-call | tf_op jit(solution)/shard_map/pallas_call | solution.py:108
  136.2 6.5 %shard_map.307 = bf16[256,256]{1,0:T(8,128)(2,1)} custom-call(bf16[256,256]{1,0:T(8,128)(2,1)} %get-tuple-element.50.query_ref, bf16[2048,512]{1,0:T(8,128)(2,1)} %all-gather.6.cloned.1.call-done.pair_ref), custom_call_target="tpu_custom_call" | custom-call | tf_op jit(solution)/shard_map/pallas_call | solution.py:108
  142.7 17.2 %all-gather.4.cloned.1.call-done.pair_ref = bf16[2048,512]{1,0:T(8,128)(2,1)} async-done(((bf16[256,512]{1,0:T(8,128)(2,1)}), bf16[2048,512]{1,0:T(8,128)(2,1)}) %all-gather.4.cloned.1.call-update) | async-done | bytes 2097168 | tf_op jit(solution)/shard_map/all_gather | solution.py:539
  159.8 6.4 %shard_map.306 = bf16[256,256]{1,0:T(8,128)(2,1)} custom-call(bf16[256,256]{1,0:T(8,128)(2,1)} %get-tuple-element.49.query_ref, bf16[2048,512]{1,0:T(8,128)(2,1)} %all-gather.4.cloned.1.call-done.pair_ref), custom_call_target="tpu_custom_call" | custom-call | tf_op jit(solution)/shard_map/pallas_call | solution.py:108
  166.2 1.9 fusion.53
  168.4 3.7 multiply_convert_fusion
  172.2 1.5 fusion.54
  174.3 1.2 fusion.47
  175.6 0.7 convert_reduce_fusion.2
  176.3 3.3 convert_reduce_fusion
  179.6 2.2 multiply_reduce_fusion.1
  182.2 0.8 copy-done.1
  183.1 0.7 convert_reduce_fusion.3
  184.3 0.8 fusion.49
  185.1 11.1 %shard_map.309 = (bf16[256,256]{1,0:T(8,128)(2,1)}, bf16[2048,512]{1,0:T(8,128)(2,1)}) custom-call(bf16[256,256]{1,0:T(8,128)(2,1)} %get-tuple-element.49.query_ref, bf16[256,256]{1,0:T(8,128)(2,1)} %get-tuple-element.103.grad_ref, bf16[2048,512]{1,0:T(8,128)(2,1)} %all-gather.4.cloned.1.call-done.pair_ref), custom_call_target="tpu_custom_call" | custom-call | tf_op jit(solution)/shard_map/pallas_call | solution.py:120
  196.2 11.1 %shard_map.310 = (bf16[256,256]{1,0:T(8,128)(2,1)}, bf16[2048,512]{1,0:T(8,128)(2,1)}) custom-call(bf16[256,256]{1,0:T(8,128)(2,1)} %get-tuple-element.50.query_ref, bf16[256,256]{1,0:T(8,128)(2,1)} %get-tuple-element.102.grad_ref, bf16[2048,512]{1,0:T(8,128)(2,1)} %all-gather.6.cloned.1.call-done.pair_ref), custom_call_target="tpu_custom_call" | custom-call | tf_op jit(solution)/shard_map/pallas_call | solution.py:120
  207.4 11.3 %shard_map.311 = (bf16[256,256]{1,0:T(8,128)(2,1)}, bf16[2048,512]{1,0:T(8,128)(2,1)}) custom-call(bf16[256,256]{1,0:T(8,128)(2,1)} %get-tuple-element.51.query_ref, bf16[256,256]{1,0:T(8,128)(2,1)} %get-tuple-element.101.grad_ref, bf16[2048,512]{1,0:T(8,128)(2,1)} %all-gather.8.cloned.1.call-done.pair_ref), custom_call_target="tpu_custom_call" | custom-call | tf_op jit(solution)/shard_map/pallas_call | solution.py:120
  219.4 0.8 reshape.362
  220.2 2.7 convolution_convert_fusion.4
  222.9 2.7 fusion.10
  225.7 3.6 convolution_convert_fusion.1
  229.3 3.8 convolution_convert_fusion
  233.1 1.5 copy.48
  234.9 95.9 %shard_map.312 = (bf16[4,96,768]{2,1,0:T(8,128)(2,1)}, bf16[4,24,3072]{2,1,0:T(8,128)(2,1)}, bf16[4,24,768]{2,1,0:T(8,128)(2,1)}, bf16[4,24,768]{2,1,0:T(8,128)(2,1)}) custom-call(bf16[2,2,2,4,96,768]{5,4,3,2,1,0:T(8,128)(2,1)} %bitcast.118, bf16[2,2,2,4,24,3072]{5,4,3,2,1,0:T(8,128)(2,1)} %bitcast.119, bf16[2,2,2,4,24,768]{5,4,3,2,1,0:T(8,128)(2,1)} %bitcast.123, ...), custom_call_target="tpu_custom_call" | custom-call | tf_op jit(solution)/shard_map/pallas_call | solution.py:436
  330.9 1.7 bitcast_convert_fusion.4
  332.6 1.6 bitcast_convert_fusion.3
  334.2 2.2 bitcast_convert_fusion
  336.5 1.2 bitcast_convert_fusion.1
  337.6 1.0 constant_dynamic-update-slice_fusion.27
  338.6 1.0 constant_dynamic-update-slice_fusion.26
  339.6 1.0 constant_dynamic-update-slice_fusion.25
  340.7 4.7 %multiply_reduce_fusion = (f32[]{:T(128)}, f32[256,768]{1,0:T(8,128)}) fusion(bf16[256,2304]{1,0:T(8,128)(2,1)S(1)} %constant_dynamic-update-slice_fusion.25, bf16[768,2304]{1,0:T(8,128)(2,1)} %bitcast.153, f32[256,768]{1,0:T(8,128)S(1)} %copy-done.2, f32[256]{0:T(256)S(1)} %copy-done.29), kind=kOutput, calls=%fused_computation.44 | convolution fusion | flops 906756096 | bytes 6292484 | tf_op jit(solution)/shard_map/dot_general | solution.py:39
  347.3 2.3 convolution_convert_fusion.2
  349.5 31.9 %shard_map.313 = (bf16[4,24,1536]{2,1,0:T(8,128)(2,1)}, f32[4,8,128]{2,1,0:T(8,128)}) custom-call(bf16[2,2,2,4,24,1536]{5,4,3,2,1,0:T(8,128)(2,1)} %bitcast.122, f32[2,2,2,4,8,128]{5,4,3,2,1,0:T(8,128)} %bitcast.126), custom_call_target="tpu_custom_call" | custom-call | tf_op jit(solution)/shard_map/pallas_call | solution.py:436
  381.4 1.5 fusion.52
  383.0 1.3 slice.371
  384.3 1.2 slice.375
  385.5 1.0 bitcast_convert_fusion.2
  387.3 0.7 copy-done.24
  (176 shorter events, 9.3 us)
Async XLA Ops:
  7.2 122.1 %all-gather.8.cloned.1.call-start = ((), (), s32[]{:S(2)}) async-start(), calls=%async_computation.5 | async-start | bytes 2359296 | tf_op jit(solution)/shard_map/all_gather | solution.py:539
  17.1 4.1 %copy-start.6 = (bf16[96,2304]{1,0:T(8,128)(2,1)}, bf16[96,2304]{1,0:T(8,128)(2,1)S(1)}, u32[]{:S(2)}) copy-start(bf16[96,2304]{1,0:T(8,128)(2,1)S(1)} %constant_dynamic-update-slice_fusion) | copy-start | bytes 1327108
  55.6 3.3 copy-start.8
  55.6 3.3 copy-start.13
  55.6 70.8 %copy-start.30 = (bf16[1,256,768]{2,1,0:T(8,128)(2,1)S(1)}, bf16[1,256,768]{2,1,0:T(8,128)(2,1)}, u32[]{:S(2)}) copy-start(bf16[1,256,768]{2,1,0:T(8,128)(2,1)} %param.17) | copy-start | bytes 1179652
  56.5 79.7 %all-gather.6.cloned.1.call-start = ((), (), s32[]{:S(2)}) async-start(), calls=%async_computation.4 | async-start | bytes 2359296 | tf_op jit(solution)/shard_map/all_gather | solution.py:539
  57.3 102.6 %all-gather.4.cloned.1.call-start = ((), (), s32[]{:S(2)}) async-start(), calls=%async_computation.3 | async-start | bytes 2359296 | tf_op jit(solution)/shard_map/all_gather | solution.py:539
  58.0 279.6 %reduce-scatter.4.cloned.1.call-start = ((), (), s32[]{:S(2)}) async-start(), calls=%async_computation.6 | async-start | bytes 2359296 | tf_op jit(solution)/shard_map/reduce_scatter | solution.py:599
  136.2 30.0 %copy-start.14 = (bf16[256,256]{1,0:T(8,128)(2,1)S(1)}, bf16[256,256]{1,0:T(8,128)(2,1)}, u32[]{:S(2)}) copy-start(bf16[256,256]{1,0:T(8,128)(2,1)} %shard_map.308) | copy-start | bytes 393220
  142.7 23.5 %copy-start.15 = (bf16[256,256]{1,0:T(8,128)(2,1)S(1)}, bf16[256,256]{1,0:T(8,128)(2,1)}, u32[]{:S(2)}) copy-start(bf16[256,256]{1,0:T(8,128)(2,1)} %shard_map.307) | copy-start | bytes 393220
  168.1 4.0 %slice-start.2 = ((s8[4718592]{0:T(1024)(128)(4,1)}), s8[4194304]{0:T(1024)(128)(4,1)S(1)}, s32[]{:S(2)}) async-start(s8[4718592]{0:T(1024)(128)(4,1)} %bitcast.147), calls=%async_computation.11 | async-start | bytes 8388608
  168.4 13.5 %copy-start.21 = (f32[256]{0:T(256)}, f32[256]{0:T(256)S(1)}, u32[]{:S(2)}) copy-start(f32[256]{0:T(256)S(1)} %fusion.38) | copy-start | bytes 3076
  168.4 3.8 slice-start.3
  172.2 1.8 copy-start
  175.6 4.1 %slice-start = ((s8[5898240]{0:T(1024)(128)(4,1)}), s8[4194304]{0:T(1024)(128)(4,1)S(1)}, s32[]{:S(2)}) async-start(s8[5898240]{0:T(1024)(128)(4,1)} %bitcast.143), calls=%async_computation.9 | async-start | bytes 8388608
  176.3 3.4 slice-start.1
  179.6 2.2 copy-start.3
  182.2 0.9 copy-start.1
  182.2 1.6 copy-start.28
  183.8 1.3 copy-start.9
  196.2 142.4 %reduce-scatter.6.cloned.1.call-start = ((), (), s32[]{:S(2)}) async-start(), calls=%async_computation.7 | async-start | bytes 2359296 | tf_op jit(solution)/shard_map/reduce_scatter | solution.py:599
  207.4 132.3 %reduce-scatter.8.cloned.1.call-start = ((), (), s32[]{:S(2)}) async-start(), calls=%async_computation.8 | async-start | bytes 2359296 | tf_op jit(solution)/shard_map/reduce_scatter | solution.py:599
  225.7 3.6 copy-start.4
  225.7 3.6 copy-start.22
  229.3 3.8 copy-start.5
  233.0 1.5 copy-start.20
  233.0 1.6 copy-start.27
  233.0 1.6 copy-start.26
  233.0 1.7 copy-start.23
  233.1 1.7 copy-start.19
  234.9 95.9 %copy-start.16 = (bf16[256,256]{1,0:T(8,128)(2,1)S(1)}, bf16[256,256]{1,0:T(8,128)(2,1)}, u32[]{:S(2)}) copy-start(bf16[256,256]{1,0:T(8,128)(2,1)} %get-tuple-element.54) | copy-start | bytes 393220
  234.9 95.9 %copy-start.17 = (bf16[256,256]{1,0:T(8,128)(2,1)S(1)}, bf16[256,256]{1,0:T(8,128)(2,1)}, u32[]{:S(2)}) copy-start(bf16[256,256]{1,0:T(8,128)(2,1)} %get-tuple-element.55) | copy-start | bytes 393220
  234.9 96.0 %copy-start.18 = (bf16[256,256]{1,0:T(8,128)(2,1)S(1)}, bf16[256,256]{1,0:T(8,128)(2,1)}, u32[]{:S(2)}) copy-start(bf16[256,256]{1,0:T(8,128)(2,1)} %get-tuple-element.56) | copy-start | bytes 393220
  330.8 5.7 %copy-start.7 = (bf16[4,24,3072]{2,1,0:T(8,128)(2,1)S(1)}, bf16[4,24,3072]{2,1,0:T(8,128)(2,1)}, u32[]{:S(2)}) copy-start(bf16[4,24,3072]{2,1,0:T(8,128)(2,1)} %get-tuple-element.68) | copy-start | bytes 1769476
  334.2 6.4 %copy-start.2 = (f32[256,768]{1,0:T(8,128)S(1)}, f32[256,768]{1,0:T(8,128)}, u32[]{:S(2)}) copy-start(f32[256,768]{1,0:T(8,128)} %copy-done.1) | copy-start | bytes 2359300
  334.2 6.4 %copy-start.29 = (f32[256]{0:T(256)S(1)}, f32[256]{0:T(256)}, u32[]{:S(2)}) copy-start(f32[256]{0:T(256)} %copy-done.28) | copy-start | bytes 3076
  340.6 6.6 %copy-start.10 = (bf16[256,512]{1,0:T(8,128)(2,1)S(1)}, bf16[256,512]{1,0:T(8,128)(2,1)}, u32[]{:S(2)}) copy-start(bf16[256,512]{1,0:T(8,128)(2,1)} %reduce-scatter.4.cloned.1.call-done) | copy-start | bytes 786436
  340.6 6.6 %copy-start.11 = (bf16[256,512]{1,0:T(8,128)(2,1)S(1)}, bf16[256,512]{1,0:T(8,128)(2,1)}, u32[]{:S(2)}) copy-start(bf16[256,512]{1,0:T(8,128)(2,1)} %reduce-scatter.6.cloned.1.call-done) | copy-start | bytes 786436
  340.6 6.6 %copy-start.12 = (bf16[256,512]{1,0:T(8,128)(2,1)S(1)}, bf16[256,512]{1,0:T(8,128)(2,1)}, u32[]{:S(2)}) copy-start(bf16[256,512]{1,0:T(8,128)(2,1)} %reduce-scatter.8.cloned.1.call-done) | copy-start | bytes 786436
  340.7 6.6 %copy-start.31 = (bf16[1,256,768]{2,1,0:T(8,128)(2,1)S(1)}, bf16[1,256,768]{2,1,0:T(8,128)(2,1)}, u32[]{:S(2)}) copy-start(bf16[1,256,768]{2,1,0:T(8,128)(2,1)} %param.17) | copy-start | bytes 1179652
  387.3 0.7 copy-start.24
  387.3 0.8 copy-start.25
Sparse Core Ops, SparseCore 0:
  56.6 41.4 all-gather.7
  100.3 28.7 all-gather.5
  131.3 28.5 all-gather.3
  196.3 35.2 reduce-scatter.3
  233.8 36.1 reduce-scatter.5
  272.1 41.8 reduce-scatter.7
where the time goes:
time: 402 us; the launch traced here: 396 us
  Pallas kernels  278 us (69%)
  matrix products  37.3 us (9%)
  local copies, waits for them, and re-layouts  31.2 us (8%)
  waiting for transfers between devices  18.6 us (5%)
  between operations  16.9 us (4%)
  other arithmetic  14.2 us (4%)
    pallas_call x2, Pallas kernels, reduce_many(): pl.pallas_call(functools.partial(reduce_kernel, units, count, reps), out_...  128 us
    pallas_call x2, Pallas kernels, gather_many(): pl.pallas_call(functools.partial(gather_kernel, units, count, reps), out_...  96.9 us
    pallas_call x3, Pallas kernels, attend_back(): pl.pallas_call(backward_kernel, grid=(width // PAIR,), in_specs=[column_b...  33.5 us
    pallas_call x3, Pallas kernels, attend(): pl.pallas_call(forward_kernel, grid=(width // PAIR,), in_specs=[column_bl...  19.7 us
    all_gather x3, waiting for transfers between devices, on_device(): lax.all_gather(pair_rows[:, 2 * chunk * i:2 * chunk * (i + 1)], 'cp', axi...  17.2 us
    dot_general x5, matrix products, over_rows(): lax.dot_general(left, right, (((0,), (0,)), ((), ())), preferred_element_...  15.1 us
    unnamed x120, local copies, waits for them, and re-layouts  13.8 us
    dot_general x5, matrix products, matmul(): return jnp.dot(left, right, preferred_element_type=F32)  11.5 us
  transfers between devices with their start and end apart: 6, of which 1 were waited for; matrix products, arithmetic and copies ran while one was open for 7% of the time, Pallas kernels for 50%

commit v1 on v0

--- a/solution.py
+++ b/solution.py
@@ -64,11 +64,7 @@
     context_ref[...] = total.astype(BF16)
 
 
-def backward_kernel(query_ref, grad_ref, pair_ref, grad_query_ref, grad_pair_ref):
-    keys = pair_ref[:, :PAIR]
-    values = pair_ref[:, PAIR:]
-    query = query_ref[...]
-    grad = grad_ref[...]
+def pair_grads(query, grad, keys, values):
     zeros = jnp.zeros_like(query)
     key_part = value_part = query_part = None
     for head in range(2):
@@ -93,9 +89,14 @@
             value_part = value_part + new_value
             row = lax.broadcasted_iota(jnp.int32, new_query.shape, 0)
             query_part = jnp.where(row < HD, query_part, new_query)
-    grad_query_ref[...] = (query_part.T * (1.0 / math.sqrt(HD))).astype(BF16)
-    grad_pair_ref[:, :PAIR] = key_part.astype(BF16)
-    grad_pair_ref[:, PAIR:] = value_part.astype(BF16)
+    query_part = (query_part.T * (1.0 / math.sqrt(HD))).astype(BF16)
+    return query_part, key_part.astype(BF16), value_part.astype(BF16)
+
+
+def backward_kernel(query_ref, grad_ref, pair_ref, grad_query_ref, grad_pair_ref):
+    grad_query_ref[...], grad_pair_ref[:, :PAIR], grad_pair_ref[:, PAIR:] = pair_grads(
+        query_ref[...], grad_ref[...], pair_ref[:, :PAIR], pair_ref[:, PAIR:]
+    )
 
 
 def column_block(rows, width):
@@ -314,28 +315,35 @@
     return total.astype(kind)
 
 
-def reduce_kernel(units, count, reps, *refs):
+def reduce_kernel(units, count, reps, chunks, *refs):
     ins = refs[:count]
-    outs = refs[count : 2 * count]
-    at = 2 * count
+    at = count
+    if chunks:
+        query_ref, grad_ref = refs[at : at + 2]
+        pair_refs = refs[at + 2 : at + 2 + chunks]
+        at += 2 + chunks
+    outs = refs[at : at + count]
+    at += count
+    if chunks:
+        grad_query_ref, grad_pair_ref = refs[at : at + 2]
+        at += 2
     size = len(units)
     first, second, third, fourth, own = [
         refs[at + i * size : at + (i + 1) * size] for i in range(5)
     ]
     sems = refs[at + 5 * size :]
-    sends_c, recvs_c, sends_r, recvs_r, sends_z, recvs_z, sends_g, recvs_g = sems
+    sends_c, recvs_c, sends_r, recvs_r, sends_z, recvs_z, sends_g, recvs_g = sems[:8]
     rep, high, low, core = places()
     me = (rep, place_of(high, low, core))
     sibling = (rep, place_of(high, low, 1 - core))
     far = (rep, place_of(1 - high, low, core))
     near = (rep, place_of(high, 1 - low, core))
     enter(reps)
-    sent = []
-
     def send(src, dst, sends, recvs, at, peer):
-        copy = remote(src, dst, sends, recvs, at, peer)
-        copy.start()
-        sent.append(copy)
+        remote(src, dst, sends, recvs, at, peer).start()
+
+    def left(block, sends, recvs, at):
+        remote(block, block, sends, recvs, at, me).wait_send()
 
     def arrived(block, sends, recvs, at):
         remote(block, block, sends, recvs, at, me).wait_recv()
@@ -397,16 +405,117 @@
             send(block, block, sends_g, recvs_g, u * (reps - 1) + k - 1, peer)
 
     stages = (over_core, over_rep, over_near, over_far)
-    for step in range(size + len(stages) - 1):
+
+    def advance(step):
         for lag, stage in enumerate(stages):
             if 0 <= step - lag < size:
                 stage(step - lag)
+
+    steps = size + len(stages) - 1
+    if not chunks:
+        for step in range(steps):
+            advance(step)
+    else:
+        terms, merged, from_near, from_far, held, sends_k, recvs_k, fetched = sems[8:]
+        pairs = terms.shape[0]
+        each = pairs // chunks
+
+        def fetch(p, wait):
+            for i in range(pairs):
+
+                @pl.when(p == i)
+                def _(i=i):
+                    copy = pltpu.make_async_copy(
+                        pair_refs[i // each].at[:, pl.ds(2 * PAIR * (i % each), 2 * PAIR)],
+                        held.at[i % 2],
+                        fetched.at[i % 2],
+                    )
+                    copy.wait() if wait else copy.start()
+
+        def hop(p, which):
+            if which == 0:
+                return remote(
+                    terms.at[p, :, :, 1 - core], merged.at[p], sends_k, recvs_k, 3 * p, sibling
+                )
+            if which == 1:
+                return remote(
+                    merged.at[p, :, 1 - low], from_near.at[p], sends_k, recvs_k, 3 * p + 1, near
+                )
+            return remote(
+                merged.at[p, 1 - high, low], from_far.at[p], sends_k, recvs_k, 3 * p + 2, far
+            )
+
+        def merge_core(p):
+            arrived(merged.at[p], sends_k, recvs_k, 3 * p)
+            for h in range(2):
+                for w in range(2):
+                    both = [merged[p, h, w], terms[p, h, w, core]]
+                    merged[p, h, w] = summed(both, BF16)
+            hop(p, 1).start()
+
+        def merge_near(p):
+            arrived(from_near.at[p], sends_k, recvs_k, 3 * p + 1)
+            for h in range(2):
+                merged[p, h, low] = summed([merged[p, h, low], from_near[p, h]], BF16)
+            hop(p, 2).start()
+
+        def merge_far(p):
+            arrived(from_far.at[p], sends_k, recvs_k, 3 * p + 2)
+            cols = pl.ds(pl.multiple_of(p * 2 * PAIR, 2 * PAIR), 2 * PAIR)
+            grad_pair_ref[:, cols] = summed([merged[p, high, low], from_far[p]], BF16)
+
+        def compute(p):
+            fetch(p, True)
+            fetch(p + 1, False)
+            cols = pl.ds(pl.multiple_of(p * PAIR, PAIR), PAIR)
+            slot = p % 2
+            query_part, key_part, value_part = pair_grads(
+                query_ref[:, cols], grad_ref[:, cols], held[slot, :, :PAIR], held[slot, :, PAIR:]
+            )
+            grad_query_ref[:, cols] = query_part
+            shape = terms.shape[1:5] + (PAIR,)
+            terms[p, :, :, :, :, :PAIR] = key_part.reshape(shape)
+            terms[p, :, :, :, :, PAIR:] = value_part.reshape(shape)
+            hop(p, 0).start()
+
+        fetch(0, False)
+
+        def step_all(t, carry):
+            for lag, merge in ((1, merge_core), (2, merge_near), (3, merge_far)):
+
+                @pl.when((t >= lag) & (t < pairs + lag))
+                def _(lag=lag, merge=merge):
+                    merge(t - lag)
+
+            @pl.when(t < pairs)
+            def _():
+                compute(t)
+
+            for i in range(steps):
+
+                @pl.when(t == i)
+                def _(i=i):
+                    advance(i)
+
+            return carry
+
+        lax.fori_loop(0, max(pairs + 3, steps), step_all, 0)
+        for p in range(pairs):
+            for which in range(3):
+                hop(p, which).wait_send()
     for u, (a, start, width) in enumerate(units):
         for k in range(1, reps):
             block = outs[a].at[(rep + reps - k) % reps, :, pl.ds(start, width)]
             arrived(block, sends_g, recvs_g, u * (reps - 1) + k - 1)
-    for copy in sent:
-        copy.wait_send()
+    for u, (a, start, width) in enumerate(units):
+        cols = pl.ds(start, width)
+        left(ins[a].at[:, :, 1 - core, :, :, cols], sends_c, recvs_c, u)
+        left(own[u].at[:, 1 - low], sends_z, recvs_z, 2 * u)
+        left(own[u].at[1 - high, low], sends_z, recvs_z, 2 * u + 1)
+        for k in range(1, reps):
+            index = u * (reps - 1) + k - 1
+            left(first[u].at[:, :, (rep + k) % reps], sends_r, recvs_r, index)
+            left(outs[a].at[rep, :, cols], sends_g, recvs_g, index)
 
 
 def split_rows(part):
@@ -415,7 +524,7 @@
     return part.reshape(2, 2, 2, reps, rows // (8 * reps), width)
 
 
-def reduce_many(blocks, pieces, identity):
+def reduce_many(blocks, pieces, identity, query=None, grad=None, pairs=()):
     reps = lax.axis_size("rep")
     count = len(blocks)
     units = [
@@ -433,13 +542,37 @@
         ]
 
     total = len(units)
+    out_shape = [
+        jax.ShapeDtypeStruct((reps,) + block.shape[4:], block.dtype) for block in blocks
+    ]
+    operands = list(blocks)
+    in_specs = [vmem] * count
+    more = []
+    if pairs:
+        tokens, width = query.shape
+        number = width // PAIR
+        block = (tokens, 2 * PAIR)
+        operands += [query, grad] + list(pairs)
+        in_specs += [vmem] * 2 + [pl.BlockSpec(memory_space=pl.ANY)] * len(pairs)
+        out_shape += [
+            jax.ShapeDtypeStruct((tokens, width), BF16),
+            jax.ShapeDtypeStruct((tokens, 2 * width), BF16),
+        ]
+        more = [
+            pltpu.VMEM((number, 2, 2, 2) + block, BF16),
+            pltpu.VMEM((number, 2, 2) + block, BF16),
+            pltpu.VMEM((number, 2) + block, BF16),
+            pltpu.VMEM((number,) + block, BF16),
+            pltpu.VMEM((2, pairs[0].shape[0], 2 * PAIR), BF16),
+            dma((3 * number,)),
+            dma((3 * number,)),
+            dma((2,)),
+        ]
     sums = pl.pallas_call(
-        functools.partial(reduce_kernel, units, count, reps),
-        out_shape=[
-            jax.ShapeDtypeStruct((reps,) + block.shape[4:], block.dtype) for block in blocks
-        ],
-        in_specs=[vmem] * count,
-        out_specs=[vmem] * count,
+        functools.partial(reduce_kernel, units, count, reps, len(pairs)),
+        out_shape=out_shape,
+        in_specs=in_specs,
+        out_specs=[vmem] * len(out_shape),
         scratch_shapes=buffers(2, 2, reps)
         + buffers(reps - 1, 2, 2)
         + buffers(2)
@@ -448,12 +581,14 @@
         + [dma((total,))] * 2
         + [dma((total * (reps - 1),))] * 2
         + [dma((total * 2,))] * 2
-        + [dma((total * (reps - 1),))] * 2,
+        + [dma((total * (reps - 1),))] * 2
+        + more,
         compiler_params=pltpu.CompilerParams(
-            collective_id=identity, has_side_effects=True, vmem_limit_bytes=56 * 1024 * 1024
+            collective_id=identity, has_side_effects=True, vmem_limit_bytes=60 * 1024 * 1024
         ),
-    )(*blocks)
-    return [total.reshape(-1, total.shape[2]).astype(F32) for total in sums]
+    )(*operands)
+    totals = [total.reshape(-1, total.shape[2]).astype(F32) for total in sums[:count]]
+    return totals + list(sums[count:])
 
 
 def blocked(shard):
@@ -586,29 +721,30 @@
     part_output = over_rows(context_low, grad_attn).astype(BF16)
     grad_context = against(grad_attn, w_output).astype(BF16)
 
-    grad_queries = []
-    grad_pairs = []
-    terms = []
-    for i in range(CHUNKS):
-        grad_query, grad_terms = attend_back(
-            queries[i], grad_context[:, chunk * i : chunk * (i + 1)], pairs[i]
+    if fast:
+        full_down, full_up, full_output, grad_query_low, grad_pair_low = reduce_many(
+            [split_rows(part) for part in (part_down, part_up, part_output)],
+            (2, 2, 1),
+            3,
+            query_scaled,
+            grad_context,
+            pairs,
         )
-        grad_queries.append(grad_query)
-        terms.append(grad_terms)
-        grad_pairs.append(
-            lax.psum_scatter(grad_terms, "cp", scatter_dimension=0, tiled=True)
-        )
-    grad_query_low = jnp.concatenate(grad_queries, axis=1)
-    part_query = over_rows(local_tokens, grad_query_low).astype(BF16)
-    if fast:
-        parts = (part_down, part_up, part_output, part_query)
-        parts, _ = lax.optimization_barrier((parts, terms))
-        full_down, full_up, full_output, full_query = reduce_many(
-            [split_rows(part) for part in parts], (2, 2, 1, 1), 3
-        )
-    grad_pair_low = jnp.concatenate(grad_pairs, axis=1)
+    else:
+        grad_queries = []
+        grad_pairs = []
+        for i in range(CHUNKS):
+            grad_query, grad_terms = attend_back(
+                queries[i], grad_context[:, chunk * i : chunk * (i + 1)], pairs[i]
+            )
+            grad_queries.append(grad_query)
+            grad_pairs.append(
+                lax.psum_scatter(grad_terms, "cp", scatter_dimension=0, tiled=True)
+            )
+        grad_query_low = jnp.concatenate(grad_queries, axis=1)
+        grad_pair_low = jnp.concatenate(grad_pairs, axis=1)
     grad_proj = jnp.concatenate([grad_query_low, grad_pair_low], axis=1)
-    part_pair = over_rows(local_tokens, grad_pair_low).astype(BF16)
+    part_proj = over_rows(local_tokens, grad_proj).astype(BF16)
     grad_tokens = grad_resid1 + against(grad_proj, w_proj)
     proj_sums = column_sum(grad_proj)
     _, grad_value_bias = unmixed(proj_sums[None, width:])
@@ -631,16 +767,16 @@
     )
     if fast:
         flat = jnp.pad(flat, ((0, 0), (0, -flat.shape[1] % (8 * 128 * reps))))
-        full_pair, sums = reduce_many(
-            (split_rows(part_pair), flat.reshape(2, 2, 2, reps, -1, 128)), (3, 1), 4
+        full_proj, sums = reduce_many(
+            (split_rows(part_proj), flat.reshape(2, 2, 2, reps, -1, 128)), (3, 1), 4
         )
         sums = sums.reshape(-1)
     else:
         shards = [
             scatter_all(part)
-            for part in (part_down, part_up, part_output, part_query, part_pair)
+            for part in (part_down, part_up, part_output, part_proj)
         ]
-        full_down, full_up, full_output, full_query, full_pair = [
+        full_down, full_up, full_output, full_proj = [
             part.astype(F32) for part in lax.psum(tuple(shards), "rep")
         ]
         sums = lax.psum(flat, ("rep", "cp"))
@@ -653,11 +789,11 @@
     entries = lax.axis_size("rep") * owners * row_count * width
     rms_values = jnp.sqrt(sums[at : at + 1] / entries)
 
-    grad_key_weight, grad_value_weight = unmixed(full_pair)
+    grad_key_weight, grad_value_weight = unmixed(full_proj[:, width:])
     return (
         layer_out[None],
         grad_tokens[None],
-        full_query,
+        full_proj[:, :width],
         reduced[0],
         grad_key_weight,
         grad_value_weight,

time: 402 us -> 364 us (0.905); the launches traced: 396 us -> 363 us
  Pallas kernels: 278 us -> 258 us
  matrix products: 37.3 us -> 31.9 us
  other arithmetic: 14.2 us -> 8.82 us
    pallas_call x5 -> x2, Pallas kernels: 161 us -> 143 us  [reduce_many(): pl.pallas_call(functools.partial(reduce_kernel, units, count, reps, len(p...]
    dot_general x5 -> x4, matrix products: 15.1 us -> 11.8 us  [over_rows(): lax.dot_general(left, right, (((0,), (0,)), ((), ())), preferred_element_...]
    unnamed x120 -> x84, local copies, waits for them, and re-layouts: 13.8 us -> 12.9 us
  transfers between devices with their start and end apart: 6 -> 3, of which waited for: 1 -> 1; matrix products, arithmetic and copies ran while one was open for 7% -> 1% of each run, Pallas kernels for 50% -> 22%
where the time goes in v1:
time: 364 us; the launch traced here: 363 us
  Pallas kernels  258 us (71%)
  matrix products  31.9 us (9%)
  local copies, waits for them, and re-layouts  28.4 us (8%)
  waiting for transfers between devices  19.3 us (5%)
  between operations  16.1 us (4%)
  other arithmetic  8.82 us (2%)
    pallas_call x2, Pallas kernels, reduce_many(): pl.pallas_call(functools.partial(reduce_kernel, units, count, reps, len(p...  143 us
    pallas_call x2, Pallas kernels, gather_many(): pl.pallas_call(functools.partial(gather_kernel, units, count, reps), out_...  96.3 us
    pallas_call x3, Pallas kernels, attend(): pl.pallas_call(forward_kernel, grid=(width // PAIR,), in_specs=[column_bl...  19.4 us
    all_gather x3, waiting for transfers between devices, on_device(): lax.all_gather(pair_rows[:, 2 * chunk * i:2 * chunk * (i + 1)], 'cp', axi...  18 us
    unnamed x84, local copies, waits for them, and re-layouts  12.9 us
    dot_general x4, matrix products, over_rows(): lax.dot_general(left, right, (((0,), (0,)), ((), ())), preferred_element_...  11.8 us
    dot_general x5, matrix products, matmul(): return jnp.dot(left, right, preferred_element_type=F32)  11.6 us
    dot_general x4, matrix products, against(): lax.dot_general(left, right, (((1,), (1,)), ((), ())), preferred_element_...  8.56 us
  transfers between devices with their start and end apart: 3, of which 1 were waited for; matrix products, arithmetic and copies ran while one was open for 1% of the time, Pallas kernels for 22%

profile of v1, /device:TPU:0, one launch (start us, length us, event | category | flops | bytes accessed | tf_op | source)
XLA Modules:
  0.0 363.0 jit_solution(12488973024623605722)
XLA Ops:
  7.2 0.7 pad_bitcast_fusion.2
  7.9 0.7 pad_bitcast_fusion.4
  8.6 0.7 pad_bitcast_fusion.6
  9.3 0.7 pad_bitcast_fusion.8
  10.0 0.7 concatenate.33
  10.7 0.6 pad_bitcast_fusion.1.refs_1_
  11.3 0.9 constant_dynamic-update-slice_fusion.12
  12.2 0.8 constant_dynamic-update-slice_fusion.11
  13.0 0.8 constant_dynamic-update-slice_fusion.10
  13.7 0.7 constant_dynamic-update-slice_fusion.9
  14.5 0.7 constant_dynamic-update-slice_fusion.8
  15.2 0.7 constant_dynamic-update-slice_fusion.7
  16.0 0.7 constant_dynamic-update-slice_fusion.6
  16.7 0.7 constant_dynamic-update-slice_fusion.5
  17.5 0.7 constant_dynamic-update-slice_fusion.4
  18.2 0.7 constant_dynamic-update-slice_fusion.3
  19.0 0.7 constant_dynamic-update-slice_fusion.2
  19.7 0.7 constant_dynamic-update-slice_fusion.1
  20.5 0.7 constant_dynamic-update-slice_fusion
  21.2 0.8 copy-done.2
  22.0 30.4 %shard_map.304 = (bf16[2,2,2,4,24,2304]{5,4,3,2,1,0:T(8,128)(2,1)}, bf16[2,2,2,4,8,128]{5,4,3,2,1,0:T(8,128)(2,1)}) custom-call(bf16[4,24,2304]{2,1,0:T(8,128)(2,1)} %bitcast.116, bf16[4,8,128]{2,1,0:T(8,128)(2,1)} %pad_bitcast_fusion.1.refs_1_), custom_call_target="tpu_custom_call" | custom-call | tf_op jit(solution)/shard_map/pallas_call | solution.py:296
  52.4 1.0 fusion.36
  53.7 2.6 fusion.8
  56.4 0.9 fusion.34
  57.3 0.7 all-gather.6.cloned.1.call-update
  58.1 0.7 all-gather.8.cloned.1.call-update
  58.8 0.9 pad_maximum_fusion
  59.8 65.9 %shard_map.305 = (bf16[2,2,2,4,24,3840]{5,4,3,2,1,0:T(8,128)(2,1)}, bf16[2,2,2,4,96,768]{5,4,3,2,1,0:T(8,128)(2,1)}) custom-call(bf16[4,24,3840]{2,1,0:T(8,128)(2,1)} %bitcast.114, bf16[4,96,768]{2,1,0:T(8,128)(2,1)} %bitcast.117), custom_call_target="tpu_custom_call" | custom-call | tf_op jit(solution)/shard_map/pallas_call | solution.py:296
  125.7 1.8 fusion.17.refs_3_
  127.5 0.8 fusion.35
  128.6 0.7 slice_convert_fusion
  129.7 6.6 %shard_map.306 = bf16[256,256]{1,0:T(8,128)(2,1)} custom-call(bf16[256,256]{1,0:T(8,128)(2,1)} %get-tuple-element.40.query_ref, bf16[2048,512]{1,0:T(8,128)(2,1)} %all-gather.4.cloned.1.call-done.pair_ref.refs_5_), custom_call_target="tpu_custom_call" | custom-call | tf_op jit(solution)/shard_map/pallas_call | solution.py:109
  136.3 6.4 %shard_map.307 = bf16[256,256]{1,0:T(8,128)(2,1)} custom-call(bf16[256,256]{1,0:T(8,128)(2,1)} %get-tuple-element.41.query_ref, bf16[2048,512]{1,0:T(8,128)(2,1)} %all-gather.6.cloned.1.call-done.pair_ref.refs_6_), custom_call_target="tpu_custom_call" | custom-call | tf_op jit(solution)/shard_map/pallas_call | solution.py:109
  142.7 18.0 %all-gather.8.cloned.1.call-done.pair_ref.refs_7_ = bf16[2048,512]{1,0:T(8,128)(2,1)} async-done(((bf16[256,512]{1,0:T(8,128)(2,1)}), bf16[2048,512]{1,0:T(8,128)(2,1)}) %all-gather.8.cloned.1.call-update) | async-done | bytes 2097168 | tf_op jit(solution)/shard_map/all_gather | solution.py:674
  160.6 6.4 %shard_map.308 = bf16[256,256]{1,0:T(8,128)(2,1)} custom-call(bf16[256,256]{1,0:T(8,128)(2,1)} %get-tuple-element.42.query_ref, bf16[2048,512]{1,0:T(8,128)(2,1)} %all-gather.8.cloned.1.call-done.pair_ref.refs_7_), custom_call_target="tpu_custom_call" | custom-call | tf_op jit(solution)/shard_map/pallas_call | solution.py:109
  167.0 2.0 fusion.38
  169.3 3.7 %multiply_convert_fusion = (bf16[256,3072]{1,0:T(8,128)(2,1)S(1)}, f32[256,3072]{1,0:T(8,128)S(1)}) fusion(f32[3072]{0:T(1024)S(1)} %reshape.362, bf16[768,3840]{1,0:T(8,128)(2,1)} %bitcast.134, f32[256,768]{1,0:T(8,128)S(1)} %get-tuple-element.103, f32[768]{0:T(1024)S(1)} %reshape.361, f32[768]{0:T(1024)S(1)} %reshape.360, f32[256]{0:T(256)S(1)} %fusion.26, ...), kind=kOutput, calls=%fused_computation.10 | convolution fusion | flops 1213661184 | bytes 10244096 | tf_op jit(solution)/shard_map/dot_general | solution.py:31
  173.0 1.5 fusion.39
  174.8 0.3 fusion.21
  175.2 1.2 fusion.33
  176.6 3.0 convert_reduce_fusion
  179.6 1.7 multiply_reduce_fusion.1
  181.4 0.3 fusion.32
  181.9 1.3 convolution_convert_fusion.4.refs_4_
  183.1 1.5 convolution_convert_fusion.3
  184.7 3.7 %convolution_convert_fusion.1 = bf16[768,3072]{1,0:T(8,128)(2,1)} fusion(bf16[256,3072]{1,0:T(8,128)(2,1)S(1)} %get-tuple-element.60, f32[256,768]{1,0:T(8,128)S(1)} %get-tuple-element.103, f32[768]{0:T(1024)S(1)} %reshape.361, f32[768]{0:T(1024)S(1)} %reshape.360, f32[256]{0:T(256)S(1)} %fusion.26, f32[256]{0:T(256)S(1)} %broadcast_multiply_fusion.1), kind=kOutput, calls=%fused_computation.1 | convolution fusion | flops 1211301888 | bytes 7086080 | tf_op jit(solution)/shard_map/dot_general | solution.py:35
  188.4 3.6 convolution_convert_fusion.2
  192.0 103.5 %shard_map.309 = (bf16[4,96,768]{2,1,0:T(8,128)(2,1)}, bf16[4,24,3072]{2,1,0:T(8,128)(2,1)}, bf16[4,24,768]{2,1,0:T(8,128)(2,1)}, bf16[256,768]{1,0:T(8,128)(2,1)}, bf16[256,1536]{1,0:T(8,128)(2,1)}) custom-call(bf16[2,2,2,4,96,768]{5,4,3,2,1,0:T(8,128)(2,1)} %bitcast.111, bf16[2,2,2,4,24,3072]{5,4,3,2,1,0:T(8,128)(2,1)} %bitcast.112, ...), custom_call_target="tpu_custom_call" | custom-call | tf_op jit(solution)/shard_map/pallas_call | solution.py:571
  295.5 1.2 constant_dynamic-update-slice_fusion.26
  296.7 1.2 constant_dynamic-update-slice_fusion.25
  298.1 2.6 multiply_reduce_fusion
  300.7 2.9 convolution_convert_fusion
  304.2 0.7 broadcast_in_dim.44
  305.0 0.7 copy.57
  305.7 39.2 %shard_map.310 = (bf16[4,24,2304]{2,1,0:T(8,128)(2,1)}, f32[4,8,128]{2,1,0:T(8,128)}) custom-call(bf16[2,2,2,4,24,2304]{5,4,3,2,1,0:T(8,128)(2,1)} %bitcast.113, f32[2,2,2,4,8,128]{5,4,3,2,1,0:T(8,128)} %bitcast.118), custom_call_target="tpu_custom_call" | custom-call | tf_op jit(solution)/shard_map/pallas_call | solution.py:571
  344.8 1.1 bitcast_convert_fusion.2
  346.0 0.7 slice.356
  346.7 1.5 fusion.37
  348.2 1.3 slice.374
  349.6 1.2 slice.378
  351.4 1.1 bitcast_convert_fusion
  352.6 1.2 bitcast_convert_fusion.1
  353.7 0.7 bitcast_convert_fusion.3
  354.6 0.7 copy-done.13
  (126 shorter events, 3.0 us)
Async XLA Ops:
  7.2 122.5 %all-gather.4.cloned.1.call-start = ((), (), s32[]{:S(2)}) async-start(), calls=%async_computation | async-start | bytes 2359296 | tf_op jit(solution)/shard_map/all_gather | solution.py:674
  21.2 0.8 copy-start.2
  53.7 5.1 %copy-start.5 = (bf16[96,3072]{1,0:T(8,128)(2,1)S(1)}, bf16[96,3072]{1,0:T(8,128)(2,1)}, u32[]{:S(2)}) copy-start(bf16[96,3072]{1,0:T(8,128)(2,1)} %param.27) | copy-start | bytes 1769476
  53.7 5.1 %copy-start.7 = (bf16[96,768]{1,0:T(8,128)(2,1)S(1)}, bf16[96,768]{1,0:T(8,128)(2,1)}, u32[]{:S(2)}) copy-start(bf16[96,768]{1,0:T(8,128)(2,1)} %param.23) | copy-start | bytes 442372
  56.3 69.3 %copy-start.6 = (bf16[1,256,768]{2,1,0:T(8,128)(2,1)S(1)}, bf16[1,256,768]{2,1,0:T(8,128)(2,1)}, u32[]{:S(2)}) copy-start(bf16[1,256,768]{2,1,0:T(8,128)(2,1)} %param.17) | copy-start | bytes 1179652
  57.3 79.0 %all-gather.6.cloned.1.call-start = ((), (), s32[]{:S(2)}) async-start(), calls=%async_computation.1 | async-start | bytes 2359296 | tf_op jit(solution)/shard_map/all_gather | solution.py:674
  58.0 102.6 %all-gather.8.cloned.1.call-start = ((), (), s32[]{:S(2)}) async-start(), calls=%async_computation.2 | async-start | bytes 2359296 | tf_op jit(solution)/shard_map/all_gather | solution.py:674
  58.8 70.8 %copy-start = (f32[1,256,768]{2,1,0:T(8,128)S(1)}, f32[1,256,768]{2,1,0:T(8,128)}, u32[]{:S(2)}) copy-start(f32[1,256,768]{2,1,0:T(8,128)} %param.33) | copy-start | bytes 2359300
  127.5 15.2 %copy-start.1 = (bf16[256,768]{1,0:T(8,128)(2,1)}, bf16[256,768]{1,0:T(8,128)(2,1)S(1)}, u32[]{:S(2)}) copy-start(bf16[256,768]{1,0:T(8,128)(2,1)S(1)} %fusion.17.refs_3_) | copy-start | bytes 1179652
  136.3 30.8 %copy-start.9 = (bf16[256,256]{1,0:T(8,128)(2,1)S(1)}, bf16[256,256]{1,0:T(8,128)(2,1)}, u32[]{:S(2)}) copy-start(bf16[256,256]{1,0:T(8,128)(2,1)} %shard_map.306) | copy-start | bytes 393220
  169.0 4.0 %slice-start.3 = ((s8[4718592]{0:T(1024)(128)(4,1)}), s8[4194304]{0:T(1024)(128)(4,1)S(1)}, s32[]{:S(2)}) async-start(s8[4718592]{0:T(1024)(128)(4,1)} %bitcast.139), calls=%async_computation.6 | async-start | bytes 8388608
  169.3 3.8 %slice-start.4 = ((s8[4718592]{0:T(1024)(128)(4,1)}), s8[524288]{0:T(1024)(128)(4,1)S(1)}, s32[]{:S(2)}) async-start(s8[4718592]{0:T(1024)(128)(4,1)} %bitcast.139), calls=%async_computation.7 | async-start | bytes 1048576
  176.4 3.2 slice-start.1
  176.6 3.0 slice-start.2
  181.3 1.8 copy-start.10
  181.3 1.8 copy-start.11
  295.5 2.6 copy-start.15
  298.1 2.6 copy-start.12
  300.7 3.1 slice-start
  304.9 46.5 %copy-start.4 = (bf16[4,96,768]{2,1,0:T(8,128)(2,1)S(1)}, bf16[4,96,768]{2,1,0:T(8,128)(2,1)}, u32[]{:S(2)}) copy-start(bf16[4,96,768]{2,1,0:T(8,128)(2,1)} %get-tuple-element.51) | copy-start | bytes 1769476
  305.7 46.9 %copy-start.3 = (bf16[4,24,3072]{2,1,0:T(8,128)(2,1)S(1)}, bf16[4,24,3072]{2,1,0:T(8,128)(2,1)}, u32[]{:S(2)}) copy-start(bf16[4,24,3072]{2,1,0:T(8,128)(2,1)} %get-tuple-element.50) | copy-start | bytes 1769476
  344.8 8.9 %copy-start.8 = (bf16[4,24,768]{2,1,0:T(8,128)(2,1)S(1)}, bf16[4,24,768]{2,1,0:T(8,128)(2,1)}, u32[]{:S(2)}) copy-start(bf16[4,24,768]{2,1,0:T(8,128)(2,1)} %get-tuple-element.49) | copy-start | bytes 442372
  354.6 0.7 copy-start.13
  354.6 0.8 copy-start.14
Sparse Core Ops, SparseCore 0:
  57.4 41.5 all-gather.3
  101.1 28.7 all-gather.5
  132.1 28.5 all-gather.7

commit v2 on v1

--- a/solution.py
+++ b/solution.py
@@ -48,10 +48,7 @@
     return (lane >= head * HD) & (lane < (head + 1) * HD)
 
 
-def forward_kernel(query_ref, pair_ref, context_ref):
-    keys = pair_ref[:, :PAIR]
-    values = pair_ref[:, PAIR:]
-    query = query_ref[...]
+def pair_context(query, keys, values):
     total = None
     for head in range(2):
         mask = head_mask(query.shape, head)
@@ -61,7 +58,11 @@
         inverse = 1.0 / jnp.sum(weight, axis=-1, keepdims=True)
         part = matmul((weight * inverse).astype(BF16), values)
         total = part if head == 0 else jnp.where(mask, part, total)
-    context_ref[...] = total.astype(BF16)
+    return total.astype(BF16)
+
+
+def forward_kernel(query_ref, pair_ref, context_ref):
+    context_ref[...] = pair_context(query_ref[...], pair_ref[:, :PAIR], pair_ref[:, PAIR:])
 
 
 def pair_grads(query, grad, keys, values):
@@ -192,23 +193,31 @@
     )
 
 
-def gather_kernel(units, count, reps, *refs):
+def gather_kernel(units, count, reps, pairs, *refs):
     ins = refs[:count]
-    outs = refs[count : 2 * count]
-    sends_z, recvs_z, sends_r, recvs_r, sends_c, recvs_c, local = refs[2 * count :]
+    at = count
+    if pairs:
+        query_ref, rows_ref = refs[at : at + 2]
+        at += 2
+    outs = refs[at : at + count]
+    at += count
+    if pairs:
+        context_ref, pair_ref = refs[at : at + 2]
+        at += 2
+    sends_z, recvs_z, sends_r, recvs_r, sends_c, recvs_c, local = refs[at : at + 7]
     rep, high, low, core = places()
     me = (rep, place_of(high, low, core))
     sibling = (rep, place_of(high, low, 1 - core))
     far = (rep, place_of(1 - high, low, core))
     near = (rep, place_of(high, 1 - low, core))
     enter(reps)
-    sent = []
     copies = []
 
     def send(src, dst, sends, recvs, at, peer):
-        copy = remote(src, dst, sends, recvs, at, peer)
-        copy.start()
-        sent.append(copy)
+        remote(src, dst, sends, recvs, at, peer).start()
+
+    def left(block, sends, recvs, at):
+        remote(block, block, sends, recvs, at, me).wait_send()
 
     def arrived(block, sends, recvs, at):
         remote(block, block, sends, recvs, at, me).wait_recv()
@@ -225,6 +234,18 @@
         from_high, from_low = origins[which]
         return outs[at].at[from_high, from_low, side, quarter, :, pl.ds(start, size)]
 
+    def held(p, which, side):
+        from_high, from_low = origins[which]
+        return pair_ref.at[p, from_high, from_low, side]
+
+    if pairs:
+        sends_k, recvs_k, sends_s, recvs_s = refs[at + 7 :]
+        for p in range(pairs):
+            pair_ref[p, high, low, core] = rows_ref[:, 2 * PAIR * p : 2 * PAIR * (p + 1)]
+            own = held(p, 0, core)
+            send(own, own, sends_k, recvs_k, 3 * p + 1, far)
+            send(own, own, sends_k, recvs_k, 3 * p, near)
+            send(own, own, sends_s, recvs_s, 4 * p, sibling)
     for u, (at, start, size) in enumerate(units):
         block = ins[at].at[rep, :, pl.ds(start, size)]
         send(block, block_of(u, 0, core, rep), sends_z, recvs_z, 3 * u + 1, far)
@@ -256,7 +277,8 @@
         send(whole, whole, sends_c, recvs_c, 4 * u + which, sibling)
 
     total = len(units)
-    for step in range(total + 2):
+
+    def advance(step):
         if step < total:
             spread(step, 1)
             spread(step, 2)
@@ -265,12 +287,74 @@
         if 2 <= step:
             for which in range(1, 4):
                 pass_on(step - 2, which)
+
+    def take(p, which):
+        block = held(p, which, core)
+        arrived(block, sends_k, recvs_k, 3 * p + which - 1)
+        if which == 2:
+            send(block, block, sends_k, recvs_k, 3 * p + 2, near)
+        send(block, block, sends_s, recvs_s, 4 * p + which, sibling)
+
+    def compute(p):
+        for which in range(4):
+            arrived(held(p, which, 1 - core), sends_s, recvs_s, 4 * p + which)
+        cols = pl.ds(pl.multiple_of(p * PAIR, PAIR), PAIR)
+        shape = (-1, PAIR)
+        context_ref[:, cols] = pair_context(
+            query_ref[:, cols],
+            pair_ref[p, :, :, :, :, :PAIR].reshape(shape),
+            pair_ref[p, :, :, :, :, PAIR:].reshape(shape),
+        )
+
+    steps = total + 2
+    if not pairs:
+        for step in range(steps):
+            advance(step)
+    else:
+
+        def step_all(t, carry):
+            @pl.when(t < pairs)
+            def _():
+                take(t, 1)
+                take(t, 2)
+
+            @pl.when((t >= 1) & (t < pairs + 1))
+            def _():
+                take(t - 1, 3)
+
+            for i in range(steps):
+
+                @pl.when(t == i)
+                def _(i=i):
+                    advance(i)
+
+            @pl.when((t >= 2) & (t < pairs + 2))
+            def _():
+                compute(t - 2)
+
+            return carry
+
+        lax.fori_loop(0, max(pairs + 2, steps), step_all, 0)
     for u in range(total):
         for which in range(4):
             block = block_of(u, which, 1 - core, slice(None))
             arrived(block, sends_c, recvs_c, 4 * u + which)
-    for copy in sent:
-        copy.wait_send()
+    for u, (at, start, size) in enumerate(units):
+        cols = pl.ds(start, size)
+        left(ins[at].at[rep, :, cols], sends_z, recvs_z, 3 * u)
+        left(ins[at].at[rep, :, cols], sends_z, recvs_z, 3 * u + 1)
+        left(block_of(u, 2, core, rep), sends_z, recvs_z, 3 * u + 2)
+        left(ins[at].at[:, :, cols], sends_c, recvs_c, 4 * u)
+        for which in range(1, 4):
+            left(block_of(u, which, core, slice(None)), sends_c, recvs_c, 4 * u + which)
+            for j in range(1, reps):
+                index = (3 * u + which - 1) * (reps - 1) + j - 1
+                left(block_of(u, which, core, rep), sends_r, recvs_r, index)
+    for p in range(pairs):
+        for at, which in enumerate((0, 0, 2)):
+            left(held(p, which, core), sends_k, recvs_k, 3 * p + at)
+        for which in range(4):
+            left(held(p, which, core), sends_s, recvs_s, 4 * p + which)
     for copy in copies:
         copy.wait()
 
@@ -282,7 +366,7 @@
     return [(size * i, size) for i in range(pieces)]
 
 
-def gather_many(shards, pieces, identity):
+def gather_many(shards, pieces, identity, query=None, rows=None):
     reps = lax.axis_size("rep")
     count = len(shards)
     units = [
@@ -293,19 +377,37 @@
     total = len(units)
     hops = 3 * total * (reps - 1)
     dma = pltpu.SemaphoreType.DMA
+    vmem = pl.BlockSpec(memory_space=pltpu.VMEM)
+    out_shape = [
+        jax.ShapeDtypeStruct((2, 2, 2) + shard.shape, shard.dtype) for shard in shards
+    ]
+    operands = list(shards)
+    spaces = []
+    more = []
+    pairs = 0
+    if query is not None:
+        pairs = query.shape[1] // PAIR
+        operands += [query, rows]
+        spaces = [vmem] * 2
+        out_shape += [
+            jax.ShapeDtypeStruct(query.shape, BF16),
+            jax.ShapeDtypeStruct((pairs, 2, 2, 2, rows.shape[0], 2 * PAIR), BF16),
+        ]
+        more = [dma((3 * pairs,))] * 2 + [dma((4 * pairs,))] * 2
     return pl.pallas_call(
-        functools.partial(gather_kernel, units, count, reps),
-        out_shape=[
-            jax.ShapeDtypeStruct((2, 2, 2) + shard.shape, shard.dtype) for shard in shards
-        ],
-        in_specs=[pl.BlockSpec(memory_space=pl.ANY)] * count,
-        out_specs=[pl.BlockSpec(memory_space=pl.ANY)] * count,
+        functools.partial(gather_kernel, units, count, reps, pairs),
+        out_shape=out_shape,
+        in_specs=[pl.BlockSpec(memory_space=pl.ANY)] * count + spaces,
+        out_specs=[pl.BlockSpec(memory_space=pl.ANY)] * count + spaces,
         scratch_shapes=[dma((3 * total,))] * 2
         + [dma((hops,))] * 2
         + [dma((4 * total,))] * 2
-        + [dma((count,))],
-        compiler_params=pltpu.CompilerParams(collective_id=identity, has_side_effects=True),
-    )(*shards)
+        + [dma((count,))]
+        + more,
+        compiler_params=pltpu.CompilerParams(
+            collective_id=identity, has_side_effects=True, vmem_limit_bytes=60 * 1024 * 1024
+        ),
+    )(*operands)
 
 
 def summed(parts, kind):
@@ -315,16 +417,15 @@
     return total.astype(kind)
 
 
-def reduce_kernel(units, count, reps, chunks, *refs):
+def reduce_kernel(units, count, reps, fused, *refs):
     ins = refs[:count]
     at = count
-    if chunks:
-        query_ref, grad_ref = refs[at : at + 2]
-        pair_refs = refs[at + 2 : at + 2 + chunks]
-        at += 2 + chunks
+    if fused:
+        query_ref, grad_ref, pair_ref = refs[at : at + 3]
+        at += 3
     outs = refs[at : at + count]
     at += count
-    if chunks:
+    if fused:
         grad_query_ref, grad_pair_ref = refs[at : at + 2]
         at += 2
     size = len(units)
@@ -412,25 +513,15 @@
                 stage(step - lag)
 
     steps = size + len(stages) - 1
-    if not chunks:
+    if not fused:
         for step in range(steps):
             advance(step)
     else:
         terms, merged, from_near, from_far, held, sends_k, recvs_k, fetched = sems[8:]
         pairs = terms.shape[0]
-        each = pairs // chunks
-
-        def fetch(p, wait):
-            for i in range(pairs):
-
-                @pl.when(p == i)
-                def _(i=i):
-                    copy = pltpu.make_async_copy(
-                        pair_refs[i // each].at[:, pl.ds(2 * PAIR * (i % each), 2 * PAIR)],
-                        held.at[i % 2],
-                        fetched.at[i % 2],
-                    )
-                    copy.wait() if wait else copy.start()
+
+        def fetch(p):
+            return pltpu.make_async_copy(pair_ref.at[p], held.at[p % 2], fetched.at[p % 2])
 
         def hop(p, which):
             if which == 0:
@@ -465,8 +556,12 @@
             grad_pair_ref[:, cols] = summed([merged[p, high, low], from_far[p]], BF16)
 
         def compute(p):
-            fetch(p, True)
-            fetch(p + 1, False)
+            fetch(p).wait()
+
+            @pl.when(p < pairs - 1)
+            def _():
+                fetch(p + 1).start()
+
             cols = pl.ds(pl.multiple_of(p * PAIR, PAIR), PAIR)
             slot = p % 2
             query_part, key_part, value_part = pair_grads(
@@ -478,7 +573,7 @@
             terms[p, :, :, :, :, PAIR:] = value_part.reshape(shape)
             hop(p, 0).start()
 
-        fetch(0, False)
+        fetch(0).start()
 
         def step_all(t, carry):
             for lag, merge in ((1, merge_core), (2, merge_near), (3, merge_far)):
@@ -524,7 +619,7 @@
     return part.reshape(2, 2, 2, reps, rows // (8 * reps), width)
 
 
-def reduce_many(blocks, pieces, identity, query=None, grad=None, pairs=()):
+def reduce_many(blocks, pieces, identity, query=None, grad=None, pairs=None):
     reps = lax.axis_size("rep")
     count = len(blocks)
     units = [
@@ -548,12 +643,12 @@
     operands = list(blocks)
     in_specs = [vmem] * count
     more = []
-    if pairs:
+    if pairs is not None:
         tokens, width = query.shape
         number = width // PAIR
         block = (tokens, 2 * PAIR)
-        operands += [query, grad] + list(pairs)
-        in_specs += [vmem] * 2 + [pl.BlockSpec(memory_space=pl.ANY)] * len(pairs)
+        operands += [query, grad, pairs]
+        in_specs += [vmem] * 2 + [pl.BlockSpec(memory_space=pl.ANY)]
         out_shape += [
             jax.ShapeDtypeStruct((tokens, width), BF16),
             jax.ShapeDtypeStruct((tokens, 2 * width), BF16),
@@ -563,13 +658,13 @@
             pltpu.VMEM((number, 2, 2) + block, BF16),
             pltpu.VMEM((number, 2) + block, BF16),
             pltpu.VMEM((number,) + block, BF16),
-            pltpu.VMEM((2, pairs[0].shape[0], 2 * PAIR), BF16),
+            pltpu.VMEM((2,) + pairs.shape[1:], BF16),
             dma((3 * number,)),
             dma((3 * number,)),
             dma((2,)),
         ]
     sums = pl.pallas_call(
-        functools.partial(reduce_kernel, units, count, reps, len(pairs)),
+        functools.partial(reduce_kernel, units, count, reps, pairs is not None),
         out_shape=out_shape,
         in_specs=in_specs,
         out_specs=[vmem] * len(out_shape),
@@ -670,33 +765,31 @@
     pair_bias = mixed(jnp.zeros_like(b_value)[None], b_value[None])
     pair_rows = (matmul(local_tokens, w_pair) + pair_bias).astype(BF16)
     chunk = width // CHUNKS
-    pairs = [
-        lax.all_gather(
-            pair_rows[:, 2 * chunk * i : 2 * chunk * (i + 1)], "cp", axis=0, tiled=True
-        )
-        for i in range(CHUNKS)
-    ]
     query_rows = (matmul(local_tokens, w_proj[:, :width]) + b_query).astype(BF16)
     query_scaled = query_rows * jnp.asarray(1.0 / math.sqrt(HD), BF16)
-    queries = [query_scaled[:, chunk * i : chunk * (i + 1)] for i in range(CHUNKS)]
     wide_shard = jnp.concatenate([output_weight, up_weight], axis=1)
     if fast:
-        wide_shard, down_shard, _ = lax.optimization_barrier(
-            (wide_shard, down_weight, pair_rows)
+        w_wide, w_down, context_low, pairs = gather_many(
+            (blocked(wide_shard), blocked(down_weight)), (2, 2), 2, query_scaled, pair_rows
         )
-        w_wide, w_down = gather_many((blocked(wide_shard), blocked(down_shard)), (2, 2), 2)
         w_wide = w_wide.reshape(-1, wide_shard.shape[1])
         w_down = w_down.reshape(-1, width)
-        w_wide, queries = lax.optimization_barrier((w_wide, queries))
+        pairs = pairs.reshape(pairs.shape[0], -1, 2 * PAIR)
     else:
         w_wide = gather_all(wide_shard)
         w_down = gather_all(down_weight)
+        queries = [query_scaled[:, chunk * i : chunk * (i + 1)] for i in range(CHUNKS)]
+        pairs = [
+            lax.all_gather(
+                pair_rows[:, 2 * chunk * i : 2 * chunk * (i + 1)], "cp", axis=0, tiled=True
+            )
+            for i in range(CHUNKS)
+        ]
+        context_low = jnp.concatenate(
+            [attend(query, pair) for query, pair in zip(queries, pairs)], axis=1
+        )
     w_output = w_wide[:, :width]
     w_up = w_wide[:, width:]
-
-    context_low = jnp.concatenate(
-        [attend(query, pair) for query, pair in zip(queries, pairs)], axis=1
-    )
     attn_out = matmul(context_low, w_output) + b_output
     resid_first = local_tokens.astype(F32) + attn_out
     first_norm, pull_first = jax.vjp(normalize, resid_first, gain_one, shift_one)

time: 364 us -> 362 us (level)
  Pallas kernels: 258 us -> 279 us
  waiting for transfers between devices: 19.3 us -> 0 us
  between operations: 16.1 us -> 2.97 us
  matrix products: 31.9 us -> 43.2 us
    pallas_call x7 -> x4, Pallas kernels: 258 us -> 279 us  [the longest x2 142 us: reduce_many(): pl.pallas_call(functools.partial(reduce_kernel, units, count, reps, pairs...]
    all_gather x3 -> x0, waiting for transfers between devices: 18 us -> none  [on_device(): lax.all_gather(pair_rows[:, 2 * chunk * i:2 * chunk * (i + 1)], 'cp', axi...]
    dot_general x5, matrix products: 11.6 us -> 18.6 us  [matmul(): return jnp.dot(left, right, preferred_element_type=F32)]
    dot_general x4, matrix products: 8.56 us -> 12.5 us  [against(): lax.dot_general(left, right, (((1,), (1,)), ((), ())), preferred_element_...]
    unnamed x84 -> x74, local copies, waits for them, and re-layouts: 12.9 us -> 12.7 us
  transfers between devices with their start and end apart: 3 -> 0, of which waited for: 1 -> 0; matrix products, arithmetic and copies ran while one was open for 1% -> 0% of each run, Pallas kernels for 22% -> 0%
where the time goes in v2:
time: 362 us; the launch traced here: 361 us
  Pallas kernels  279 us (77%)
  matrix products  43.2 us (12%)
  local copies, waits for them, and re-layouts  26.5 us (7%)
  other arithmetic  8.8 us (2%)
    pallas_call x2, Pallas kernels, reduce_many(): pl.pallas_call(functools.partial(reduce_kernel, units, count, reps, pairs...  142 us
    pallas_call x2, Pallas kernels, gather_many(): pl.pallas_call(functools.partial(gather_kernel, units, count, reps, pairs...  138 us
    dot_general x5, matrix products, matmul(): return jnp.dot(left, right, preferred_element_type=F32)  18.6 us
    unnamed x74, local copies, waits for them, and re-layouts  12.7 us
    dot_general x4, matrix products, against(): lax.dot_general(left, right, (((1,), (1,)), ((), ())), preferred_element_...  12.5 us
    dot_general x4, matrix products, over_rows(): lax.dot_general(left, right, (((0,), (0,)), ((), ())), preferred_element_...  12.1 us

profile of v2, /device:TPU:0, one launch (start us, length us, event | category | flops | bytes accessed | tf_op | source)
XLA Modules:
  0.0 360.9 jit_solution(6345183042369594635)
XLA Ops:
  0.7 0.7 pad_bitcast_fusion.4
  1.3 0.7 pad_bitcast_fusion.6
  2.0 0.7 pad_bitcast_fusion.8
  2.7 0.7 pad_bitcast_fusion.2
  3.4 0.7 concatenate.30
  4.1 0.6 pad_bitcast_fusion.1.refs_1_
  4.7 1.0 constant_dynamic-update-slice_fusion.12
  5.7 0.8 constant_dynamic-update-slice_fusion.11
  6.4 0.7 constant_dynamic-update-slice_fusion.10
  7.2 0.7 constant_dynamic-update-slice_fusion.9
  7.9 0.7 constant_dynamic-update-slice_fusion.8
  8.7 0.7 constant_dynamic-update-slice_fusion.7
  9.4 0.7 constant_dynamic-update-slice_fusion.6
  10.2 0.7 constant_dynamic-update-slice_fusion.5
  10.9 0.7 constant_dynamic-update-slice_fusion.4
  11.7 0.7 constant_dynamic-update-slice_fusion.3
  12.4 0.7 constant_dynamic-update-slice_fusion.2
  13.2 0.7 constant_dynamic-update-slice_fusion.1
  13.9 0.7 constant_dynamic-update-slice_fusion
  14.7 0.8 copy-done.2
  15.4 30.4 %shard_map.304 = (bf16[2,2,2,4,24,2304]{5,4,3,2,1,0:T(8,128)(2,1)}, bf16[2,2,2,4,8,128]{5,4,3,2,1,0:T(8,128)(2,1)}) custom-call(bf16[4,24,2304]{2,1,0:T(8,128)(2,1)} %bitcast.120, bf16[4,8,128]{2,1,0:T(8,128)(2,1)} %pad_bitcast_fusion.1.refs_1_), custom_call_target="tpu_custom_call" | custom-call | tf_op jit(solution)/shard_map/pallas_call | solution.py:397
  45.9 1.0 fusion.32
  46.9 0.1 reshape.362
  47.1 3.5 fusion.8.refs_3_
  50.6 0.1 reshape.361
  50.7 2.5 fusion.17.refs_2_.refs_3_
  53.2 0.9 pad_maximum_fusion
  54.1 107.4 %shard_map.305 = (bf16[2,2,2,4,24,3840]{5,4,3,2,1,0:T(8,128)(2,1)}, bf16[2,2,2,4,96,768]{5,4,3,2,1,0:T(8,128)(2,1)}, bf16[256,768]{1,0:T(8,128)(2,1)}, bf16[6,2,2,2,256,256]{5,4,3,2,1,0:T(8,128)(2,1)}) custom-call(bf16[4,24,3840]{2,1,0:T(8,128)(2,1)} %bitcast.119, bf16[4,96,768]{2,1,0:T(8,128)(2,1)} %bitcast.121, bf16[256,768]{1,0:T(8,128)(2,1)} %fusion.17.refs_2_.refs_3_, ...), custom_call_target="tpu_custom_call" | custom-call | tf_op jit(solution)/shard_map/pallas_call | solution.py:397
  161.6 2.0 fusion.34
  163.6 0.2 multiply_reduce_fusion.5
  164.0 0.7 slice_convert_fusion
  164.8 6.3 %multiply_convert_fusion = (bf16[256,3072]{1,0:T(8,128)(2,1)}, f32[256,3072]{1,0:T(8,128)}) fusion(f32[3072]{0:T(1024)S(1)} %reshape.366, bf16[768,3840]{1,0:T(8,128)(2,1)} %bitcast.138, f32[256,768]{1,0:T(8,128)S(1)} %get-tuple-element.89, f32[768]{0:T(1024)S(1)} %reshape.365, f32[768]{0:T(1024)S(1)} %reshape.364, f32[256]{0:T(256)S(1)} %fusion.26, ...), kind=kOutput, calls=%fused_computation.10 | convolution fusion | flops 1213661184 | bytes 10244096 | tf_op jit(solution)/shard_map/dot_general | solution.py:31
  171.1 4.4 %fusion.35 = (f32[256]{0:T(256)S(1)}, f32[256,768]{1,0:T(8,128)S(1)}) fusion(f32[768]{0:T(1024)S(1)} %reshape.367, bf16[256,3072]{1,0:T(8,128)(2,1)} %get-tuple-element.90, bf16[3072,768]{1,0:T(8,128)(2,1)} %bitcast.143, f32[768]{0:T(1024)S(1)} %reshape.365, f32[768]{0:T(1024)S(1)} %reshape.364, f32[256]{0:T(256)S(1)} %fusion.26, ...), kind=kOutput, calls=%fused_computation.145 | convolution fusion | flops 1209335552 | bytes 7876608 | tf_op jit(solution)/shard_map/dot_general | solution.py:31
  175.5 0.2 multiply_reduce_fusion.4
  175.8 0.3 fusion.21
  176.2 1.2 fusion.31
  177.5 0.1 convert_reduce_fusion.2
  177.6 0.8 copy-done.12
  178.4 4.9 %convert_reduce_fusion = (f32[3072]{0:T(1024)S(1)}, bf16[256,3072]{1,0:T(8,128)(2,1)S(1)}) fusion(f32[256,3072]{1,0:T(8,128)S(1)} %copy-done.12, bf16[256,768]{1,0:T(8,128)(2,1)S(1)} %get-tuple-element.50, bf16[3072,768]{1,0:T(8,128)(2,1)} %bitcast.144), kind=kOutput, calls=%fused_computation.8 | convolution fusion | flops 1219752960 | bytes 9842688 | tf_op jit(solution)/shard_map/dot_general | solution.py:39
  183.4 1.7 multiply_reduce_fusion.1
  185.1 0.3 fusion.30
  185.4 0.1 convert_reduce_fusion.3
  185.6 1.3 convolution_convert_fusion.4.refs_4_
  186.8 1.5 convolution_convert_fusion.3
  188.4 3.8 %convolution_convert_fusion.1 = bf16[768,3072]{1,0:T(8,128)(2,1)} fusion(bf16[256,3072]{1,0:T(8,128)(2,1)S(1)} %get-tuple-element.52, f32[256,768]{1,0:T(8,128)S(1)} %get-tuple-element.89, f32[768]{0:T(1024)S(1)} %reshape.365, f32[768]{0:T(1024)S(1)} %reshape.364, f32[256]{0:T(256)S(1)} %fusion.26, f32[256]{0:T(256)S(1)} %broadcast_multiply_fusion.1), kind=kOutput, calls=%fused_computation.1 | convolution fusion | flops 1211301888 | bytes 7086080 | tf_op jit(solution)/shard_map/dot_general | solution.py:35
  192.2 3.9 %convolution_convert_fusion.2 = bf16[3072,768]{1,0:T(8,128)(2,1)} fusion(bf16[256,3072]{1,0:T(8,128)(2,1)S(1)} %copy-done.1, bf16[256,768]{1,0:T(8,128)(2,1)S(1)} %get-tuple-element.50), kind=kOutput, calls=%fused_computation.2 | convolution fusion | flops 1210318848 | bytes 6684672 | tf_op jit(solution)/shard_map/dot_general | solution.py:35
  196.1 99.3 %shard_map.306 = (bf16[4,96,768]{2,1,0:T(8,128)(2,1)}, bf16[4,24,3072]{2,1,0:T(8,128)(2,1)}, bf16[4,24,768]{2,1,0:T(8,128)(2,1)}, bf16[256,768]{1,0:T(8,128)(2,1)}, bf16[256,1536]{1,0:T(8,128)(2,1)}) custom-call(bf16[2,2,2,4,96,768]{5,4,3,2,1,0:T(8,128)(2,1)} %bitcast.114, bf16[2,2,2,4,24,3072]{5,4,3,2,1,0:T(8,128)(2,1)} %bitcast.115, ...), custom_call_target="tpu_custom_call" | custom-call | tf_op jit(solution)/shard_map/pallas_call | solution.py:666
  295.4 1.0 constant_dynamic-update-slice_fusion.26
  296.5 1.2 constant_dynamic-update-slice_fusion.25
  297.6 0.2 convert_reduce_fusion.1
  298.0 4.6 %multiply_reduce_fusion = (f32[]{:T(128)}, f32[256,768]{1,0:T(8,128)}) fusion(bf16[256,2304]{1,0:T(8,128)(2,1)S(1)} %constant_dynamic-update-slice_fusion.25, bf16[768,2304]{1,0:T(8,128)(2,1)} %bitcast.147, f32[256,768]{1,0:T(8,128)S(1)} %get-tuple-element.56, f32[256]{0:T(256)S(1)} %negate_multiply_fusion), kind=kOutput, calls=%fused_computation.37 | convolution fusion | flops 906756096 | bytes 6292484 | tf_op jit(solution)/shard_map/dot_general | solution.py:39
  302.6 0.6 broadcast_in_dim.44
  303.9 0.1 concatenate.34
  304.0 0.7 copy.57
  304.7 2.9 convolution_convert_fusion
  307.6 42.3 %shard_map.307 = (bf16[4,24,2304]{2,1,0:T(8,128)(2,1)}, f32[4,8,128]{2,1,0:T(8,128)}) custom-call(bf16[2,2,2,4,24,2304]{5,4,3,2,1,0:T(8,128)(2,1)} %bitcast.116, f32[2,2,2,4,8,128]{5,4,3,2,1,0:T(8,128)} %bitcast.122), custom_call_target="tpu_custom_call" | custom-call | tf_op jit(solution)/shard_map/pallas_call | solution.py:666
  349.9 1.1 bitcast_convert_fusion.2
  351.1 0.8 slice.328
  352.0 1.5 fusion.33
  353.5 1.3 slice.346
  354.8 1.2 slice.350
  356.7 1.1 bitcast_convert_fusion
  357.8 1.2 bitcast_convert_fusion.1
  359.0 0.7 bitcast_convert_fusion.3
  (100 shorter events, 1.6 us)
Async XLA Ops:
  4.7 46.0 %copy-start.6 = (bf16[1,256,768]{2,1,0:T(8,128)(2,1)S(1)}, bf16[1,256,768]{2,1,0:T(8,128)(2,1)}, u32[]{:S(2)}) copy-start(bf16[1,256,768]{2,1,0:T(8,128)(2,1)} %param.17) | copy-start | bytes 1179652
  14.7 0.8 copy-start.2
  47.1 6.1 %copy-start.5 = (bf16[96,3072]{1,0:T(8,128)(2,1)S(1)}, bf16[96,3072]{1,0:T(8,128)(2,1)}, u32[]{:S(2)}) copy-start(bf16[96,3072]{1,0:T(8,128)(2,1)} %param.27) | copy-start | bytes 1769476
  47.1 6.1 %copy-start.8 = (bf16[96,768]{1,0:T(8,128)(2,1)S(1)}, bf16[96,768]{1,0:T(8,128)(2,1)}, u32[]{:S(2)}) copy-start(bf16[96,768]{1,0:T(8,128)(2,1)} %param.23) | copy-start | bytes 442372
  171.1 4.7 %copy-start = (f32[1,256,768]{2,1,0:T(8,128)S(1)}, f32[1,256,768]{2,1,0:T(8,128)}, u32[]{:S(2)}) copy-start(f32[1,256,768]{2,1,0:T(8,128)} %param.33) | copy-start | bytes 2359300
  176.2 2.2 copy-start.12
  177.5 5.9 %slice-start = ((s8[5898240]{0:T(1024)(128)(4,1)}), s8[4194304]{0:T(1024)(128)(4,1)S(1)}, s32[]{:S(2)}) async-start(s8[5898240]{0:T(1024)(128)(4,1)} %bitcast.139), calls=%async_computation | async-start | bytes 8388608
  178.4 4.9 %slice-start.1 = ((s8[5898240]{0:T(1024)(128)(4,1)}), s8[1703936]{0:T(1024)(128)(4,1)S(1)}, s32[]{:S(2)}) async-start(s8[5898240]{0:T(1024)(128)(4,1)} %bitcast.139), calls=%async_computation.1 | async-start | bytes 3407872
  185.1 1.8 copy-start.7
  188.4 3.8 %copy-start.1 = (bf16[256,3072]{1,0:T(8,128)(2,1)S(1)}, bf16[256,3072]{1,0:T(8,128)(2,1)}, u32[]{:S(2)}) copy-start(bf16[256,3072]{1,0:T(8,128)(2,1)} %get-tuple-element.90) | copy-start | bytes 4718596
  307.6 49.1 %copy-start.4 = (bf16[4,96,768]{2,1,0:T(8,128)(2,1)S(1)}, bf16[4,96,768]{2,1,0:T(8,128)(2,1)}, u32[]{:S(2)}) copy-start(bf16[4,96,768]{2,1,0:T(8,128)(2,1)} %get-tuple-element.43) | copy-start | bytes 1769476
  349.8 8.0 %copy-start.3 = (bf16[4,24,3072]{2,1,0:T(8,128)(2,1)S(1)}, bf16[4,24,3072]{2,1,0:T(8,128)(2,1)}, u32[]{:S(2)}) copy-start(bf16[4,24,3072]{2,1,0:T(8,128)(2,1)} %get-tuple-element.42) | copy-start | bytes 1769476
  349.9 9.1 %copy-start.9 = (bf16[4,24,768]{2,1,0:T(8,128)(2,1)S(1)}, bf16[4,24,768]{2,1,0:T(8,128)(2,1)}, u32[]{:S(2)}) copy-start(bf16[4,24,768]{2,1,0:T(8,128)(2,1)} %get-tuple-element.41) | copy-start | bytes 442372
  351.1 8.6 %copy-start.10 = (f32[96,768]{1,0:T(8,128)}, f32[96,768]{1,0:T(8,128)S(1)}, u32[]{:S(2)}) copy-start(f32[96,768]{1,0:T(8,128)S(1)} %get-tuple-element.59) | copy-start | bytes 884740
  351.1 8.6 %copy-start.11 = (f32[96,768]{1,0:T(8,128)}, f32[96,768]{1,0:T(8,128)S(1)}, u32[]{:S(2)}) copy-start(f32[96,768]{1,0:T(8,128)S(1)} %get-tuple-element.60) | copy-start | bytes 884740

commit v3 on v2

--- a/solution.py
+++ b/solution.py
@@ -11,6 +11,7 @@
 HD = 64
 PAIR = 2 * HD
 CHUNKS = 3
+AHEAD = 2
 EPSILON = 1e-12
 BF16 = jnp.bfloat16
 F32 = jnp.float32
@@ -197,8 +198,8 @@
     ins = refs[:count]
     at = count
     if pairs:
-        query_ref, rows_ref = refs[at : at + 2]
-        at += 2
+        query_ref, key_ref, value_ref = refs[at : at + 3]
+        at += 3
     outs = refs[at : at + count]
     at += count
     if pairs:
@@ -240,12 +241,13 @@
 
     if pairs:
         sends_k, recvs_k, sends_s, recvs_s = refs[at + 7 :]
-        for p in range(pairs):
-            pair_ref[p, high, low, core] = rows_ref[:, 2 * PAIR * p : 2 * PAIR * (p + 1)]
-            own = held(p, 0, core)
-            send(own, own, sends_k, recvs_k, 3 * p + 1, far)
-            send(own, own, sends_k, recvs_k, 3 * p, near)
-            send(own, own, sends_s, recvs_s, 4 * p, sibling)
+
+    def offer(p):
+        own = held(p, 0, core)
+        send(own, own, sends_k, recvs_k, 3 * p + 1, far)
+        send(own, own, sends_k, recvs_k, 3 * p, near)
+        send(own, own, sends_s, recvs_s, 4 * p, sibling)
+
     for u, (at, start, size) in enumerate(units):
         block = ins[at].at[rep, :, pl.ds(start, size)]
         send(block, block_of(u, 0, core, rep), sends_z, recvs_z, 3 * u + 1, far)
@@ -258,6 +260,13 @@
         copy.start()
         copies.append(copy)
 
+    for p in range(pairs):
+        cols = pl.ds(PAIR * p, PAIR)
+        pair_ref[p, high, low, core, :, :PAIR] = key_ref[:, cols]
+        pair_ref[p, high, low, core, :, PAIR:] = value_ref[:, cols]
+        if p < AHEAD:
+            offer(p)
+
     def spread(u, which):
         block = block_of(u, which, core, rep)
         arrived(block, sends_z, recvs_z, 3 * u + which - 1)
@@ -317,6 +326,10 @@
             def _():
                 take(t, 1)
                 take(t, 2)
+
+            @pl.when(t < pairs - AHEAD)
+            def _():
+                offer(t + AHEAD)
 
             @pl.when((t >= 1) & (t < pairs + 1))
             def _():
@@ -366,7 +379,7 @@
     return [(size * i, size) for i in range(pieces)]
 
 
-def gather_many(shards, pieces, identity, query=None, rows=None):
+def gather_many(shards, pieces, identity, query=None, keys=None, values=None):
     reps = lax.axis_size("rep")
     count = len(shards)
     units = [
@@ -387,18 +400,18 @@
     pairs = 0
     if query is not None:
         pairs = query.shape[1] // PAIR
-        operands += [query, rows]
-        spaces = [vmem] * 2
+        operands += [query, keys, values]
+        spaces = [vmem] * 3
         out_shape += [
             jax.ShapeDtypeStruct(query.shape, BF16),
-            jax.ShapeDtypeStruct((pairs, 2, 2, 2, rows.shape[0], 2 * PAIR), BF16),
+            jax.ShapeDtypeStruct((pairs, 2, 2, 2, keys.shape[0], 2 * PAIR), BF16),
         ]
         more = [dma((3 * pairs,))] * 2 + [dma((4 * pairs,))] * 2
     return pl.pallas_call(
         functools.partial(gather_kernel, units, count, reps, pairs),
         out_shape=out_shape,
         in_specs=[pl.BlockSpec(memory_space=pl.ANY)] * count + spaces,
-        out_specs=[pl.BlockSpec(memory_space=pl.ANY)] * count + spaces,
+        out_specs=[pl.BlockSpec(memory_space=pl.ANY)] * count + spaces[:2],
         scratch_shapes=[dma((3 * total,))] * 2
         + [dma((hops,))] * 2
         + [dma((4 * total,))] * 2
@@ -426,8 +439,8 @@
     outs = refs[at : at + count]
     at += count
     if fused:
-        grad_query_ref, grad_pair_ref = refs[at : at + 2]
-        at += 2
+        grad_query_ref, grad_key_ref, grad_value_ref = refs[at : at + 3]
+        at += 3
     size = len(units)
     first, second, third, fourth, own = [
         refs[at + i * size : at + (i + 1) * size] for i in range(5)
@@ -514,8 +527,9 @@
 
     steps = size + len(stages) - 1
     if not fused:
-        for step in range(steps):
-            advance(step)
+        for stage in stages:
+            for u in range(size):
+                stage(u)
     else:
         terms, merged, from_near, from_far, held, sends_k, recvs_k, fetched = sems[8:]
         pairs = terms.shape[0]
@@ -552,8 +566,10 @@
 
         def merge_far(p):
             arrived(from_far.at[p], sends_k, recvs_k, 3 * p + 2)
-            cols = pl.ds(pl.multiple_of(p * 2 * PAIR, 2 * PAIR), 2 * PAIR)
-            grad_pair_ref[:, cols] = summed([merged[p, high, low], from_far[p]], BF16)
+            cols = pl.ds(pl.multiple_of(p * PAIR, PAIR), PAIR)
+            both = summed([merged[p, high, low], from_far[p]], BF16)
+            grad_key_ref[:, cols] = both[:, :PAIR]
+            grad_value_ref[:, cols] = both[:, PAIR:]
 
         def compute(p):
             fetch(p).wait()
@@ -649,10 +665,7 @@
         block = (tokens, 2 * PAIR)
         operands += [query, grad, pairs]
         in_specs += [vmem] * 2 + [pl.BlockSpec(memory_space=pl.ANY)]
-        out_shape += [
-            jax.ShapeDtypeStruct((tokens, width), BF16),
-            jax.ShapeDtypeStruct((tokens, 2 * width), BF16),
-        ]
+        out_shape += [jax.ShapeDtypeStruct((tokens, width), BF16)] * 3
         more = [
             pltpu.VMEM((number, 2, 2, 2) + block, BF16),
             pltpu.VMEM((number, 2, 2) + block, BF16),
@@ -719,7 +732,6 @@
     local_tokens = tokens[0]
     fast = divides(query_weight.shape[0])
     reps = lax.axis_size("rep")
-    proj_shard = jnp.concatenate([query_weight, mixed(key_weight, value_weight)], axis=1)
     small = (
         query_bias,
         value_bias,
@@ -740,13 +752,16 @@
             )
         packed = jnp.concatenate(rows, axis=0)
         packed = jnp.pad(packed, ((0, -packed.shape[0] % (8 * reps)), (0, 0))).astype(BF16)
-        w_proj, gathered = gather_many(
-            (blocked(proj_shard), blocked(packed)), (3, 1), 1
+        shards = (key_weight, value_weight, query_weight, packed)
+        w_key, w_value, w_query, gathered = gather_many(
+            [blocked(shard) for shard in shards], (1, 1, 1, 1), 1
         )
-        w_proj = w_proj.reshape(-1, proj_shard.shape[1])
+        w_key, w_value, w_query = [w.reshape(-1, width) for w in (w_key, w_value, w_query)]
         gathered = gathered.reshape(-1, packed.shape[0], 128)
     else:
-        w_proj = gather_all(proj_shard)
+        w_query, w_key, w_value = [
+            gather_all(shard) for shard in (query_weight, key_weight, value_weight)
+        ]
         gathered = lax.all_gather(jnp.concatenate(small)[None], "cp", axis=0, tiled=True)
     vectors = []
     at = 0
@@ -761,23 +776,29 @@
             at += size
         vectors.append(part.reshape(-1).astype(F32))
     b_query, b_value, b_output, gain_one, shift_one, b_up, b_down, gain_two, shift_two = vectors
-    w_pair = w_proj[:, width:]
-    pair_bias = mixed(jnp.zeros_like(b_value)[None], b_value[None])
-    pair_rows = (matmul(local_tokens, w_pair) + pair_bias).astype(BF16)
+    key_rows = matmul(local_tokens, w_key).astype(BF16)
+    value_rows = (matmul(local_tokens, w_value) + b_value).astype(BF16)
     chunk = width // CHUNKS
-    query_rows = (matmul(local_tokens, w_proj[:, :width]) + b_query).astype(BF16)
+    query_rows = (matmul(local_tokens, w_query) + b_query).astype(BF16)
     query_scaled = query_rows * jnp.asarray(1.0 / math.sqrt(HD), BF16)
-    wide_shard = jnp.concatenate([output_weight, up_weight], axis=1)
     if fast:
-        w_wide, w_down, context_low, pairs = gather_many(
-            (blocked(wide_shard), blocked(down_weight)), (2, 2), 2, query_scaled, pair_rows
+        shards = (output_weight, up_weight, down_weight)
+        w_output, w_up, w_down, context_low, pairs = gather_many(
+            [blocked(shard) for shard in shards],
+            (1, 2, 2),
+            2,
+            query_scaled,
+            key_rows,
+            value_rows,
         )
-        w_wide = w_wide.reshape(-1, wide_shard.shape[1])
-        w_down = w_down.reshape(-1, width)
+        w_output, w_down = w_output.reshape(-1, width), w_down.reshape(-1, width)
+        w_up = w_up.reshape(-1, up_weight.shape[1])
         pairs = pairs.reshape(pairs.shape[0], -1, 2 * PAIR)
     else:
-        w_wide = gather_all(wide_shard)
-        w_down = gather_all(down_weight)
+        w_output, w_up, w_down = [
+            gather_all(shard) for shard in (output_weight, up_weight, down_weight)
+        ]
+        pair_rows = mixed(key_rows, value_rows)
         queries = [query_scaled[:, chunk * i : chunk * (i + 1)] for i in range(CHUNKS)]
         pairs = [
             lax.all_gather(
@@ -788,8 +809,6 @@
         context_low = jnp.concatenate(
             [attend(query, pair) for query, pair in zip(queries, pairs)], axis=1
         )
-    w_output = w_wide[:, :width]
-    w_up = w_wide[:, width:]
     attn_out = matmul(context_low, w_output) + b_output
     resid_first = local_tokens.astype(F32) + attn_out
     first_norm, pull_first = jax.vjp(normalize, resid_first, gain_one, shift_one)
@@ -815,7 +834,14 @@
     grad_context = against(grad_attn, w_output).astype(BF16)
 
     if fast:
-        full_down, full_up, full_output, grad_query_low, grad_pair_low = reduce_many(
+        (
+            full_down,
+            full_up,
+            full_output,
+            grad_query_low,
+            grad_key_low,
+            grad_value_low,
+        ) = reduce_many(
             [split_rows(part) for part in (part_down, part_up, part_output)],
             (2, 2, 1),
             3,
@@ -835,16 +861,20 @@
                 lax.psum_scatter(grad_terms, "cp", scatter_dimension=0, tiled=True)
             )
         grad_query_low = jnp.concatenate(grad_queries, axis=1)
-        grad_pair_low = jnp.concatenate(grad_pairs, axis=1)
-    grad_proj = jnp.concatenate([grad_query_low, grad_pair_low], axis=1)
-    part_proj = over_rows(local_tokens, grad_proj).astype(BF16)
-    grad_tokens = grad_resid1 + against(grad_proj, w_proj)
-    proj_sums = column_sum(grad_proj)
-    _, grad_value_bias = unmixed(proj_sums[None, width:])
+        grad_key_low, grad_value_low = unmixed(jnp.concatenate(grad_pairs, axis=1))
+    part_query = over_rows(local_tokens, grad_query_low).astype(BF16)
+    part_key = over_rows(local_tokens, grad_key_low).astype(BF16)
+    part_value = over_rows(local_tokens, grad_value_low).astype(BF16)
+    grad_tokens = (
+        grad_resid1
+        + against(grad_query_low, w_query)
+        + against(grad_key_low, w_key)
+        + against(grad_value_low, w_value)
+    )
 
     small_grads = (
-        proj_sums[:width],
-        grad_value_bias[0],
+        column_sum(grad_query_low),
+        column_sum(grad_value_low),
         grad_output_bias,
         grad_gain1,
         grad_shift1,
@@ -860,16 +890,15 @@
     )
     if fast:
         flat = jnp.pad(flat, ((0, 0), (0, -flat.shape[1] % (8 * 128 * reps))))
-        full_proj, sums = reduce_many(
-            (split_rows(part_proj), flat.reshape(2, 2, 2, reps, -1, 128)), (3, 1), 4
+        blocks = [split_rows(part) for part in (part_query, part_key, part_value)]
+        full_query, full_key, full_value, sums = reduce_many(
+            blocks + [flat.reshape(2, 2, 2, reps, -1, 128)], (1, 1, 1, 1), 4
         )
         sums = sums.reshape(-1)
     else:
-        shards = [
-            scatter_all(part)
-            for part in (part_down, part_up, part_output, part_proj)
-        ]
-        full_down, full_up, full_output, full_proj = [
+        parts = (part_down, part_up, part_output, part_query, part_key, part_value)
+        shards = [scatter_all(part) for part in parts]
+        full_down, full_up, full_output, full_query, full_key, full_value = [
             part.astype(F32) for part in lax.psum(tuple(shards), "rep")
         ]
         sums = lax.psum(flat, ("rep", "cp"))
@@ -882,14 +911,13 @@
     entries = lax.axis_size("rep") * owners * row_count * width
     rms_values = jnp.sqrt(sums[at : at + 1] / entries)
 
-    grad_key_weight, grad_value_weight = unmixed(full_proj[:, width:])
     return (
         layer_out[None],
         grad_tokens[None],
-        full_proj[:, :width],
+        full_query,
         reduced[0],
-        grad_key_weight,
-        grad_value_weight,
+        full_key,
+        full_value,
         reduced[1],
         full_output,
         reduced[2],

time: 362 us -> 339 us (0.936)
  Pallas kernels: 279 us -> 266 us
  local copies, waits for them, and re-layouts: 26.5 us -> 14.2 us
    pallas_call x2, Pallas kernels: 138 us -> 122 us  [gather_many(): pl.pallas_call(functools.partial(gather_kernel, units, count, reps, pairs...]
    unnamed x74 -> x46, local copies, waits for them, and re-layouts: 12.7 us -> 3.12 us
    convert_element_type x4 -> x6, other arithmetic: 4.16 us -> 8.02 us  [reduce_many(): total.reshape(-1, total.shape[2]).astype(F32)]
    dot_general x4 -> x6, matrix products: 12.1 us -> 13.6 us  [over_rows(): lax.dot_general(left, right, (((0,), (0,)), ((), ())), preferred_element_...]
    dot_general x5 -> x6, matrix products: 18.6 us -> 17.5 us  [matmul(): return jnp.dot(left, right, preferred_element_type=F32)]
    dot_general x4 -> x6, matrix products: 12.5 us -> 12.5 us  [against(): lax.dot_general(left, right, (((1,), (1,)), ((), ())), preferred_element_...]
where the time goes in v3:
time: 339 us; the launch traced here: 338 us
  Pallas kernels  266 us (78%)
  matrix products  43.6 us (13%)
  local copies, waits for them, and re-layouts  14.2 us (4%)
  other arithmetic  11.7 us (3%)
    pallas_call x2, Pallas kernels, reduce_many(): pl.pallas_call(functools.partial(reduce_kernel, units, count, reps, pairs...  144 us
    pallas_call x2, Pallas kernels, gather_many(): pl.pallas_call(functools.partial(gather_kernel, units, count, reps, pairs...  122 us
    dot_general x6, matrix products, matmul(): return jnp.dot(left, right, preferred_element_type=F32)  17.5 us
    dot_general x6, matrix products, over_rows(): lax.dot_general(left, right, (((0,), (0,)), ((), ())), preferred_element_...  13.6 us
    dot_general x6, matrix products, against(): lax.dot_general(left, right, (((1,), (1,)), ((), ())), preferred_element_...  12.5 us
    convert_element_type x6, other arithmetic, reduce_many(): total.reshape(-1, total.shape[2]).astype(F32)  8.02 us

profile of v3, /device:TPU:0, one launch (start us, length us, event | category | flops | bytes accessed | tf_op | source)
XLA Modules:
  0.0 338.3 jit_solution(155905691983705076)
XLA Ops:
  0.7 0.7 pad_bitcast_fusion.4
  1.4 0.7 pad_bitcast_fusion.6
  2.1 0.7 pad_bitcast_fusion.8
  2.7 0.7 pad_bitcast_fusion.2
  3.4 0.7 concatenate.7
  4.2 0.6 pad_bitcast_fusion.1.refs_3_
  4.8 30.1 %shard_map.304 = (bf16[2,2,2,4,24,768]{5,4,3,2,1,0:T(8,128)(2,1)}, bf16[2,2,2,4,24,768]{5,4,3,2,1,0:T(8,128)(2,1)}, bf16[2,2,2,4,24,768]{5,4,3,2,1,0:T(8,128)(2,1)}, bf16[2,2,2,4,8,128]{5,4,3,2,1,0:T(8,128)(2,1)}) custom-call(bf16[4,24,768]{2,1,0:T(8,128)(2,1)} %bitcast.173, bf16[4,24,768]{2,1,0:T(8,128)(2,1)} %bitcast.174, bf16[4,24,768]{2,1,0:T(8,128)(2,1)} %bitcast.175, ...), custom_call_target="tpu_custom_call" | custom-call | tf_op jit(solution)/shard_map/pallas_call | solution.py:410
  34.9 1.0 fusion.22
  36.0 0.1 reshape.390
  36.0 2.6 fusion.7.refs_3_
  38.7 0.1 reshape.391
  38.8 1.2 fusion.5.refs_5_
  40.0 1.2 fusion.4.refs_4_
  41.2 92.0 %shard_map.305 = (bf16[2,2,2,4,24,768]{5,4,3,2,1,0:T(8,128)(2,1)}, bf16[2,2,2,4,24,3072]{5,4,3,2,1,0:T(8,128)(2,1)}, bf16[2,2,2,4,96,768]{5,4,3,2,1,0:T(8,128)(2...) custom-call(bf16[4,24,768]{2,1,0:T(8,128)(2,1)} %bitcast.172, bf16[4,24,3072]{2,1,0:T(8,128)(2,1)} %bitcast.169, ...), custom_call_target="tpu_custom_call" | custom-call | tf_op jit(solution)/shard_map/pallas_call | solution.py:410
  133.2 0.1 reshape.392
  133.3 2.0 fusion.24
  135.3 0.2 multiply_reduce_fusion.5
  135.6 0.1 reshape.394
  135.7 0.7 slice_convert_fusion
  136.4 6.1 %multiply_convert_fusion = (bf16[256,3072]{1,0:T(8,128)(2,1)}, f32[256,3072]{1,0:T(8,128)}) fusion(f32[3072]{0:T(1024)S(1)} %reshape.395, bf16[768,3072]{1,0:T(8,128)(2,1)} %bitcast.190, f32[256,768]{1,0:T(8,128)S(1)} %get-tuple-element.89, f32[768]{0:T(1024)S(1)} %reshape.394, f32[768]{0:T(1024)S(1)} %reshape.393, f32[256]{0:T(256)S(1)} %fusion.16, ...), kind=kOutput, calls=%fused_computation.5 | convolution fusion | flops 1213661184 | bytes 10244096 | tf_op jit(solution)/shard_map/dot_general | solution.py:32
  142.5 0.1 reshape.396
  142.6 4.4 %fusion.25 = (f32[256]{0:T(256)S(1)}, f32[256,768]{1,0:T(8,128)S(1)}) fusion(f32[768]{0:T(1024)S(1)} %reshape.396, bf16[256,3072]{1,0:T(8,128)(2,1)} %get-tuple-element.90, bf16[3072,768]{1,0:T(8,128)(2,1)} %bitcast.194, f32[768]{0:T(1024)S(1)} %reshape.394, f32[768]{0:T(1024)S(1)} %reshape.393, f32[256]{0:T(256)S(1)} %fusion.16, ...), kind=kOutput, calls=%fused_computation.103 | convolution fusion | flops 1209335552 | bytes 7876608 | tf_op jit(solution)/shard_map/dot_general | solution.py:32
  147.0 0.2 multiply_reduce_fusion.4
  147.2 0.1 reshape.397
  147.3 0.3 fusion.8
  147.7 0.1 reshape.398
  147.8 1.2 fusion.21
  149.0 0.1 convert_reduce_fusion.1
  149.2 0.8 copy-done.15
  150.0 4.9 %convert_reduce_fusion = (f32[3072]{0:T(1024)S(1)}, bf16[256,3072]{1,0:T(8,128)(2,1)S(1)}) fusion(f32[256,3072]{1,0:T(8,128)S(1)} %copy-done.15, bf16[256,768]{1,0:T(8,128)(2,1)S(1)} %get-tuple-element.62, bf16[3072,768]{1,0:T(8,128)(2,1)} %bitcast.195), kind=kOutput, calls=%fused_computation.3 | convolution fusion | flops 1219752960 | bytes 9842688 | tf_op jit(solution)/shard_map/dot_general | solution.py:40
  154.9 1.9 multiply_reduce_fusion.1
  156.8 0.3 fusion.20
  157.2 0.1 convert_reduce_fusion.2
  157.3 0.7 copy-done.4
  158.0 1.2 convolution_convert_fusion.7.refs_4_
  159.3 1.5 convolution_convert_fusion.5
  160.8 3.8 %convolution_convert_fusion = bf16[768,3072]{1,0:T(8,128)(2,1)} fusion(bf16[256,3072]{1,0:T(8,128)(2,1)S(1)} %get-tuple-element.64, f32[256,768]{1,0:T(8,128)S(1)} %get-tuple-element.89, f32[768]{0:T(1024)S(1)} %reshape.394, f32[768]{0:T(1024)S(1)} %reshape.393, f32[256]{0:T(256)S(1)} %fusion.16, f32[256]{0:T(256)S(1)} %broadcast_multiply_fusion.1), kind=kOutput, calls=%fused_computation | convolution fusion | flops 1211301888 | bytes 7086080 | tf_op jit(solution)/shard_map/dot_general | solution.py:36
  164.6 3.7 %convolution_convert_fusion.1 = bf16[3072,768]{1,0:T(8,128)(2,1)} fusion(bf16[256,3072]{1,0:T(8,128)(2,1)S(1)} %copy-done.5, bf16[256,768]{1,0:T(8,128)(2,1)S(1)} %get-tuple-element.62), kind=kOutput, calls=%fused_computation.1 | convolution fusion | flops 1210318848 | bytes 6684672 | tf_op jit(solution)/shard_map/dot_general | solution.py:36
  168.3 103.3 %shard_map.306 = (bf16[4,96,768]{2,1,0:T(8,128)(2,1)}, bf16[4,24,3072]{2,1,0:T(8,128)(2,1)}, bf16[4,24,768]{2,1,0:T(8,128)(2,1)}, bf16[256,768]{1,0:T(8,128)(2,1...) custom-call(bf16[2,2,2,4,96,768]{5,4,3,2,1,0:T(8,128)(2,1)} %bitcast.153, ...), custom_call_target="tpu_custom_call" | custom-call | tf_op jit(solution)/shard_map/pallas_call | solution.py:679
  271.7 2.0 convolution_add_fusion.5
  273.7 0.5 convolution_add_fusion.4
  274.2 0.4 copy-done.6
  274.7 0.4 copy-done.11
  275.1 2.0 multiply_reduce_fusion
  277.1 0.6 broadcast_in_dim.40
  277.7 0.1 convert_reduce_fusion.4
  277.9 0.1 convert_reduce_fusion.3
  278.0 0.1 reshape.381
  278.3 0.1 reshape.386
  278.5 0.1 concatenate.8
  278.7 0.7 copy.60
  279.3 1.5 convolution_convert_fusion.4
  280.9 1.5 convolution_convert_fusion.3
  282.4 1.5 convolution_convert_fusion.2
  283.9 40.4 %shard_map.307 = (bf16[4,24,768]{2,1,0:T(8,128)(2,1)}, bf16[4,24,768]{2,1,0:T(8,128)(2,1)}, bf16[4,24,768]{2,1,0:T(8,128)(2,1)}, f32[4,8,128]{2,1,0:T(8,128)}) custom-call(bf16[2,2,2,4,24,768]{5,4,3,2,1,0:T(8,128)(2,1)} %bitcast.159, bf16[2,2,2,4,24,768]{5,4,3,2,1,0:T(8,128)(2,1)} %bitcast.160, bf16[2,2,2,4,24,768]{5,4,3,2,1,0:T(8,128)(2,1)} %bitcast.161, ...), custom_call_target="tpu_custom_call" | custom-call | tf_op jit(solution)/shard_map/pallas_call | solution.py:679
  324.4 1.7 bitcast_convert_fusion.3
  326.1 1.6 bitcast_convert_fusion.4
  327.7 1.6 bitcast_convert_fusion.5
  329.4 1.5 fusion.23
  330.9 1.3 slice.122
  332.3 1.2 slice.126
  334.2 1.1 bitcast_convert_fusion
  335.3 1.2 bitcast_convert_fusion.1
  336.4 0.7 bitcast_convert_fusion.2
  (68 shorter events, 0.8 us)
Async XLA Ops:
  0.7 38.1 %copy-start = (bf16[1,256,768]{2,1,0:T(8,128)(2,1)S(1)}, bf16[1,256,768]{2,1,0:T(8,128)(2,1)}, u32[]{:S(2)}) copy-start(bf16[1,256,768]{2,1,0:T(8,128)(2,1)} %param.17) | copy-start | bytes 1179652
  34.9 3.8 %copy-start.10 = (bf16[2,2,2,4,24,768]{5,4,3,2,1,0:T(8,128)(2,1)S(1)}, bf16[2,2,2,4,24,768]{5,4,3,2,1,0:T(8,128)(2,1)}, u32[]{:S(2)}) copy-start(bf16[2,2,2,4,24,768]{5,4,3,2,1,0:T(8,128)(2,1)} %get-tuple-element.40) | copy-start | bytes 3538948
  34.9 5.1 %copy-start.2 = (bf16[2,2,2,4,24,768]{5,4,3,2,1,0:T(8,128)(2,1)S(1)}, bf16[2,2,2,4,24,768]{5,4,3,2,1,0:T(8,128)(2,1)}, u32[]{:S(2)}) copy-start(bf16[2,2,2,4,24,768]{5,4,3,2,1,0:T(8,128)(2,1)} %get-tuple-element.39) | copy-start | bytes 3538948
  142.6 4.7 %copy-start.1 = (f32[1,256,768]{2,1,0:T(8,128)S(1)}, f32[1,256,768]{2,1,0:T(8,128)}, u32[]{:S(2)}) copy-start(f32[1,256,768]{2,1,0:T(8,128)} %param.33) | copy-start | bytes 2359300
  147.8 2.2 copy-start.15
  149.0 5.8 %slice-start = ((s8[4718592]{0:T(1024)(128)(4,1)}), s8[4194304]{0:T(1024)(128)(4,1)S(1)}, s32[]{:S(2)}) async-start(s8[4718592]{0:T(1024)(128)(4,1)} %bitcast.191), calls=%async_computation | async-start | bytes 8388608
  150.0 4.9 %slice-start.1 = ((s8[4718592]{0:T(1024)(128)(4,1)}), s8[524288]{0:T(1024)(128)(4,1)S(1)}, s32[]{:S(2)}) async-start(s8[4718592]{0:T(1024)(128)(4,1)} %bitcast.191), calls=%async_computation.1 | async-start | bytes 1048576
  156.8 1.3 copy-start.4
  156.8 2.5 copy-start.8
  160.8 3.8 %copy-start.5 = (bf16[256,3072]{1,0:T(8,128)(2,1)S(1)}, bf16[256,3072]{1,0:T(8,128)(2,1)}, u32[]{:S(2)}) copy-start(bf16[256,3072]{1,0:T(8,128)(2,1)} %get-tuple-element.90) | copy-start | bytes 4718596
  271.6 2.1 copy-start.3
  271.6 2.1 copy-start.9
  273.7 1.0 copy-start.6
  273.7 1.4 copy-start.11
  274.2 3.5 %copy-start.7 = (bf16[256,768]{1,0:T(8,128)(2,1)S(1)}, bf16[256,768]{1,0:T(8,128)(2,1)}, u32[]{:S(2)}) copy-start(bf16[256,768]{1,0:T(8,128)(2,1)} %get-tuple-element.46) | copy-start | bytes 1179652
  283.9 50.2 %copy-start.13 = (bf16[4,96,768]{2,1,0:T(8,128)(2,1)S(1)}, bf16[4,96,768]{2,1,0:T(8,128)(2,1)}, u32[]{:S(2)}) copy-start(bf16[4,96,768]{2,1,0:T(8,128)(2,1)} %get-tuple-element.55) | copy-start | bytes 1769476
  324.4 10.9 %copy-start.12 = (bf16[4,24,3072]{2,1,0:T(8,128)(2,1)S(1)}, bf16[4,24,3072]{2,1,0:T(8,128)(2,1)}, u32[]{:S(2)}) copy-start(bf16[4,24,3072]{2,1,0:T(8,128)(2,1)} %get-tuple-element.54) | copy-start | bytes 1769476
  324.4 12.1 %copy-start.14 = (bf16[4,24,768]{2,1,0:T(8,128)(2,1)S(1)}, bf16[4,24,768]{2,1,0:T(8,128)(2,1)}, u32[]{:S(2)}) copy-start(bf16[4,24,768]{2,1,0:T(8,128)(2,1)} %get-tuple-element.53) | copy-start | bytes 442372

commit v4 on v3

--- a/solution.py
+++ b/solution.py
@@ -12,6 +12,7 @@
 PAIR = 2 * HD
 CHUNKS = 3
 AHEAD = 2
+FULL, DEPTH, REST = range(3)
 EPSILON = 1e-12
 BF16 = jnp.bfloat16
 F32 = jnp.float32
@@ -194,7 +195,8 @@
     )
 
 
-def gather_kernel(units, count, reps, pairs, *refs):
+def gather_kernel(units, kinds, reps, pairs, *refs):
+    count = len(kinds)
     ins = refs[:count]
     at = count
     if pairs:
@@ -248,17 +250,34 @@
         send(own, own, sends_k, recvs_k, 3 * p, near)
         send(own, own, sends_s, recvs_s, 4 * p, sibling)
 
-    for u, (at, start, size) in enumerate(units):
+    total = len(units)
+    kind_of = [kinds[at] for at, _, _ in units]
+
+    def begin(u):
+        at, start, size = units[u]
         block = ins[at].at[rep, :, pl.ds(start, size)]
         send(block, block_of(u, 0, core, rep), sends_z, recvs_z, 3 * u + 1, far)
         send(block, block_of(u, 0, core, rep), sends_z, recvs_z, 3 * u, near)
-    for u, (at, start, size) in enumerate(units):
-        whole = ins[at].at[:, :, pl.ds(start, size)]
-        send(whole, block_of(u, 0, core, slice(None)), sends_c, recvs_c, 4 * u, sibling)
+
+    def own_whole(u):
+        at, start, size = units[u]
+        if kind_of[u] == REST:
+            return block_of(u, 0, core, slice(None))
+        return ins[at].at[:, :, pl.ds(start, size)]
+
+    for u in range(total):
+        if kind_of[u] == FULL:
+            begin(u)
+    for u in range(total):
+        if kind_of[u] != DEPTH:
+            send(
+                own_whole(u), block_of(u, 0, core, slice(None)), sends_c, recvs_c, 4 * u, sibling
+            )
     for at in range(count):
-        copy = pltpu.make_async_copy(ins[at], outs[at].at[high, low, core], local.at[at])
-        copy.start()
-        copies.append(copy)
+        if kinds[at] != REST:
+            copy = pltpu.make_async_copy(ins[at], outs[at].at[high, low, core], local.at[at])
+            copy.start()
+            copies.append(copy)
 
     for p in range(pairs):
         cols = pl.ds(PAIR * p, PAIR)
@@ -269,15 +288,20 @@
 
     def spread(u, which):
         block = block_of(u, which, core, rep)
-        arrived(block, sends_z, recvs_z, 3 * u + which - 1)
-        if which == 2:
-            send(block, block, sends_z, recvs_z, 3 * u + 2, near)
+        if kind_of[u] != REST:
+            arrived(block, sends_z, recvs_z, 3 * u + which - 1)
+            if which == 2:
+                send(block, block, sends_z, recvs_z, 3 * u + 2, near)
+        if kind_of[u] == DEPTH:
+            return
         for j in range(1, reps):
             index = (3 * u + which - 1) * (reps - 1) + j - 1
             peer = ((rep + j) % reps, me[1])
             send(block, block, sends_r, recvs_r, index, peer)
 
     def pass_on(u, which):
+        if kind_of[u] == DEPTH:
+            return
         for j in range(1, reps):
             index = (3 * u + which - 1) * (reps - 1) + j - 1
             block = block_of(u, which, core, (rep + reps - j) % reps)
@@ -285,12 +309,16 @@
         whole = block_of(u, which, core, slice(None))
         send(whole, whole, sends_c, recvs_c, 4 * u + which, sibling)
 
-    total = len(units)
+    lead = kind_of.count(FULL)
 
     def advance(step):
         if step < total:
             spread(step, 1)
             spread(step, 2)
+            if step < lead:
+                for u in range(lead, total):
+                    if (u - lead) * lead // (total - lead) == step:
+                        begin(u)
         if 1 <= step < total + 1:
             spread(step - 1, 3)
         if 2 <= step:
@@ -316,6 +344,16 @@
         )
 
     steps = total + 2
+    if pairs:
+        for u in range(total):
+            for which in range(1, 4):
+                spread(u, which)
+
+    def finish(step):
+        if 0 < step <= total:
+            for which in range(1, 4):
+                pass_on(step - 1, which)
+
     if not pairs:
         for step in range(steps):
             advance(step)
@@ -339,7 +377,7 @@
 
                 @pl.when(t == i)
                 def _(i=i):
-                    advance(i)
+                    finish(i)
 
             @pl.when((t >= 2) & (t < pairs + 2))
             def _():
@@ -349,27 +387,30 @@
 
         lax.fori_loop(0, max(pairs + 2, steps), step_all, 0)
     for u in range(total):
-        for which in range(4):
-            block = block_of(u, which, 1 - core, slice(None))
-            arrived(block, sends_c, recvs_c, 4 * u + which)
+        if kind_of[u] != DEPTH:
+            for which in range(4):
+                block = block_of(u, which, 1 - core, slice(None))
+                arrived(block, sends_c, recvs_c, 4 * u + which)
+    for copy in copies:
+        copy.wait()
     for u, (at, start, size) in enumerate(units):
-        cols = pl.ds(start, size)
-        left(ins[at].at[rep, :, cols], sends_z, recvs_z, 3 * u)
-        left(ins[at].at[rep, :, cols], sends_z, recvs_z, 3 * u + 1)
-        left(block_of(u, 2, core, rep), sends_z, recvs_z, 3 * u + 2)
-        left(ins[at].at[:, :, cols], sends_c, recvs_c, 4 * u)
-        for which in range(1, 4):
-            left(block_of(u, which, core, slice(None)), sends_c, recvs_c, 4 * u + which)
-            for j in range(1, reps):
-                index = (3 * u + which - 1) * (reps - 1) + j - 1
-                left(block_of(u, which, core, rep), sends_r, recvs_r, index)
+        if kind_of[u] != REST:
+            block = ins[at].at[rep, :, pl.ds(start, size)]
+            left(block, sends_z, recvs_z, 3 * u)
+            left(block, sends_z, recvs_z, 3 * u + 1)
+            left(block_of(u, 2, core, rep), sends_z, recvs_z, 3 * u + 2)
+        if kind_of[u] != DEPTH:
+            left(own_whole(u), sends_c, recvs_c, 4 * u)
+            for which in range(1, 4):
+                left(block_of(u, which, core, slice(None)), sends_c, recvs_c, 4 * u + which)
+                for j in range(1, reps):
+                    index = (3 * u + which - 1) * (reps - 1) + j - 1
+                    left(block_of(u, which, core, rep), sends_r, recvs_r, index)
     for p in range(pairs):
         for at, which in enumerate((0, 0, 2)):
             left(held(p, which, core), sends_k, recvs_k, 3 * p + at)
         for which in range(4):
             left(held(p, which, core), sends_s, recvs_s, 4 * p + which)
-    for copy in copies:
-        copy.wait()
 
 
 def cut(width, pieces):
@@ -379,20 +420,23 @@
     return [(size * i, size) for i in range(pieces)]
 
 
-def gather_many(shards, pieces, identity, query=None, keys=None, values=None):
+def gather_many(shards, pieces, kinds, identity, query=None, keys=None, values=None):
     reps = lax.axis_size("rep")
     count = len(shards)
     units = [
         (at, low, size)
         for at, shard in enumerate(shards)
-        for low, size in cut(shard.shape[2], pieces[at])
+        for low, size in cut(shard.shape[-1], pieces[at])
     ]
     total = len(units)
     hops = 3 * total * (reps - 1)
     dma = pltpu.SemaphoreType.DMA
     vmem = pl.BlockSpec(memory_space=pltpu.VMEM)
     out_shape = [
-        jax.ShapeDtypeStruct((2, 2, 2) + shard.shape, shard.dtype) for shard in shards
+        jax.ShapeDtypeStruct(
+            shard.shape if kind == REST else (2, 2, 2) + shard.shape, shard.dtype
+        )
+        for shard, kind in zip(shards, kinds)
     ]
     operands = list(shards)
     spaces = []
@@ -408,7 +452,8 @@
         ]
         more = [dma((3 * pairs,))] * 2 + [dma((4 * pairs,))] * 2
     return pl.pallas_call(
-        functools.partial(gather_kernel, units, count, reps, pairs),
+        functools.partial(gather_kernel, units, tuple(kinds), reps, pairs),
+        input_output_aliases={at: at for at in range(count) if kinds[at] == REST},
         out_shape=out_shape,
         in_specs=[pl.BlockSpec(memory_space=pl.ANY)] * count + spaces,
         out_specs=[pl.BlockSpec(memory_space=pl.ANY)] * count + spaces[:2],
@@ -430,7 +475,8 @@
     return total.astype(kind)
 
 
-def reduce_kernel(units, count, reps, fused, *refs):
+def reduce_kernel(units, kinds, reps, fused, *refs):
+    count = len(kinds)
     ins = refs[:count]
     at = count
     if fused:
@@ -442,10 +488,11 @@
         grad_query_ref, grad_key_ref, grad_value_ref = refs[at : at + 3]
         at += 3
     size = len(units)
-    first, second, third, fourth, own = [
-        refs[at + i * size : at + (i + 1) * size] for i in range(5)
+    first, second, third, fourth, own, mid = [
+        refs[at + i * size : at + (i + 1) * size] for i in range(6)
     ]
-    sems = refs[at + 5 * size :]
+    sems = refs[at + 6 * size :]
+    kind_of = [kinds[a] for a, _, _ in units]
     sends_c, recvs_c, sends_r, recvs_r, sends_z, recvs_z, sends_g, recvs_g = sems[:8]
     rep, high, low, core = places()
     me = (rep, place_of(high, low, core))
@@ -463,11 +510,17 @@
         remote(block, block, sends, recvs, at, me).wait_recv()
 
     for u, (a, start, width) in enumerate(units):
+        if kind_of[u] == DEPTH:
+            own[u][...] = ins[a][:, :, :, start : start + width]
+            send(own[u].at[:, 1 - low], third[u], sends_z, recvs_z, 2 * u, near)
+            continue
         block = ins[a].at[:, :, 1 - core, :, :, pl.ds(start, width)]
         send(block, first[u], sends_c, recvs_c, u, sibling)
 
     def over_core(u):
         a, start, width = units[u]
+        if kind_of[u] == DEPTH:
+            return
         arrived(first[u], sends_c, recvs_c, u)
 
         def step(i, carry):
@@ -489,31 +542,40 @@
             )
 
     def over_rep(u):
+        a, start, width = units[u]
+        if kind_of[u] == DEPTH:
+            return
         for k in range(1, reps):
             arrived(second[u].at[k - 1], sends_r, recvs_r, u * (reps - 1) + k - 1)
 
         def step(i, carry):
             h, w = i // 2, i % 2
             parts = [first[u][h, w, rep]] + [second[u][k, h, w] for k in range(reps - 1)]
-            own[u][h, w] = summed(parts, own[u].dtype)
+            total = summed(parts, first[u].dtype)
+            if kind_of[u] == REST:
+                outs[a][h, w, :, start : start + width] = total
+            else:
+                own[u][h, w] = total
             return carry
 
         lax.fori_loop(0, 4, step, 0)
-        send(own[u].at[:, 1 - low], third[u], sends_z, recvs_z, 2 * u, near)
+        if kind_of[u] == FULL:
+            send(own[u].at[:, 1 - low], third[u], sends_z, recvs_z, 2 * u, near)
 
     def over_near(u):
+        if kind_of[u] == REST:
+            return
         arrived(third[u], sends_z, recvs_z, 2 * u)
         for h in range(2):
             own[u][h, low] = summed([own[u][h, low], third[u][h]], own[u].dtype)
         send(own[u].at[1 - high, low], fourth[u], sends_z, recvs_z, 2 * u + 1, far)
 
     def over_far(u):
-        a, start, width = units[u]
+        if kind_of[u] == REST:
+            return
         arrived(fourth[u], sends_z, recvs_z, 2 * u + 1)
-        outs[a][rep, :, start : start + width] = summed(
-            [own[u][high, low], fourth[u][...]], outs[a].dtype
-        )
-        block = outs[a].at[rep, :, pl.ds(start, width)]
+        mid[u][rep] = summed([own[u][high, low], fourth[u][...]], mid[u].dtype)
+        block = mid[u].at[rep]
         for k in range(1, reps):
             peer = ((rep + k) % reps, me[1])
             send(block, block, sends_g, recvs_g, u * (reps - 1) + k - 1, peer)
@@ -615,18 +677,24 @@
             for which in range(3):
                 hop(p, which).wait_send()
     for u, (a, start, width) in enumerate(units):
-        for k in range(1, reps):
-            block = outs[a].at[(rep + reps - k) % reps, :, pl.ds(start, width)]
-            arrived(block, sends_g, recvs_g, u * (reps - 1) + k - 1)
+        if kind_of[u] != REST:
+            for k in range(1, reps):
+                block = mid[u].at[(rep + reps - k) % reps]
+                arrived(block, sends_g, recvs_g, u * (reps - 1) + k - 1)
+            outs[a][:, :, start : start + width] = mid[u][...].astype(F32)
     for u, (a, start, width) in enumerate(units):
         cols = pl.ds(start, width)
-        left(ins[a].at[:, :, 1 - core, :, :, cols], sends_c, recvs_c, u)
-        left(own[u].at[:, 1 - low], sends_z, recvs_z, 2 * u)
-        left(own[u].at[1 - high, low], sends_z, recvs_z, 2 * u + 1)
+        if kind_of[u] != DEPTH:
+            left(ins[a].at[:, :, 1 - core, :, :, cols], sends_c, recvs_c, u)
+        if kind_of[u] != REST:
+            left(own[u].at[:, 1 - low], sends_z, recvs_z, 2 * u)
+            left(own[u].at[1 - high, low], sends_z, recvs_z, 2 * u + 1)
         for k in range(1, reps):
             index = u * (reps - 1) + k - 1
-            left(first[u].at[:, :, (rep + k) % reps], sends_r, recvs_r, index)
-            left(outs[a].at[rep, :, cols], sends_g, recvs_g, index)
+            if kind_of[u] != DEPTH:
+                left(first[u].at[:, :, (rep + k) % reps], sends_r, recvs_r, index)
+            if kind_of[u] != REST:
+                left(mid[u].at[rep], sends_g, recvs_g, index)
 
 
 def split_rows(part):
@@ -635,26 +703,33 @@
     return part.reshape(2, 2, 2, reps, rows // (8 * reps), width)
 
 
-def reduce_many(blocks, pieces, identity, query=None, grad=None, pairs=None):
+def reduce_many(blocks, pieces, kinds, identity, query=None, grad=None, pairs=None):
     reps = lax.axis_size("rep")
     count = len(blocks)
     units = [
         (at, low, size)
         for at, block in enumerate(blocks)
-        for low, size in cut(block.shape[5], pieces[at])
+        for low, size in cut(block.shape[-1], pieces[at])
     ]
     dma = pltpu.SemaphoreType.DMA
     vmem = pl.BlockSpec(memory_space=pltpu.VMEM)
 
-    def buffers(*lead):
-        return [
-            pltpu.VMEM(lead + (blocks[at].shape[4], size), blocks[at].dtype)
-            for at, _, size in units
-        ]
+    def buffers(without, *lead):
+        shapes = []
+        for at, _, size in units:
+            tile = (blocks[at].shape[-2], size)
+            if kinds[at] == without:
+                shapes.append(pltpu.VMEM((8, 128), BF16))
+            else:
+                shapes.append(pltpu.VMEM(lead + tile, blocks[at].dtype))
+        return shapes
 
     total = len(units)
     out_shape = [
-        jax.ShapeDtypeStruct((reps,) + block.shape[4:], block.dtype) for block in blocks
+        jax.ShapeDtypeStruct((2, 2) + block.shape[4:], block.dtype)
+        if kind == REST
+        else jax.ShapeDtypeStruct((reps,) + block.shape[-2:], F32)
+        for block, kind in zip(blocks, kinds)
     ]
     operands = list(blocks)
     in_specs = [vmem] * count
@@ -677,15 +752,16 @@
             dma((2,)),
         ]
     sums = pl.pallas_call(
-        functools.partial(reduce_kernel, units, count, reps, pairs is not None),
+        functools.partial(reduce_kernel, units, tuple(kinds), reps, pairs is not None),
         out_shape=out_shape,
         in_specs=in_specs,
         out_specs=[vmem] * len(out_shape),
-        scratch_shapes=buffers(2, 2, reps)
-        + buffers(reps - 1, 2, 2)
-        + buffers(2)
-        + buffers()
-        + buffers(2, 2)
+        scratch_shapes=buffers(DEPTH, 2, 2, reps)
+        + buffers(DEPTH, reps - 1, 2, 2)
+        + buffers(REST, 2)
+        + buffers(REST)
+        + buffers(REST, 2, 2)
+        + buffers(REST, reps)
         + [dma((total,))] * 2
         + [dma((total * (reps - 1),))] * 2
         + [dma((total * 2,))] * 2
@@ -695,7 +771,10 @@
             collective_id=identity, has_side_effects=True, vmem_limit_bytes=60 * 1024 * 1024
         ),
     )(*operands)
-    totals = [total.reshape(-1, total.shape[2]).astype(F32) for total in sums[:count]]
+    totals = [
+        total if kind == REST else total.reshape(-1, total.shape[2])
+        for total, kind in zip(sums, kinds)
+    ]
     return totals + list(sums[count:])
 
 
@@ -753,8 +832,12 @@
         packed = jnp.concatenate(rows, axis=0)
         packed = jnp.pad(packed, ((0, -packed.shape[0] % (8 * reps)), (0, 0))).astype(BF16)
         shards = (key_weight, value_weight, query_weight, packed)
-        w_key, w_value, w_query, gathered = gather_many(
-            [blocked(shard) for shard in shards], (1, 1, 1, 1), 1
+        shards += (output_weight, up_weight, down_weight)
+        w_key, w_value, w_query, gathered, *begun = gather_many(
+            [blocked(shard) for shard in shards],
+            (1, 1, 1, 1, 1, 2, 2),
+            (FULL,) * 4 + (DEPTH,) * 3,
+            1,
         )
         w_key, w_value, w_query = [w.reshape(-1, width) for w in (w_key, w_value, w_query)]
         gathered = gathered.reshape(-1, packed.shape[0], 128)
@@ -782,10 +865,10 @@
     query_rows = (matmul(local_tokens, w_query) + b_query).astype(BF16)
     query_scaled = query_rows * jnp.asarray(1.0 / math.sqrt(HD), BF16)
     if fast:
-        shards = (output_weight, up_weight, down_weight)
         w_output, w_up, w_down, context_low, pairs = gather_many(
-            [blocked(shard) for shard in shards],
+            begun,
             (1, 2, 2),
+            (REST,) * 3,
             2,
             query_scaled,
             key_rows,
@@ -835,15 +918,14 @@
 
     if fast:
         (
-            full_down,
-            full_up,
-            full_output,
+            *begun,
             grad_query_low,
             grad_key_low,
             grad_value_low,
         ) = reduce_many(
             [split_rows(part) for part in (part_down, part_up, part_output)],
             (2, 2, 1),
+            (REST,) * 3,
             3,
             query_scaled,
             grad_context,
@@ -891,8 +973,11 @@
     if fast:
         flat = jnp.pad(flat, ((0, 0), (0, -flat.shape[1] % (8 * 128 * reps))))
         blocks = [split_rows(part) for part in (part_query, part_key, part_value)]
-        full_query, full_key, full_value, sums = reduce_many(
-            blocks + [flat.reshape(2, 2, 2, reps, -1, 128)], (1, 1, 1, 1), 4
+        full_query, full_key, full_value, sums, full_down, full_up, full_output = reduce_many(
+            blocks + [flat.reshape(2, 2, 2, reps, -1, 128)] + begun,
+            (1,) * 7,
+            (FULL,) * 4 + (DEPTH,) * 3,
+            4,
         )
         sums = sums.reshape(-1)
     else:

time: 339 us -> 366 us (1.080)
  Pallas kernels: 266 us -> 286 us
  local copies, waits for them, and re-layouts: 14.2 us -> 26.7 us
  other arithmetic: 11.7 us -> 7.11 us
    pallas_call x4, Pallas kernels: 266 us -> 286 us  [the longest x2 158 us: reduce_many(): pl.pallas_call(functools.partial(reduce_kernel, units, tuple(kinds), reps...]
    unnamed x46 -> x82, local copies, waits for them, and re-layouts: 3.12 us -> 11.4 us
    convert_element_type x6 -> x0, other arithmetic: 8.02 us -> none  [reduce_many(): total.reshape(-1, total.shape[2]).astype(F32)]
    reshape x9, local copies, waits for them, and re-layouts: 0.58 us -> 4.72 us  [on_device(): vector.reshape(owners, -1)]
where the time goes in v4:
time: 366 us; the launch traced here: 365 us
  Pallas kernels  286 us (78%)
  matrix products  42.8 us (12%)
  local copies, waits for them, and re-layouts  26.7 us (7%)
  other arithmetic  7.11 us (2%)
    pallas_call x2, Pallas kernels, reduce_many(): pl.pallas_call(functools.partial(reduce_kernel, units, tuple(kinds), reps...  158 us
    pallas_call x2, Pallas kernels, gather_many(): pl.pallas_call(functools.partial(gather_kernel, units, tuple(kinds), reps...  128 us
    dot_general x6, matrix products, over_rows(): lax.dot_general(left, right, (((0,), (0,)), ((), ())), preferred_element_...  15.5 us
    dot_general x6, matrix products, matmul(): return jnp.dot(left, right, preferred_element_type=F32)  14.4 us
    dot_general x6, matrix products, against(): lax.dot_general(left, right, (((1,), (1,)), ((), ())), preferred_element_...  13 us
    unnamed x82, local copies, waits for them, and re-layouts  11.4 us

profile of v4, /device:TPU:0, one launch (start us, length us, event | category | flops | bytes accessed | tf_op | source)
XLA Modules:
  0.0 365.2 jit_solution(12214467709524796078)
XLA Ops:
  0.7 0.7 pad_bitcast_fusion.8
  1.4 0.7 pad_bitcast_fusion.6
  2.1 0.7 pad_bitcast_fusion.4
  2.7 0.7 pad_bitcast_fusion.2
  3.4 0.7 concatenate.7
  4.2 0.6 pad_bitcast_fusion.1.refs_3_
  4.8 1.2 reduce_sum.210
  6.0 0.7 reshape.388
  6.6 61.8 %shard_map.304 = (bf16[2,2,2,4,24,768]{5,4,3,2,1,0:T(8,128)(2,1)}, bf16[2,2,2,4,24,768]{5,4,3,2,1,0:T(8,128)(2,1)}, bf16[2,2,2,4,24,768]{5,4,3,2,1,0:T(8,128)(2,...) custom-call(bf16[4,24,768]{2,1,0:T(8,128)(2,1)} %bitcast.174, ...), custom_call_target="tpu_custom_call" | custom-call | tf_op jit(solution)/shard_map/pallas_call | solution.py:454
  68.4 0.8 slice_convert_fusion
  69.2 1.0 fusion.22
  70.6 0.1 reshape.399
  71.0 2.5 fusion.7.refs_3_
  73.5 1.2 fusion.5.refs_5_
  74.8 1.2 fusion.4.refs_4_
  76.0 66.2 %shard_map.305 = (bf16[2,2,2,4,24,768]{5,4,3,2,1,0:T(8,128)(2,1)}, bf16[2,2,2,4,24,3072]{5,4,3,2,1,0:T(8,128)(2,1)}, bf16[2,2,2,4,96,768]{5,4,3,2,1,0:T(8,128)(2...) custom-call(bf16[2,2,2,4,24,768]{5,4,3,2,1,0:T(8,128)(2,1)} %get-tup, ...), custom_call_target="tpu_custom_call", output_to_operand_aliasing={{0}: (0, {}), {1}: (1, {}), {2}: (2, {})} | custom-call | tf_op jit(solution)/shard_map/pallas_call | solution.py:454
  142.2 2.0 fusion.24
  144.2 0.2 multiply_reduce_fusion.5
  144.5 5.9 %multiply_convert_fusion = (bf16[256,3072]{1,0:T(8,128)(2,1)S(1)}, f32[256,3072]{1,0:T(8,128)}) fusion(f32[3072]{0:T(1024)S(1)} %reshape.401, bf16[768,3072]{1,0:T(8,128)(2,1)} %bitcast.152, f32[256,768]{1,0:T(8,128)S(1)} %get-tuple-element.101, f32[768]{0:T(1024)S(1)} %reshape.400, f32[768]{0:T(1024)S(1)} %reshape.399, f32[256]{0:T(256)S(1)} %fusion.16, ...), kind=kOutput, calls=%fused_computation.5 | convolution fusion | flops 1213661184 | bytes 10244096 | tf_op jit(solution)/shard_map/dot_general | solution.py:33
  150.4 1.5 fusion.25
  152.0 0.2 multiply_reduce_fusion.4
  152.2 0.3 fusion.8
  152.5 0.7 reshape.387
  153.2 1.2 fusion.21
  154.4 0.1 convert_reduce_fusion.1
  154.6 0.8 copy-done.28
  155.4 5.1 %convert_reduce_fusion = (f32[3072]{0:T(1024)S(1)}, bf16[256,3072]{1,0:T(8,128)(2,1)S(1)}) fusion(f32[256,3072]{1,0:T(8,128)S(1)} %copy-done.28, bf16[256,768]{1,0:T(8,128)(2,1)S(1)} %get-tuple-element.74, bf16[3072,768]{1,0:T(8,128)(2,1)} %bitcast.156), kind=kOutput, calls=%fused_computation.3 | convolution fusion | flops 1219752960 | bytes 9842688 | tf_op jit(solution)/shard_map/dot_general | solution.py:41
  160.5 2.5 multiply_reduce_fusion.1
  163.0 0.6 reshape.385
  163.6 0.7 reshape.383
  164.3 0.7 reshape.386
  165.0 1.5 fusion.20
  166.4 0.5 negate_multiply_fusion
  166.9 0.7 reshape.384
  167.6 0.7 convert_reduce_fusion.2
  168.4 1.3 convolution_convert_fusion.7.refs_4_
  169.6 0.7 reshape.382
  170.3 2.6 convolution_convert_fusion.5
  172.9 4.6 %convolution_convert_fusion = bf16[768,3072]{1,0:T(8,128)(2,1)} fusion(bf16[256,3072]{1,0:T(8,128)(2,1)S(1)} %copy-done.13, f32[256,768]{1,0:T(8,128)S(1)} %get-tuple-element.101, f32[768]{0:T(1024)S(1)} %reshape.400, f32[768]{0:T(1024)S(1)} %reshape.399, f32[256]{0:T(256)} %copy-done.26, f32[256]{0:T(256)S(1)} %broadcast_multiply_fusion.1), kind=kOutput, calls=%fused_computation | convolution fusion | flops 1211301888 | bytes 7086080 | tf_op jit(solution)/shard_map/dot_general | solution.py:37
  177.6 3.6 convolution_convert_fusion.1
  181.2 90.6 %shard_map.306 = (bf16[2,2,96,768]{3,2,1,0:T(8,128)(2,1)}, bf16[2,2,24,3072]{3,2,1,0:T(8,128)(2,1)}, bf16[2,2,24,768]{3,2,1,0:T(8,128)(2,1)}, bf16[256,768]{1,0:...) custom-call(bf16[2,2,2,4,96,768]{5,4,3,2,1,0:T(8,128)(2,1)} %bitcast.141, ...), custom_call_target="tpu_custom_call" | custom-call | tf_op jit(solution)/shard_map/pallas_call | solution.py:754
  271.9 1.6 convolution_add_fusion.5
  273.5 0.5 convolution_add_fusion.4
  274.0 0.4 copy-done.8
  274.5 0.4 copy-done.15
  274.9 2.0 multiply_reduce_fusion
  276.9 0.6 broadcast_in_dim.40
  277.6 0.1 convert_reduce_fusion.4
  277.7 0.1 convert_reduce_fusion.3
  277.9 0.1 concatenate.8
  278.1 0.7 copy.63
  278.7 1.5 convolution_convert_fusion.2
  280.3 1.5 convolution_convert_fusion.4
  281.8 1.5 convolution_convert_fusion.3
  283.3 66.9 %shard_map.307 = (f32[4,24,768]{2,1,0:T(8,128)}, f32[4,24,768]{2,1,0:T(8,128)}, f32[4,24,768]{2,1,0:T(8,128)}, f32[4,8,128]{2,1,0:T(8,128)}, f32[4,96,768]{2,1,0...) custom-call(bf16[2,2,2,4,24,768]{5,4,3,2,1,0:T(8,128)(2,1)} %bitcast.150, ...), custom_call_target="tpu_custom_call" | custom-call | tf_op jit(solution)/shard_map/pallas_call | solution.py:754
  350.3 1.3 slice.126
  352.2 1.3 slice.122
  353.6 1.5 fusion.23
  355.1 1.8 copy.89
  356.9 1.7 copy.90
  358.6 1.7 copy.91
  360.3 1.7 copy.92
  362.0 1.0 copy.93
  363.0 1.0 copy.94
  (99 shorter events, 1.0 us)
Async XLA Ops:
  0.7 70.4 %copy-start.1 = (bf16[1,256,768]{2,1,0:T(8,128)(2,1)S(1)}, bf16[1,256,768]{2,1,0:T(8,128)(2,1)}, u32[]{:S(2)}) copy-start(bf16[1,256,768]{2,1,0:T(8,128)(2,1)} %param.17) | copy-start | bytes 1179652
  68.4 5.1 %copy-start.14 = (bf16[2,2,2,4,24,768]{5,4,3,2,1,0:T(8,128)(2,1)S(1)}, bf16[2,2,2,4,24,768]{5,4,3,2,1,0:T(8,128)(2,1)}, u32[]{:S(2)}) copy-start(bf16[2,2,2,4,24,768]{5,4,3,2,1,0:T(8,128)(2,1)} %get-tuple-element.49) | copy-start | bytes 3538948
  70.3 4.5 %copy-start.3 = (bf16[2,2,2,4,24,768]{5,4,3,2,1,0:T(8,128)(2,1)S(1)}, bf16[2,2,2,4,24,768]{5,4,3,2,1,0:T(8,128)(2,1)}, u32[]{:S(2)}) copy-start(bf16[2,2,2,4,24,768]{5,4,3,2,1,0:T(8,128)(2,1)} %get-tuple-element.48) | copy-start | bytes 3538948
  144.2 6.2 %slice-start.2 = ((s8[4718592]{0:T(1024)(128)(4,1)}), s8[4194304]{0:T(1024)(128)(4,1)S(1)}, s32[]{:S(2)}) async-start(s8[4718592]{0:T(1024)(128)(4,1)} %bitcast.157), calls=%async_computation.2 | async-start | bytes 8388608
  144.4 20.5 %copy-start.26 = (f32[256]{0:T(256)}, f32[256]{0:T(256)S(1)}, u32[]{:S(2)}) copy-start(f32[256]{0:T(256)S(1)} %fusion.16) | copy-start | bytes 3076
  144.5 6.0 %slice-start.3 = ((s8[4718592]{0:T(1024)(128)(4,1)}), s8[524288]{0:T(1024)(128)(4,1)S(1)}, s32[]{:S(2)}) async-start(s8[4718592]{0:T(1024)(128)(4,1)} %bitcast.157), calls=%async_computation.3 | async-start | bytes 1048576
  150.4 1.6 copy-start.5
  150.4 1.8 copy-start.2
  153.2 2.2 copy-start.28
  154.4 6.0 %slice-start = ((s8[4718592]{0:T(1024)(128)(4,1)}), s8[4194304]{0:T(1024)(128)(4,1)S(1)}, s32[]{:S(2)}) async-start(s8[4718592]{0:T(1024)(128)(4,1)} %bitcast.153), calls=%async_computation | async-start | bytes 8388608
  154.6 5.9 %copy-start.9 = (bf16[256,768]{1,0:T(8,128)(2,1)}, bf16[256,768]{1,0:T(8,128)(2,1)S(1)}, u32[]{:S(2)}) copy-start(bf16[256,768]{1,0:T(8,128)(2,1)S(1)} %get-tuple-element.74) | copy-start | bytes 1179652
  155.4 5.1 %slice-start.1 = ((s8[4718592]{0:T(1024)(128)(4,1)}), s8[524288]{0:T(1024)(128)(4,1)S(1)}, s32[]{:S(2)}) async-start(s8[4718592]{0:T(1024)(128)(4,1)} %bitcast.153), calls=%async_computation.1 | async-start | bytes 1048576
  160.4 2.6 copy-start.12
  163.0 5.3 %copy-start = (bf16[2,2,2,4,24,768]{5,4,3,2,1,0:T(8,128)(2,1)S(1)}, bf16[2,2,2,4,24,768]{5,4,3,2,1,0:T(8,128)(2,1)}, u32[]{:S(2)}) copy-start(bf16[2,2,2,4,24,768]{5,4,3,2,1,0:T(8,128)(2,1)} %get-tuple-element.51) | copy-start | bytes 3538948
  170.3 2.6 copy-start.13
  172.9 4.6 %copy-start.6 = (bf16[256,3072]{1,0:T(8,128)(2,1)S(1)}, bf16[256,3072]{1,0:T(8,128)(2,1)}, u32[]{:S(2)}) copy-start(bf16[256,3072]{1,0:T(8,128)(2,1)} %copy-done.5) | copy-start | bytes 4718596
  172.9 4.6 %copy-start.10 = (bf16[256,768]{1,0:T(8,128)(2,1)S(1)}, bf16[256,768]{1,0:T(8,128)(2,1)}, u32[]{:S(2)}) copy-start(bf16[256,768]{1,0:T(8,128)(2,1)} %copy-done.9) | copy-start | bytes 1179652
  181.2 90.6 %copy-start.16 = (bf16[2,2,2,4,24,768]{5,4,3,2,1,0:T(8,128)(2,1)S(1)}, bf16[2,2,2,4,24,768]{5,4,3,2,1,0:T(8,128)(2,1)}, u32[]{:S(2)}) copy-start(bf16[2,2,2,4,24,768]{5,4,3,2,1,0:T(8,128)(2,1)} %get-tuple-element.46) | copy-start | bytes 3538948
  181.2 90.6 %copy-start.27 = (f32[256]{0:T(256)S(1)}, f32[256]{0:T(256)}, u32[]{:S(2)}) copy-start(f32[256]{0:T(256)} %negate_multiply_fusion) | copy-start | bytes 3076
  271.8 1.7 copy-start.4
  271.8 1.7 copy-start.11
  273.5 1.0 copy-start.8
  273.5 1.4 copy-start.15
  274.9 2.7 copy-start.7
  274.9 3.0 copy-start.19
  274.9 3.0 copy-start.20
  274.9 3.0 copy-start.21
  274.9 3.0 copy-start.22
  274.9 3.0 copy-start.23
  274.9 3.0 copy-start.24
  274.9 3.0 copy-start.25
  350.3 11.7 %copy-start.18 = (f32[4,24,3072]{2,1,0:T(8,128)S(1)}, f32[4,24,3072]{2,1,0:T(8,128)}, u32[]{:S(2)}) copy-start(f32[4,24,3072]{2,1,0:T(8,128)} %get-tuple-element.66) | copy-start | bytes 3538948
  355.1 7.9 %copy-start.17 = (f32[4,96,768]{2,1,0:T(8,128)S(1)}, f32[4,96,768]{2,1,0:T(8,128)}, u32[]{:S(2)}) copy-start(f32[4,96,768]{2,1,0:T(8,128)} %get-tuple-element.67) | copy-start | bytes 3538948

commit v5 on v4

--- a/solution.py
+++ b/solution.py
@@ -455,7 +455,10 @@
         functools.partial(gather_kernel, units, tuple(kinds), reps, pairs),
         input_output_aliases={at: at for at in range(count) if kinds[at] == REST},
         out_shape=out_shape,
-        in_specs=[pl.BlockSpec(memory_space=pl.ANY)] * count + spaces,
+        in_specs=[
+            pl.BlockSpec(memory_space=pl.ANY if kind == REST else pltpu.VMEM) for kind in kinds
+        ]
+        + spaces,
         out_specs=[pl.BlockSpec(memory_space=pl.ANY)] * count + spaces[:2],
         scratch_shapes=[dma((3 * total,))] * 2
         + [dma((hops,))] * 2
@@ -589,8 +592,12 @@
 
     steps = size + len(stages) - 1
     if not fused:
-        for stage in stages:
-            for u in range(size):
+        whole = [u for u in range(size) if kind_of[u] != DEPTH]
+        rest = [u for u in range(size) if kind_of[u] == DEPTH]
+        order = [(over_core, whole), (over_near, rest), (over_rep, whole)]
+        order += [(over_far, rest), (over_near, whole), (over_far, whole)]
+        for stage, members in order:
+            for u in members:
                 stage(u)
     else:
         terms, merged, from_near, from_far, held, sends_k, recvs_k, fetched = sems[8:]

time: 366 us -> 334 us (0.913)
  Pallas kernels: 286 us -> 253 us
    pallas_call x2, Pallas kernels: 128 us -> 107 us  [gather_many(): pl.pallas_call(functools.partial(gather_kernel, units, tuple(kinds), reps...]
    pallas_call x2, Pallas kernels: 158 us -> 146 us  [reduce_many(): pl.pallas_call(functools.partial(reduce_kernel, units, tuple(kinds), reps...]
where the time goes in v5:
time: 334 us; the launch traced here: 333 us
  Pallas kernels  253 us (76%)
  matrix products  42.8 us (13%)
  local copies, waits for them, and re-layouts  26.7 us (8%)
  other arithmetic  7.11 us (2%)
    pallas_call x2, Pallas kernels, reduce_many(): pl.pallas_call(functools.partial(reduce_kernel, units, tuple(kinds), reps...  146 us
    pallas_call x2, Pallas kernels, gather_many(): pl.pallas_call(functools.partial(gather_kernel, units, tuple(kinds), reps...  107 us
    dot_general x6, matrix products, over_rows(): lax.dot_general(left, right, (((0,), (0,)), ((), ())), preferred_element_...  15.5 us
    dot_general x6, matrix products, matmul(): return jnp.dot(left, right, preferred_element_type=F32)  14.4 us
    dot_general x6, matrix products, against(): lax.dot_general(left, right, (((1,), (1,)), ((), ())), preferred_element_...  12.9 us
    unnamed x82, local copies, waits for them, and re-layouts  11.4 us

profile of v5, /device:TPU:0, one launch (start us, length us, event | category | flops | bytes accessed | tf_op | source)
XLA Modules:
  0.0 332.7 jit_solution(7530529877420958716)
XLA Ops:
  0.7 0.7 pad_bitcast_fusion.8
  1.4 0.7 pad_bitcast_fusion.6
  2.1 0.7 pad_bitcast_fusion.4
  2.7 0.7 pad_bitcast_fusion.2
  3.4 0.7 concatenate.7
  4.2 0.6 pad_bitcast_fusion.1.refs_3_
  4.8 1.2 reduce_sum.210
  6.0 0.7 reshape.388
  6.6 43.5 %shard_map.304 = (bf16[2,2,2,4,24,768]{5,4,3,2,1,0:T(8,128)(2,1)}, bf16[2,2,2,4,24,768]{5,4,3,2,1,0:T(8,128)(2,1)}, bf16[2,2,2,4,24,768]{5,4,3,2,1,0:T(8,128)(2,...) custom-call(bf16[4,24,768]{2,1,0:T(8,128)(2,1)} %bitcast.174, ...), custom_call_target="tpu_custom_call" | custom-call | tf_op jit(solution)/shard_map/pallas_call | solution.py:454
  50.2 0.8 slice_convert_fusion
  51.0 1.0 fusion.22
  52.5 0.1 reshape.397
  52.7 2.5 fusion.7.refs_3_
  55.3 1.2 fusion.5.refs_5_
  56.5 1.2 fusion.4.refs_4_
  57.7 63.6 %shard_map.305 = (bf16[2,2,2,4,24,768]{5,4,3,2,1,0:T(8,128)(2,1)}, bf16[2,2,2,4,24,3072]{5,4,3,2,1,0:T(8,128)(2,1)}, bf16[2,2,2,4,96,768]{5,4,3,2,1,0:T(8,128)(2...) custom-call(bf16[2,2,2,4,24,768]{5,4,3,2,1,0:T(8,128)(2,1)} %get-tup, ...), custom_call_target="tpu_custom_call", output_to_operand_aliasing={{0}: (0, {}), {1}: (1, {}), {2}: (2, {})} | custom-call | tf_op jit(solution)/shard_map/pallas_call | solution.py:454
  121.3 2.0 fusion.24
  123.3 0.2 multiply_reduce_fusion.5
  123.6 5.9 %multiply_convert_fusion = (bf16[256,3072]{1,0:T(8,128)(2,1)S(1)}, f32[256,3072]{1,0:T(8,128)}) fusion(f32[3072]{0:T(1024)S(1)} %reshape.401, bf16[768,3072]{1,0:T(8,128)(2,1)} %bitcast.152, f32[256,768]{1,0:T(8,128)S(1)} %get-tuple-element.101, f32[768]{0:T(1024)S(1)} %reshape.400, f32[768]{0:T(1024)S(1)} %reshape.399, f32[256]{0:T(256)S(1)} %fusion.16, ...), kind=kOutput, calls=%fused_computation.5 | convolution fusion | flops 1213661184 | bytes 10244096 | tf_op jit(solution)/shard_map/dot_general | solution.py:33
  129.5 1.5 fusion.25
  131.1 0.2 multiply_reduce_fusion.4
  131.3 0.3 fusion.8
  131.6 0.7 reshape.387
  132.3 1.2 fusion.21
  133.5 0.1 convert_reduce_fusion.1
  133.7 0.8 copy-done.28
  134.4 5.1 %convert_reduce_fusion = (f32[3072]{0:T(1024)S(1)}, bf16[256,3072]{1,0:T(8,128)(2,1)S(1)}) fusion(f32[256,3072]{1,0:T(8,128)S(1)} %copy-done.28, bf16[256,768]{1,0:T(8,128)(2,1)S(1)} %get-tuple-element.74, bf16[3072,768]{1,0:T(8,128)(2,1)} %bitcast.156), kind=kOutput, calls=%fused_computation.3 | convolution fusion | flops 1219752960 | bytes 9842688 | tf_op jit(solution)/shard_map/dot_general | solution.py:41
  139.6 2.5 multiply_reduce_fusion.1
  142.1 0.6 reshape.385
  142.7 0.7 reshape.383
  143.4 0.7 reshape.386
  144.0 1.5 fusion.20
  145.5 0.5 negate_multiply_fusion
  146.0 0.7 reshape.384
  146.7 0.7 convert_reduce_fusion.2
  147.5 1.3 convolution_convert_fusion.7.refs_4_
  148.7 0.7 reshape.382
  149.4 2.6 convolution_convert_fusion.5
  152.0 4.6 %convolution_convert_fusion = bf16[768,3072]{1,0:T(8,128)(2,1)} fusion(bf16[256,3072]{1,0:T(8,128)(2,1)S(1)} %copy-done.13, f32[256,768]{1,0:T(8,128)S(1)} %get-tuple-element.101, f32[768]{0:T(1024)S(1)} %reshape.400, f32[768]{0:T(1024)S(1)} %reshape.399, f32[256]{0:T(256)} %copy-done.26, f32[256]{0:T(256)S(1)} %broadcast_multiply_fusion.1), kind=kOutput, calls=%fused_computation | convolution fusion | flops 1211301888 | bytes 7086080 | tf_op jit(solution)/shard_map/dot_general | solution.py:37
  156.6 3.6 %convolution_convert_fusion.1 = bf16[3072,768]{1,0:T(8,128)(2,1)} fusion(bf16[256,3072]{1,0:T(8,128)(2,1)S(1)} %copy-done.6, bf16[256,768]{1,0:T(8,128)(2,1)S(1)} %copy-done.10), kind=kOutput, calls=%fused_computation.1 | convolution fusion | flops 1210318848 | bytes 6684672 | tf_op jit(solution)/shard_map/dot_general | solution.py:37
  160.3 93.9 %shard_map.306 = (bf16[2,2,96,768]{3,2,1,0:T(8,128)(2,1)}, bf16[2,2,24,3072]{3,2,1,0:T(8,128)(2,1)}, bf16[2,2,24,768]{3,2,1,0:T(8,128)(2,1)}, bf16[256,768]{1,0:...) custom-call(bf16[2,2,2,4,96,768]{5,4,3,2,1,0:T(8,128)(2,1)} %bitcast.141, ...), custom_call_target="tpu_custom_call" | custom-call | tf_op jit(solution)/shard_map/pallas_call | solution.py:761
  254.2 1.6 convolution_add_fusion.5
  255.9 0.5 convolution_add_fusion.4
  256.4 0.4 copy-done.8
  256.8 0.4 copy-done.15
  257.3 2.0 multiply_reduce_fusion
  259.3 0.6 broadcast_in_dim.40
  260.0 0.1 convert_reduce_fusion.4
  260.1 0.1 convert_reduce_fusion.3
  260.3 0.1 concatenate.8
  260.4 0.7 copy.63
  261.1 1.5 convolution_convert_fusion.2
  262.6 1.5 convolution_convert_fusion.4
  264.2 1.5 convolution_convert_fusion.3
  265.7 52.1 %shard_map.307 = (f32[4,24,768]{2,1,0:T(8,128)}, f32[4,24,768]{2,1,0:T(8,128)}, f32[4,24,768]{2,1,0:T(8,128)}, f32[4,8,128]{2,1,0:T(8,128)}, f32[4,96,768]{2,1,0...) custom-call(bf16[2,2,2,4,24,768]{5,4,3,2,1,0:T(8,128)(2,1)} %bitcast.150, ...), custom_call_target="tpu_custom_call" | custom-call | tf_op jit(solution)/shard_map/pallas_call | solution.py:761
  317.8 1.3 slice.126
  319.8 1.3 slice.122
  321.1 1.5 fusion.23
  322.6 1.8 copy.89
  324.4 1.7 copy.90
  326.1 1.7 copy.91
  327.8 1.7 copy.92
  329.5 1.0 copy.93
  330.5 1.0 copy.94
  (99 shorter events, 1.0 us)
Async XLA Ops:
  0.7 52.1 %copy-start.1 = (bf16[1,256,768]{2,1,0:T(8,128)(2,1)S(1)}, bf16[1,256,768]{2,1,0:T(8,128)(2,1)}, u32[]{:S(2)}) copy-start(bf16[1,256,768]{2,1,0:T(8,128)(2,1)} %param.17) | copy-start | bytes 1179652
  50.1 5.1 %copy-start.14 = (bf16[2,2,2,4,24,768]{5,4,3,2,1,0:T(8,128)(2,1)S(1)}, bf16[2,2,2,4,24,768]{5,4,3,2,1,0:T(8,128)(2,1)}, u32[]{:S(2)}) copy-start(bf16[2,2,2,4,24,768]{5,4,3,2,1,0:T(8,128)(2,1)} %get-tuple-element.49) | copy-start | bytes 3538948
  52.0 4.5 %copy-start.3 = (bf16[2,2,2,4,24,768]{5,4,3,2,1,0:T(8,128)(2,1)S(1)}, bf16[2,2,2,4,24,768]{5,4,3,2,1,0:T(8,128)(2,1)}, u32[]{:S(2)}) copy-start(bf16[2,2,2,4,24,768]{5,4,3,2,1,0:T(8,128)(2,1)} %get-tuple-element.48) | copy-start | bytes 3538948
  123.3 6.2 %slice-start.2 = ((s8[4718592]{0:T(1024)(128)(4,1)}), s8[4194304]{0:T(1024)(128)(4,1)S(1)}, s32[]{:S(2)}) async-start(s8[4718592]{0:T(1024)(128)(4,1)} %bitcast.157), calls=%async_computation.2 | async-start | bytes 8388608
  123.5 20.5 %copy-start.26 = (f32[256]{0:T(256)}, f32[256]{0:T(256)S(1)}, u32[]{:S(2)}) copy-start(f32[256]{0:T(256)S(1)} %fusion.16) | copy-start | bytes 3076
  123.5 6.0 %slice-start.3 = ((s8[4718592]{0:T(1024)(128)(4,1)}), s8[524288]{0:T(1024)(128)(4,1)S(1)}, s32[]{:S(2)}) async-start(s8[4718592]{0:T(1024)(128)(4,1)} %bitcast.157), calls=%async_computation.3 | async-start | bytes 1048576
  129.5 1.6 copy-start.5
  129.5 1.8 copy-start.2
  132.3 2.2 copy-start.28
  133.5 6.0 %slice-start = ((s8[4718592]{0:T(1024)(128)(4,1)}), s8[4194304]{0:T(1024)(128)(4,1)S(1)}, s32[]{:S(2)}) async-start(s8[4718592]{0:T(1024)(128)(4,1)} %bitcast.153), calls=%async_computation | async-start | bytes 8388608
  133.7 5.9 %copy-start.9 = (bf16[256,768]{1,0:T(8,128)(2,1)}, bf16[256,768]{1,0:T(8,128)(2,1)S(1)}, u32[]{:S(2)}) copy-start(bf16[256,768]{1,0:T(8,128)(2,1)S(1)} %get-tuple-element.74) | copy-start | bytes 1179652
  134.4 5.1 %slice-start.1 = ((s8[4718592]{0:T(1024)(128)(4,1)}), s8[524288]{0:T(1024)(128)(4,1)S(1)}, s32[]{:S(2)}) async-start(s8[4718592]{0:T(1024)(128)(4,1)} %bitcast.153), calls=%async_computation.1 | async-start | bytes 1048576
  139.5 2.6 copy-start.12
  142.1 5.3 %copy-start = (bf16[2,2,2,4,24,768]{5,4,3,2,1,0:T(8,128)(2,1)S(1)}, bf16[2,2,2,4,24,768]{5,4,3,2,1,0:T(8,128)(2,1)}, u32[]{:S(2)}) copy-start(bf16[2,2,2,4,24,768]{5,4,3,2,1,0:T(8,128)(2,1)} %get-tuple-element.51) | copy-start | bytes 3538948
  149.4 2.6 copy-start.13
  152.0 4.6 %copy-start.6 = (bf16[256,3072]{1,0:T(8,128)(2,1)S(1)}, bf16[256,3072]{1,0:T(8,128)(2,1)}, u32[]{:S(2)}) copy-start(bf16[256,3072]{1,0:T(8,128)(2,1)} %copy-done.5) | copy-start | bytes 4718596
  152.0 4.6 %copy-start.10 = (bf16[256,768]{1,0:T(8,128)(2,1)S(1)}, bf16[256,768]{1,0:T(8,128)(2,1)}, u32[]{:S(2)}) copy-start(bf16[256,768]{1,0:T(8,128)(2,1)} %copy-done.9) | copy-start | bytes 1179652
  160.3 93.9 %copy-start.16 = (bf16[2,2,2,4,24,768]{5,4,3,2,1,0:T(8,128)(2,1)S(1)}, bf16[2,2,2,4,24,768]{5,4,3,2,1,0:T(8,128)(2,1)}, u32[]{:S(2)}) copy-start(bf16[2,2,2,4,24,768]{5,4,3,2,1,0:T(8,128)(2,1)} %get-tuple-element.46) | copy-start | bytes 3538948
  160.3 93.9 %copy-start.27 = (f32[256]{0:T(256)S(1)}, f32[256]{0:T(256)}, u32[]{:S(2)}) copy-start(f32[256]{0:T(256)} %negate_multiply_fusion) | copy-start | bytes 3076
  254.2 1.7 copy-start.4
  254.2 1.7 copy-start.11
  255.8 1.0 copy-start.8
  255.9 1.4 copy-start.15
  257.2 2.7 copy-start.7
  257.2 3.0 copy-start.19
  257.2 3.0 copy-start.20
  257.3 3.0 copy-start.21
  257.3 3.0 copy-start.22
  257.3 3.0 copy-start.23
  257.3 3.0 copy-start.24
  257.3 3.0 copy-start.25
  317.8 11.7 %copy-start.18 = (f32[4,24,3072]{2,1,0:T(8,128)S(1)}, f32[4,24,3072]{2,1,0:T(8,128)}, u32[]{:S(2)}) copy-start(f32[4,24,3072]{2,1,0:T(8,128)} %get-tuple-element.66) | copy-start | bytes 3538948
  322.6 7.9 %copy-start.17 = (f32[4,96,768]{2,1,0:T(8,128)S(1)}, f32[4,96,768]{2,1,0:T(8,128)}, u32[]{:S(2)}) copy-start(f32[4,96,768]{2,1,0:T(8,128)} %get-tuple-element.67) | copy-start | bytes 3538948

commit v6 on v5

--- a/solution.py
+++ b/solution.py
@@ -491,10 +491,17 @@
         grad_query_ref, grad_key_ref, grad_value_ref = refs[at : at + 3]
         at += 3
     size = len(units)
-    first, second, third, fourth, own, mid = [
-        refs[at + i * size : at + (i + 1) * size] for i in range(6)
+    first, second, third, fourth, own, mid, final = [
+        refs[at + i * size : at + (i + 1) * size] for i in range(7)
     ]
-    sems = refs[at + 6 * size :]
+    written = refs[at + 7 * size]
+    sems = refs[at + 7 * size + 1 :]
+
+    def write(u):
+        a, start, width = units[u]
+        block = outs[a].at[:, :, pl.ds(start, width)]
+        return pltpu.make_async_copy(final[u], block, written.at[u])
+
     kind_of = [kinds[a] for a, _, _ in units]
     sends_c, recvs_c, sends_r, recvs_r, sends_z, recvs_z, sends_g, recvs_g = sems[:8]
     rep, high, low, core = places()
@@ -583,14 +590,6 @@
             peer = ((rep + k) % reps, me[1])
             send(block, block, sends_g, recvs_g, u * (reps - 1) + k - 1, peer)
 
-    stages = (over_core, over_rep, over_near, over_far)
-
-    def advance(step):
-        for lag, stage in enumerate(stages):
-            if 0 <= step - lag < size:
-                stage(step - lag)
-
-    steps = size + len(stages) - 1
     if not fused:
         whole = [u for u in range(size) if kind_of[u] != DEPTH]
         rest = [u for u in range(size) if kind_of[u] == DEPTH]
@@ -602,6 +601,15 @@
     else:
         terms, merged, from_near, from_far, held, sends_k, recvs_k, fetched = sems[8:]
         pairs = terms.shape[0]
+
+        def advance(step):
+            for u in range(size):
+                if step == u // 2:
+                    over_core(u)
+                if step == pairs - 1 + u // 2:
+                    over_rep(u)
+
+        steps = pairs + size // 2 + 1
 
         def fetch(p):
             return pltpu.make_async_copy(pair_ref.at[p], held.at[p % 2], fetched.at[p % 2])
@@ -688,7 +696,11 @@
             for k in range(1, reps):
                 block = mid[u].at[(rep + reps - k) % reps]
                 arrived(block, sends_g, recvs_g, u * (reps - 1) + k - 1)
-            outs[a][:, :, start : start + width] = mid[u][...].astype(F32)
+            final[u][...] = mid[u][...].astype(F32)
+            write(u).start()
+    for u in range(size):
+        if kind_of[u] != REST:
+            write(u).wait()
     for u, (a, start, width) in enumerate(units):
         cols = pl.ds(start, width)
         if kind_of[u] != DEPTH:
@@ -721,14 +733,14 @@
     dma = pltpu.SemaphoreType.DMA
     vmem = pl.BlockSpec(memory_space=pltpu.VMEM)
 
-    def buffers(without, *lead):
+    def buffers(without, *lead, kind=None):
         shapes = []
         for at, _, size in units:
             tile = (blocks[at].shape[-2], size)
             if kinds[at] == without:
                 shapes.append(pltpu.VMEM((8, 128), BF16))
             else:
-                shapes.append(pltpu.VMEM(lead + tile, blocks[at].dtype))
+                shapes.append(pltpu.VMEM(lead + tile, kind or blocks[at].dtype))
         return shapes
 
     total = len(units)
@@ -762,13 +774,18 @@
         functools.partial(reduce_kernel, units, tuple(kinds), reps, pairs is not None),
         out_shape=out_shape,
         in_specs=in_specs,
-        out_specs=[vmem] * len(out_shape),
+        out_specs=[
+            vmem if kind == REST else pl.BlockSpec(memory_space=pltpu.HBM) for kind in kinds
+        ]
+        + [vmem] * (len(out_shape) - count),
         scratch_shapes=buffers(DEPTH, 2, 2, reps)
         + buffers(DEPTH, reps - 1, 2, 2)
         + buffers(REST, 2)
         + buffers(REST)
         + buffers(REST, 2, 2)
         + buffers(REST, reps)
+        + buffers(REST, reps, kind=F32)
+        + [dma((total,))]
         + [dma((total,))] * 2
         + [dma((total * (reps - 1),))] * 2
         + [dma((total * 2,))] * 2

time: 334 us -> 318 us (0.952)
  Pallas kernels: 253 us -> 238 us
    pallas_call x2, Pallas kernels: 146 us -> 131 us  [reduce_many(): pl.pallas_call(functools.partial(reduce_kernel, units, tuple(kinds), reps...]
where the time goes in v6:
time: 318 us; the launch traced here: 317 us
  Pallas kernels  238 us (75%)
  matrix products  42.8 us (13%)
  local copies, waits for them, and re-layouts  26.7 us (8%)
  other arithmetic  7.11 us (2%)
    pallas_call x2, Pallas kernels, reduce_many(): pl.pallas_call(functools.partial(reduce_kernel, units, tuple(kinds), reps...  131 us
    pallas_call x2, Pallas kernels, gather_many(): pl.pallas_call(functools.partial(gather_kernel, units, tuple(kinds), reps...  107 us
    dot_general x6, matrix products, over_rows(): lax.dot_general(left, right, (((0,), (0,)), ((), ())), preferred_element_...  15.5 us
    dot_general x6, matrix products, matmul(): return jnp.dot(left, right, preferred_element_type=F32)  14.4 us
    dot_general x6, matrix products, against(): lax.dot_general(left, right, (((1,), (1,)), ((), ())), preferred_element_...  12.9 us
    unnamed x82, local copies, waits for them, and re-layouts  11.4 us

profile of v6, /device:TPU:0, one launch (start us, length us, event | category | flops | bytes accessed | tf_op | source)
XLA Modules:
  0.0 317.5 jit_solution(14369304690438294943)
XLA Ops:
  0.7 0.7 pad_bitcast_fusion.8
  1.4 0.7 pad_bitcast_fusion.6
  2.1 0.7 pad_bitcast_fusion.4
  2.7 0.7 pad_bitcast_fusion.2
  3.4 0.7 concatenate.7
  4.2 0.6 pad_bitcast_fusion.1.refs_3_
  4.8 1.2 reduce_sum.210
  6.0 0.7 reshape.388
  6.6 43.5 %shard_map.304 = (bf16[2,2,2,4,24,768]{5,4,3,2,1,0:T(8,128)(2,1)}, bf16[2,2,2,4,24,768]{5,4,3,2,1,0:T(8,128)(2,1)}, bf16[2,2,2,4,24,768]{5,4,3,2,1,0:T(8,128)(2,...) custom-call(bf16[4,24,768]{2,1,0:T(8,128)(2,1)} %bitcast.174, ...), custom_call_target="tpu_custom_call" | custom-call | tf_op jit(solution)/shard_map/pallas_call | solution.py:454
  50.2 0.8 slice_convert_fusion
  51.0 1.0 fusion.22
  52.1 0.1 reshape.402
  52.7 2.5 fusion.7.refs_3_
  55.3 1.2 fusion.5.refs_5_
  56.5 1.2 fusion.4.refs_4_
  57.7 63.6 %shard_map.305 = (bf16[2,2,2,4,24,768]{5,4,3,2,1,0:T(8,128)(2,1)}, bf16[2,2,2,4,24,3072]{5,4,3,2,1,0:T(8,128)(2,1)}, bf16[2,2,2,4,96,768]{5,4,3,2,1,0:T(8,128)(2...) custom-call(bf16[2,2,2,4,24,768]{5,4,3,2,1,0:T(8,128)(2,1)} %get-tup, ...), custom_call_target="tpu_custom_call", output_to_operand_aliasing={{0}: (0, {}), {1}: (1, {}), {2}: (2, {})} | custom-call | tf_op jit(solution)/shard_map/pallas_call | solution.py:454
  121.3 2.0 fusion.24
  123.3 0.2 multiply_reduce_fusion.5
  123.6 5.9 %multiply_convert_fusion = (bf16[256,3072]{1,0:T(8,128)(2,1)S(1)}, f32[256,3072]{1,0:T(8,128)}) fusion(f32[3072]{0:T(1024)S(1)} %reshape.401, bf16[768,3072]{1,0:T(8,128)(2,1)} %bitcast.152, f32[256,768]{1,0:T(8,128)S(1)} %get-tuple-element.101, f32[768]{0:T(1024)S(1)} %reshape.400, f32[768]{0:T(1024)S(1)} %reshape.399, f32[256]{0:T(256)S(1)} %fusion.16, ...), kind=kOutput, calls=%fused_computation.5 | convolution fusion | flops 1213661184 | bytes 10244096 | tf_op jit(solution)/shard_map/dot_general | solution.py:33
  129.5 1.5 fusion.25
  131.1 0.2 multiply_reduce_fusion.4
  131.3 0.3 fusion.8
  131.6 0.7 reshape.387
  132.3 1.2 fusion.21
  133.5 0.1 convert_reduce_fusion.1
  133.7 0.8 copy-done.28
  134.4 5.1 %convert_reduce_fusion = (f32[3072]{0:T(1024)S(1)}, bf16[256,3072]{1,0:T(8,128)(2,1)S(1)}) fusion(f32[256,3072]{1,0:T(8,128)S(1)} %copy-done.28, bf16[256,768]{1,0:T(8,128)(2,1)S(1)} %get-tuple-element.74, bf16[3072,768]{1,0:T(8,128)(2,1)} %bitcast.156), kind=kOutput, calls=%fused_computation.3 | convolution fusion | flops 1219752960 | bytes 9842688 | tf_op jit(solution)/shard_map/dot_general | solution.py:41
  139.6 2.5 multiply_reduce_fusion.1
  142.1 0.6 reshape.385
  142.7 0.7 reshape.383
  143.4 0.7 reshape.386
  144.0 1.5 fusion.20
  145.5 0.5 negate_multiply_fusion
  146.0 0.7 reshape.384
  146.7 0.7 convert_reduce_fusion.2
  147.5 1.3 convolution_convert_fusion.7.refs_4_
  148.7 0.7 reshape.382
  149.4 2.6 convolution_convert_fusion.5
  152.0 4.6 %convolution_convert_fusion = bf16[768,3072]{1,0:T(8,128)(2,1)} fusion(bf16[256,3072]{1,0:T(8,128)(2,1)S(1)} %copy-done.13, f32[256,768]{1,0:T(8,128)S(1)} %get-tuple-element.101, f32[768]{0:T(1024)S(1)} %reshape.400, f32[768]{0:T(1024)S(1)} %reshape.399, f32[256]{0:T(256)} %copy-done.26, f32[256]{0:T(256)S(1)} %broadcast_multiply_fusion.1), kind=kOutput, calls=%fused_computation | convolution fusion | flops 1211301888 | bytes 7086080 | tf_op jit(solution)/shard_map/dot_general | solution.py:37
  156.6 3.6 %convolution_convert_fusion.1 = bf16[3072,768]{1,0:T(8,128)(2,1)} fusion(bf16[256,3072]{1,0:T(8,128)(2,1)S(1)} %copy-done.6, bf16[256,768]{1,0:T(8,128)(2,1)S(1)} %copy-done.10), kind=kOutput, calls=%fused_computation.1 | convolution fusion | flops 1210318848 | bytes 6684672 | tf_op jit(solution)/shard_map/dot_general | solution.py:37
  160.3 76.0 %shard_map.306 = (bf16[2,2,96,768]{3,2,1,0:T(8,128)(2,1)}, bf16[2,2,24,3072]{3,2,1,0:T(8,128)(2,1)}, bf16[2,2,24,768]{3,2,1,0:T(8,128)(2,1)}, bf16[256,768]{1,0:...) custom-call(bf16[2,2,2,4,96,768]{5,4,3,2,1,0:T(8,128)(2,1)} %bitcast.141, ...), custom_call_target="tpu_custom_call" | custom-call | tf_op jit(solution)/shard_map/pallas_call | solution.py:773
  236.3 1.6 convolution_add_fusion.5
  238.0 0.5 convolution_add_fusion.4
  238.5 0.4 copy-done.8
  238.9 0.4 copy-done.15
  239.4 2.0 multiply_reduce_fusion
  241.4 0.6 broadcast_in_dim.40
  242.0 0.1 convert_reduce_fusion.4
  242.2 0.1 convert_reduce_fusion.3
  242.4 0.1 concatenate.8
  242.5 0.7 copy.63
  243.2 1.5 convolution_convert_fusion.2
  244.7 1.5 convolution_convert_fusion.4
  246.2 1.5 convolution_convert_fusion.3
  247.8 54.8 %shard_map.307 = (f32[4,24,768]{2,1,0:T(8,128)}, f32[4,24,768]{2,1,0:T(8,128)}, f32[4,24,768]{2,1,0:T(8,128)}, f32[4,8,128]{2,1,0:T(8,128)}, f32[4,96,768]{2,1,0...) custom-call(bf16[2,2,2,4,24,768]{5,4,3,2,1,0:T(8,128)(2,1)} %bitcast.150, ...), custom_call_target="tpu_custom_call" | custom-call | tf_op jit(solution)/shard_map/pallas_call | solution.py:773
  302.6 1.3 slice.126
  304.6 1.3 slice.122
  305.9 1.5 fusion.23
  307.4 1.8 copy.89
  309.2 1.7 copy.90
  310.9 1.7 copy.91
  312.6 1.7 copy.92
  314.3 1.0 copy.93
  315.3 1.0 copy.94
  (99 shorter events, 1.0 us)
Async XLA Ops:
  0.7 52.1 %copy-start.1 = (bf16[1,256,768]{2,1,0:T(8,128)(2,1)S(1)}, bf16[1,256,768]{2,1,0:T(8,128)(2,1)}, u32[]{:S(2)}) copy-start(bf16[1,256,768]{2,1,0:T(8,128)(2,1)} %param.17) | copy-start | bytes 1179652
  50.1 5.1 %copy-start.14 = (bf16[2,2,2,4,24,768]{5,4,3,2,1,0:T(8,128)(2,1)S(1)}, bf16[2,2,2,4,24,768]{5,4,3,2,1,0:T(8,128)(2,1)}, u32[]{:S(2)}) copy-start(bf16[2,2,2,4,24,768]{5,4,3,2,1,0:T(8,128)(2,1)} %get-tuple-element.49) | copy-start | bytes 3538948
  52.0 4.5 %copy-start.3 = (bf16[2,2,2,4,24,768]{5,4,3,2,1,0:T(8,128)(2,1)S(1)}, bf16[2,2,2,4,24,768]{5,4,3,2,1,0:T(8,128)(2,1)}, u32[]{:S(2)}) copy-start(bf16[2,2,2,4,24,768]{5,4,3,2,1,0:T(8,128)(2,1)} %get-tuple-element.48) | copy-start | bytes 3538948
  123.3 6.2 %slice-start.2 = ((s8[4718592]{0:T(1024)(128)(4,1)}), s8[4194304]{0:T(1024)(128)(4,1)S(1)}, s32[]{:S(2)}) async-start(s8[4718592]{0:T(1024)(128)(4,1)} %bitcast.157), calls=%async_computation.2 | async-start | bytes 8388608
  123.5 20.5 %copy-start.26 = (f32[256]{0:T(256)}, f32[256]{0:T(256)S(1)}, u32[]{:S(2)}) copy-start(f32[256]{0:T(256)S(1)} %fusion.16) | copy-start | bytes 3076
  123.5 6.0 %slice-start.3 = ((s8[4718592]{0:T(1024)(128)(4,1)}), s8[524288]{0:T(1024)(128)(4,1)S(1)}, s32[]{:S(2)}) async-start(s8[4718592]{0:T(1024)(128)(4,1)} %bitcast.157), calls=%async_computation.3 | async-start | bytes 1048576
  129.5 1.6 copy-start.5
  129.5 1.8 copy-start.2
  132.3 2.2 copy-start.28
  133.5 6.0 %slice-start = ((s8[4718592]{0:T(1024)(128)(4,1)}), s8[4194304]{0:T(1024)(128)(4,1)S(1)}, s32[]{:S(2)}) async-start(s8[4718592]{0:T(1024)(128)(4,1)} %bitcast.153), calls=%async_computation | async-start | bytes 8388608
  133.7 5.9 %copy-start.9 = (bf16[256,768]{1,0:T(8,128)(2,1)}, bf16[256,768]{1,0:T(8,128)(2,1)S(1)}, u32[]{:S(2)}) copy-start(bf16[256,768]{1,0:T(8,128)(2,1)S(1)} %get-tuple-element.74) | copy-start | bytes 1179652
  134.4 5.1 %slice-start.1 = ((s8[4718592]{0:T(1024)(128)(4,1)}), s8[524288]{0:T(1024)(128)(4,1)S(1)}, s32[]{:S(2)}) async-start(s8[4718592]{0:T(1024)(128)(4,1)} %bitcast.153), calls=%async_computation.1 | async-start | bytes 1048576
  139.5 2.6 copy-start.12
  142.1 5.3 %copy-start = (bf16[2,2,2,4,24,768]{5,4,3,2,1,0:T(8,128)(2,1)S(1)}, bf16[2,2,2,4,24,768]{5,4,3,2,1,0:T(8,128)(2,1)}, u32[]{:S(2)}) copy-start(bf16[2,2,2,4,24,768]{5,4,3,2,1,0:T(8,128)(2,1)} %get-tuple-element.51) | copy-start | bytes 3538948
  149.4 2.6 copy-start.13
  152.0 4.6 %copy-start.6 = (bf16[256,3072]{1,0:T(8,128)(2,1)S(1)}, bf16[256,3072]{1,0:T(8,128)(2,1)}, u32[]{:S(2)}) copy-start(bf16[256,3072]{1,0:T(8,128)(2,1)} %copy-done.5) | copy-start | bytes 4718596
  152.0 4.6 %copy-start.10 = (bf16[256,768]{1,0:T(8,128)(2,1)S(1)}, bf16[256,768]{1,0:T(8,128)(2,1)}, u32[]{:S(2)}) copy-start(bf16[256,768]{1,0:T(8,128)(2,1)} %copy-done.9) | copy-start | bytes 1179652
  160.3 76.0 %copy-start.16 = (bf16[2,2,2,4,24,768]{5,4,3,2,1,0:T(8,128)(2,1)S(1)}, bf16[2,2,2,4,24,768]{5,4,3,2,1,0:T(8,128)(2,1)}, u32[]{:S(2)}) copy-start(bf16[2,2,2,4,24,768]{5,4,3,2,1,0:T(8,128)(2,1)} %get-tuple-element.46) | copy-start | bytes 3538948
  160.3 76.0 %copy-start.27 = (f32[256]{0:T(256)S(1)}, f32[256]{0:T(256)}, u32[]{:S(2)}) copy-start(f32[256]{0:T(256)} %negate_multiply_fusion) | copy-start | bytes 3076
  236.3 1.7 copy-start.4
  236.3 1.7 copy-start.11
  237.9 1.0 copy-start.8
  237.9 1.4 copy-start.15
  239.3 2.7 copy-start.7
  239.3 3.0 copy-start.19
  239.3 3.0 copy-start.20
  239.3 3.0 copy-start.21
  239.3 3.0 copy-start.22
  239.4 3.0 copy-start.23
  239.4 3.0 copy-start.24
  239.4 3.0 copy-start.25
  302.6 11.7 %copy-start.18 = (f32[4,24,3072]{2,1,0:T(8,128)S(1)}, f32[4,24,3072]{2,1,0:T(8,128)}, u32[]{:S(2)}) copy-start(f32[4,24,3072]{2,1,0:T(8,128)} %get-tuple-element.66) | copy-start | bytes 3538948
  307.4 7.9 %copy-start.17 = (f32[4,96,768]{2,1,0:T(8,128)S(1)}, f32[4,96,768]{2,1,0:T(8,128)}, u32[]{:S(2)}) copy-start(f32[4,96,768]{2,1,0:T(8,128)} %get-tuple-element.67) | copy-start | bytes 3538948

commit v7 on v6

--- a/solution.py
+++ b/solution.py
@@ -11,7 +11,7 @@
 HD = 64
 PAIR = 2 * HD
 CHUNKS = 3
-AHEAD = 2
+AHEAD = 3
 FULL, DEPTH, REST = range(3)
 EPSILON = 1e-12
 BF16 = jnp.bfloat16

time: 318 us -> 320 us (level)
  no operation moved by 1% of the time
where the time goes in v7:
time: 320 us; the launch traced here: 319 us
  Pallas kernels  239 us (75%)
  matrix products  42.8 us (13%)
  local copies, waits for them, and re-layouts  26.7 us (8%)
  other arithmetic  7.11 us (2%)
    pallas_call x2, Pallas kernels, reduce_many(): pl.pallas_call(functools.partial(reduce_kernel, units, tuple(kinds), reps...  130 us
    pallas_call x2, Pallas kernels, gather_many(): pl.pallas_call(functools.partial(gather_kernel, units, tuple(kinds), reps...  109 us
    dot_general x6, matrix products, over_rows(): lax.dot_general(left, right, (((0,), (0,)), ((), ())), preferred_element_...  15.5 us
    dot_general x6, matrix products, matmul(): return jnp.dot(left, right, preferred_element_type=F32)  14.4 us
    dot_general x6, matrix products, against(): lax.dot_general(left, right, (((1,), (1,)), ((), ())), preferred_element_...  13 us
    unnamed x82, local copies, waits for them, and re-layouts  11.4 us

profile of v7, /device:TPU:0, one launch (start us, length us, event | category | flops | bytes accessed | tf_op | source)
XLA Modules:
  0.0 318.9 jit_solution(12066919450071156522)
XLA Ops:
  0.7 0.7 pad_bitcast_fusion.8
  1.4 0.7 pad_bitcast_fusion.6
  2.1 0.7 pad_bitcast_fusion.4
  2.7 0.7 pad_bitcast_fusion.2
  3.4 0.7 concatenate.7
  4.2 0.6 pad_bitcast_fusion.1.refs_3_
  4.8 1.2 reduce_sum.210
  6.0 0.7 reshape.388
  6.6 43.5 %shard_map.304 = (bf16[2,2,2,4,24,768]{5,4,3,2,1,0:T(8,128)(2,1)}, bf16[2,2,2,4,24,768]{5,4,3,2,1,0:T(8,128)(2,1)}, bf16[2,2,2,4,24,768]{5,4,3,2,1,0:T(8,128)(2,...) custom-call(bf16[4,24,768]{2,1,0:T(8,128)(2,1)} %bitcast.174, ...), custom_call_target="tpu_custom_call" | custom-call | tf_op jit(solution)/shard_map/pallas_call | solution.py:454
  50.2 0.8 slice_convert_fusion
  51.0 1.0 fusion.22
  52.1 0.1 reshape.402
  52.7 2.5 fusion.7.refs_3_
  55.3 1.2 fusion.5.refs_5_
  56.5 1.2 fusion.4.refs_4_
  57.7 65.9 %shard_map.305 = (bf16[2,2,2,4,24,768]{5,4,3,2,1,0:T(8,128)(2,1)}, bf16[2,2,2,4,24,3072]{5,4,3,2,1,0:T(8,128)(2,1)}, bf16[2,2,2,4,96,768]{5,4,3,2,1,0:T(8,128)(2...) custom-call(bf16[2,2,2,4,24,768]{5,4,3,2,1,0:T(8,128)(2,1)} %get-tup, ...), custom_call_target="tpu_custom_call", output_to_operand_aliasing={{0}: (0, {}), {1}: (1, {}), {2}: (2, {})} | custom-call | tf_op jit(solution)/shard_map/pallas_call | solution.py:454
  123.6 2.0 fusion.24
  125.6 0.2 multiply_reduce_fusion.5
  125.9 5.9 %multiply_convert_fusion = (bf16[256,3072]{1,0:T(8,128)(2,1)S(1)}, f32[256,3072]{1,0:T(8,128)}) fusion(f32[3072]{0:T(1024)S(1)} %reshape.401, bf16[768,3072]{1,0:T(8,128)(2,1)} %bitcast.152, f32[256,768]{1,0:T(8,128)S(1)} %get-tuple-element.101, f32[768]{0:T(1024)S(1)} %reshape.400, f32[768]{0:T(1024)S(1)} %reshape.399, f32[256]{0:T(256)S(1)} %fusion.16, ...), kind=kOutput, calls=%fused_computation.5 | convolution fusion | flops 1213661184 | bytes 10244096 | tf_op jit(solution)/shard_map/dot_general | solution.py:33
  131.8 1.5 fusion.25
  133.4 0.2 multiply_reduce_fusion.4
  133.6 0.3 fusion.8
  133.9 0.7 reshape.387
  134.6 1.2 fusion.21
  135.8 0.1 convert_reduce_fusion.1
  136.0 0.8 copy-done.28
  136.8 5.1 %convert_reduce_fusion = (f32[3072]{0:T(1024)S(1)}, bf16[256,3072]{1,0:T(8,128)(2,1)S(1)}) fusion(f32[256,3072]{1,0:T(8,128)S(1)} %copy-done.28, bf16[256,768]{1,0:T(8,128)(2,1)S(1)} %get-tuple-element.74, bf16[3072,768]{1,0:T(8,128)(2,1)} %bitcast.156), kind=kOutput, calls=%fused_computation.3 | convolution fusion | flops 1219752960 | bytes 9842688 | tf_op jit(solution)/shard_map/dot_general | solution.py:41
  141.9 2.5 multiply_reduce_fusion.1
  144.4 0.6 reshape.385
  145.0 0.7 reshape.383
  145.7 0.7 reshape.386
  146.4 1.5 fusion.20
  147.8 0.5 negate_multiply_fusion
  148.4 0.7 reshape.384
  149.0 0.7 convert_reduce_fusion.2
  149.8 1.3 convolution_convert_fusion.7.refs_4_
  151.0 0.7 reshape.382
  151.7 2.6 convolution_convert_fusion.5
  154.3 4.6 %convolution_convert_fusion = bf16[768,3072]{1,0:T(8,128)(2,1)} fusion(bf16[256,3072]{1,0:T(8,128)(2,1)S(1)} %copy-done.13, f32[256,768]{1,0:T(8,128)S(1)} %get-tuple-element.101, f32[768]{0:T(1024)S(1)} %reshape.400, f32[768]{0:T(1024)S(1)} %reshape.399, f32[256]{0:T(256)} %copy-done.26, f32[256]{0:T(256)S(1)} %broadcast_multiply_fusion.1), kind=kOutput, calls=%fused_computation | convolution fusion | flops 1211301888 | bytes 7086080 | tf_op jit(solution)/shard_map/dot_general | solution.py:37
  159.0 3.6 %convolution_convert_fusion.1 = bf16[3072,768]{1,0:T(8,128)(2,1)} fusion(bf16[256,3072]{1,0:T(8,128)(2,1)S(1)} %copy-done.6, bf16[256,768]{1,0:T(8,128)(2,1)S(1)} %copy-done.10), kind=kOutput, calls=%fused_computation.1 | convolution fusion | flops 1210318848 | bytes 6684672 | tf_op jit(solution)/shard_map/dot_general | solution.py:37
  162.6 75.2 %shard_map.306 = (bf16[2,2,96,768]{3,2,1,0:T(8,128)(2,1)}, bf16[2,2,24,3072]{3,2,1,0:T(8,128)(2,1)}, bf16[2,2,24,768]{3,2,1,0:T(8,128)(2,1)}, bf16[256,768]{1,0:...) custom-call(bf16[2,2,2,4,96,768]{5,4,3,2,1,0:T(8,128)(2,1)} %bitcast.141, ...), custom_call_target="tpu_custom_call" | custom-call | tf_op jit(solution)/shard_map/pallas_call | solution.py:773
  237.9 1.6 convolution_add_fusion.5
  239.5 0.5 convolution_add_fusion.4
  240.1 0.4 copy-done.8
  240.5 0.4 copy-done.15
  241.0 2.0 multiply_reduce_fusion
  242.9 0.6 broadcast_in_dim.40
  243.6 0.1 convert_reduce_fusion.4
  243.8 0.1 convert_reduce_fusion.3
  244.0 0.1 concatenate.8
  244.1 0.7 copy.63
  244.8 1.5 convolution_convert_fusion.2
  246.3 1.5 convolution_convert_fusion.4
  247.8 1.5 convolution_convert_fusion.3
  249.4 54.6 %shard_map.307 = (f32[4,24,768]{2,1,0:T(8,128)}, f32[4,24,768]{2,1,0:T(8,128)}, f32[4,24,768]{2,1,0:T(8,128)}, f32[4,8,128]{2,1,0:T(8,128)}, f32[4,96,768]{2,1,0...) custom-call(bf16[2,2,2,4,24,768]{5,4,3,2,1,0:T(8,128)(2,1)} %bitcast.150, ...), custom_call_target="tpu_custom_call" | custom-call | tf_op jit(solution)/shard_map/pallas_call | solution.py:773
  304.0 1.3 slice.126
  306.0 1.3 slice.122
  307.3 1.5 fusion.23
  308.9 1.8 copy.89
  310.7 1.7 copy.90
  312.4 1.7 copy.91
  314.0 1.7 copy.92
  315.7 1.0 copy.93
  316.8 1.0 copy.94
  (99 shorter events, 1.0 us)
Async XLA Ops:
  0.7 52.1 %copy-start.1 = (bf16[1,256,768]{2,1,0:T(8,128)(2,1)S(1)}, bf16[1,256,768]{2,1,0:T(8,128)(2,1)}, u32[]{:S(2)}) copy-start(bf16[1,256,768]{2,1,0:T(8,128)(2,1)} %param.17) | copy-start | bytes 1179652
  50.1 5.1 %copy-start.14 = (bf16[2,2,2,4,24,768]{5,4,3,2,1,0:T(8,128)(2,1)S(1)}, bf16[2,2,2,4,24,768]{5,4,3,2,1,0:T(8,128)(2,1)}, u32[]{:S(2)}) copy-start(bf16[2,2,2,4,24,768]{5,4,3,2,1,0:T(8,128)(2,1)} %get-tuple-element.49) | copy-start | bytes 3538948
  52.0 4.5 %copy-start.3 = (bf16[2,2,2,4,24,768]{5,4,3,2,1,0:T(8,128)(2,1)S(1)}, bf16[2,2,2,4,24,768]{5,4,3,2,1,0:T(8,128)(2,1)}, u32[]{:S(2)}) copy-start(bf16[2,2,2,4,24,768]{5,4,3,2,1,0:T(8,128)(2,1)} %get-tuple-element.48) | copy-start | bytes 3538948
  125.6 6.2 %slice-start.2 = ((s8[4718592]{0:T(1024)(128)(4,1)}), s8[4194304]{0:T(1024)(128)(4,1)S(1)}, s32[]{:S(2)}) async-start(s8[4718592]{0:T(1024)(128)(4,1)} %bitcast.157), calls=%async_computation.2 | async-start | bytes 8388608
  125.9 20.5 %copy-start.26 = (f32[256]{0:T(256)}, f32[256]{0:T(256)S(1)}, u32[]{:S(2)}) copy-start(f32[256]{0:T(256)S(1)} %fusion.16) | copy-start | bytes 3076
  125.9 6.0 %slice-start.3 = ((s8[4718592]{0:T(1024)(128)(4,1)}), s8[524288]{0:T(1024)(128)(4,1)S(1)}, s32[]{:S(2)}) async-start(s8[4718592]{0:T(1024)(128)(4,1)} %bitcast.157), calls=%async_computation.3 | async-start | bytes 1048576
  131.8 1.6 copy-start.5
  131.8 1.8 copy-start.2
  134.6 2.2 copy-start.28
  135.8 6.0 %slice-start = ((s8[4718592]{0:T(1024)(128)(4,1)}), s8[4194304]{0:T(1024)(128)(4,1)S(1)}, s32[]{:S(2)}) async-start(s8[4718592]{0:T(1024)(128)(4,1)} %bitcast.153), calls=%async_computation | async-start | bytes 8388608
  136.0 5.9 %copy-start.9 = (bf16[256,768]{1,0:T(8,128)(2,1)}, bf16[256,768]{1,0:T(8,128)(2,1)S(1)}, u32[]{:S(2)}) copy-start(bf16[256,768]{1,0:T(8,128)(2,1)S(1)} %get-tuple-element.74) | copy-start | bytes 1179652
  136.8 5.1 %slice-start.1 = ((s8[4718592]{0:T(1024)(128)(4,1)}), s8[524288]{0:T(1024)(128)(4,1)S(1)}, s32[]{:S(2)}) async-start(s8[4718592]{0:T(1024)(128)(4,1)} %bitcast.153), calls=%async_computation.1 | async-start | bytes 1048576
  141.9 2.6 copy-start.12
  144.4 5.3 %copy-start = (bf16[2,2,2,4,24,768]{5,4,3,2,1,0:T(8,128)(2,1)S(1)}, bf16[2,2,2,4,24,768]{5,4,3,2,1,0:T(8,128)(2,1)}, u32[]{:S(2)}) copy-start(bf16[2,2,2,4,24,768]{5,4,3,2,1,0:T(8,128)(2,1)} %get-tuple-element.51) | copy-start | bytes 3538948
  151.7 2.6 copy-start.13
  154.3 4.6 %copy-start.6 = (bf16[256,3072]{1,0:T(8,128)(2,1)S(1)}, bf16[256,3072]{1,0:T(8,128)(2,1)}, u32[]{:S(2)}) copy-start(bf16[256,3072]{1,0:T(8,128)(2,1)} %copy-done.5) | copy-start | bytes 4718596
  154.3 4.6 %copy-start.10 = (bf16[256,768]{1,0:T(8,128)(2,1)S(1)}, bf16[256,768]{1,0:T(8,128)(2,1)}, u32[]{:S(2)}) copy-start(bf16[256,768]{1,0:T(8,128)(2,1)} %copy-done.9) | copy-start | bytes 1179652
  162.6 75.3 %copy-start.16 = (bf16[2,2,2,4,24,768]{5,4,3,2,1,0:T(8,128)(2,1)S(1)}, bf16[2,2,2,4,24,768]{5,4,3,2,1,0:T(8,128)(2,1)}, u32[]{:S(2)}) copy-start(bf16[2,2,2,4,24,768]{5,4,3,2,1,0:T(8,128)(2,1)} %get-tuple-element.46) | copy-start | bytes 3538948
  162.6 75.3 %copy-start.27 = (f32[256]{0:T(256)S(1)}, f32[256]{0:T(256)}, u32[]{:S(2)}) copy-start(f32[256]{0:T(256)} %negate_multiply_fusion) | copy-start | bytes 3076
  237.8 1.7 copy-start.4
  237.9 1.7 copy-start.11
  239.5 1.0 copy-start.8
  239.5 1.4 copy-start.15
  240.9 2.7 copy-start.7
  240.9 3.0 copy-start.19
  240.9 3.0 copy-start.20
  240.9 3.0 copy-start.21
  240.9 3.0 copy-start.22
  240.9 3.0 copy-start.23
  240.9 3.0 copy-start.24
  240.9 3.0 copy-start.25
  304.0 11.7 %copy-start.18 = (f32[4,24,3072]{2,1,0:T(8,128)S(1)}, f32[4,24,3072]{2,1,0:T(8,128)}, u32[]{:S(2)}) copy-start(f32[4,24,3072]{2,1,0:T(8,128)} %get-tuple-element.66) | copy-start | bytes 3538948
  308.9 7.9 %copy-start.17 = (f32[4,96,768]{2,1,0:T(8,128)S(1)}, f32[4,96,768]{2,1,0:T(8,128)}, u32[]{:S(2)}) copy-start(f32[4,96,768]{2,1,0:T(8,128)} %get-tuple-element.67) | copy-start | bytes 3538948
